TPU v7x, 128 devices: a whole 4x4x4 slice. The times are simulated.
128 devices in a mesh: area: 32 (over z, y, core), local: 4 (over x).
Axes of the slice: x: 4, y: 4, z: 4, core: 2. Of those that a mesh axis runs over, the one named last changes fastest.
Arguments:
- potential: float32 [8, 524288], P(None, ('area', 'local')), may hold values from -6 to 6
- current: float32 [8, 524288], P(None, ('area', 'local')), may hold values from -4 to 4
- ext_drive: float32 [8, 524288], P(None, ('area', 'local')), may hold values from -6 to 6
- decay_syn: float32 [524288], P(('area', 'local')), may hold values from 0.3 to 0.97
- decay_mem: float32 [524288], P(('area', 'local')), may hold values from 0.4 to 0.95
- weights: bfloat16 [128, 128, 2, 128, 128], P(('area', 'local')), may hold values from -0.25 to 0.25
- tile_src: int32 [128, 128, 2], P(('area', 'local')), may hold values from 0 to 31
- tile_dst: int32 [128, 128, 2], P(('area', 'local')), may hold values from 0 to 31
- blk_pop: int32 [4096], P(('area', 'local')), may hold values from 0 to 7
- tile_route: int32 [5, 128, 128, 1], P(None, ('area', 'local')), may hold values from 0 to 1, as said below
- counts: int32 [5, 128, 128], P(None, ('area', 'local')), may hold values from 0 to 1, as said below
Outputs:
- volts_out: float32 [8, 524288], P(None, ('area', 'local'))
- current_out: float32 [8, 524288], P(None, ('area', 'local'))
- pop_rates: float32 [32, 5, 8, 8], P('area')
Inputs may be any that keep to these rules, and one draw needn't show every extreme that they name: `tile_route`: the 1 entries of one list name distinct tiles; entries at and beyond counts of that list are unused. `counts`: in every step some target device gets 1 tiles from every sending device.
All inputs are finite; a program needn't handle non-finite values.
Results may differ from a plain program's by a relative error of at most 0.0029.
Values may be sent and summed in bfloat16 or wider, within the bound.
No kernel may reach another device: no remote copies, remote signals or barrier semaphores. Data moves between devices by JAX's collectives and lax.ppermute only.
A program may use at most 64 MiB of HBM per device.

v0:
```python
import jax
import jax.numpy as jnp
from jax import lax
from jax.sharding import PartitionSpec as P

POPS = 8


spike_gain = 4.0
threshold = 1.0
reset_size = 0.5


def from_everyone(array, axis):
    copies = jnp.broadcast_to(array, (lax.axis_size(axis), *array.shape))
    return lax.all_to_all(copies, axis, split_axis=0, concat_axis=0, tiled=True)


def of_everyone(array, axis):
    return from_everyone(array, axis).sum(axis=0)


def shards(
    potential,
    current,
    ext_drive,
    decay_syn,
    decay_mem,
    weights,
    tile_src,
    tile_dst,
    blk_pop,
    tile_route,
    counts,
):
    dev_count = weights.shape[1]
    tile_count = weights.shape[2]
    block_width = weights.shape[3]
    blk_count = blk_pop.shape[0]
    trial_count = potential.shape[0]
    slot_count = tile_route.shape[3]
    step_count = tile_route.shape[0]
    tile_table = weights[0]
    routes = tile_route[:, 0]
    slot_valid = jnp.arange(slot_count, dtype=jnp.int32)[None, None, :] < counts[:, 0][:, :, None]
    table_shape = (step_count, dev_count, tile_count)
    src_blocks = jnp.take_along_axis(
        jnp.broadcast_to(tile_src[0][None], table_shape), routes, axis=2
    )
    dst_blocks = jnp.take_along_axis(
        jnp.broadcast_to(tile_dst[0][None], table_shape), routes, axis=2
    )
    dst_ids = jnp.where(slot_valid, dst_blocks, -1)
    arrived_ids = lax.all_to_all(
        dst_ids, ("area", "local"), split_axis=1, concat_axis=1, tiled=True
    )
    state_shape = (trial_count, blk_count, block_width)
    volts = potential.reshape(state_shape)
    syn_cur = current.reshape(state_shape)
    ext_field = ext_drive.reshape(state_shape)
    syn_decay = decay_syn.reshape((1, blk_count, block_width))
    mem_decay = decay_mem.reshape((1, blk_count, block_width))
    pop_table = (blk_pop[:, None] == jnp.arange(POPS, dtype=jnp.int32)[None, :]).astype(jnp.float32)
    block_ids = jnp.arange(blk_count, dtype=jnp.int32)

    def advance(step_idx, state_now):
        volts, syn_cur, rate_acc = state_now
        spikes = jax.nn.sigmoid(spike_gain * (volts - threshold))
        spike_blocks = jnp.transpose(spikes.astype(jnp.bfloat16), (1, 0, 2))
        activity = jnp.sum(spikes, axis=2)
        rate_now = jnp.dot(activity, pop_table, precision=lax.Precision.HIGHEST)
        rate_acc = lax.dynamic_update_index_in_dim(rate_acc, rate_now, step_idx, 0)
        chosen = routes[step_idx]
        picked = jnp.take_along_axis(tile_table, chosen[:, :, None, None], axis=1)
        senders = jnp.take(spike_blocks, src_blocks[step_idx], axis=0)
        outgoing = jnp.einsum(
            "tcrn,tcnm->tcrm", senders, picked, preferred_element_type=jnp.float32
        ).astype(jnp.bfloat16)
        arrived = lax.all_to_all(
            outgoing, ("area", "local"), split_axis=0, concat_axis=0, tiled=True
        )
        targets = arrived_ids[step_idx].reshape((dev_count * slot_count,))
        deliver = (targets[:, None] == block_ids[None, :]).astype(jnp.bfloat16)
        inflow = jnp.einsum(
            "sb,srn->rbn",
            deliver,
            arrived.reshape((dev_count * slot_count, trial_count, block_width)),
            preferred_element_type=jnp.float32,
        )
        syn_cur = syn_decay * syn_cur + inflow
        volts = mem_decay * volts + (1.0 - mem_decay) * (syn_cur + ext_field) - reset_size * spikes
        return (volts, syn_cur, rate_acc)

    rate_start = jnp.zeros((step_count, trial_count, POPS), jnp.float32)
    volts, syn_cur, rate_acc = lax.fori_loop(0, step_count, advance, (volts, syn_cur, rate_start))
    totals = of_everyone(rate_acc, "local") / (block_width * blk_count)
    return (volts.reshape((trial_count, -1)), syn_cur.reshape((trial_count, -1)), totals[None])


def solution(mesh):
    in_specs = (
        P(None, ("area", "local")),
        P(None, ("area", "local")),
        P(None, ("area", "local")),
        P(("area", "local")),
        P(("area", "local")),
        P(("area", "local"), None, None, None, None),
        P(("area", "local"), None, None),
        P(("area", "local"), None, None),
        P(("area", "local")),
        P(None, ("area", "local"), None, None),
        P(None, ("area", "local"), None),
    )
    out_specs = (
        P(None, ("area", "local")),
        P(None, ("area", "local")),
        P("area", None, None, None),
    )
    return jax.shard_map(shards, mesh=mesh, in_specs=in_specs, out_specs=out_specs, check_vma=False)
```

profile of v0, /device:TPU:1, one launch (start us, length us, event | category | flops | bytes accessed | tf_op | source)
XLA Modules:
  0.0 181.4 jit_solution(10345220873550262598)
XLA Ops:
  0.6 0.7 fusion.37
  1.4 0.8 copy.54
  2.3 5.6 %gather_fusion.2 = s32[640]{0:T(1024)S(1)} fusion(s32[5,128,2]{2,1,0:T(8,128)S(1)} %broadcast_in_dim.74, s32[640]{0:T(1024)S(1)} %bitcast.118), kind=kCustom, calls=%fused_computation.clone | custom fusion | bytes 12800 | tf_op jit(solution)/shard_map/jit(take_along_axis)/gather | solution.py:47
  8.1 5.6 %gather_fusion.3 = s32[640]{0:T(1024)S(1)} fusion(s32[5,128,2]{2,1,0:T(8,128)S(1)} %broadcast_in_dim.76, s32[640]{0:T(1024)S(1)} %bitcast.119), kind=kCustom, calls=%fused_computation.3.clone | custom fusion | bytes 12800 | tf_op jit(solution)/shard_map/jit(take_along_axis)/gather | solution.py:50
  13.8 0.7 copy.58
  14.6 11.5 %all-to-all-start.1 = ((s32[5,128,1]{0,2,1:T(1,128)}), s32[5,128,1]{0,2,1:T(1,128)S(1)}, u32[]{:S(2)}, u32[]{:S(2)}) async-start(s32[5,128,1]{0,2,1:T(1,128)} %copy.58), calls=%async_computation.1 | async-start | bytes 131072 | tf_op jit(solution)/shard_map/all_to_all | solution.py:54
  26.2 9.5 %all-to-all-done.1 = s32[5,128,1]{0,2,1:T(1,128)S(1)} async-done(((s32[5,128,1]{0,2,1:T(1,128)}), s32[5,128,1]{0,2,1:T(1,128)S(1)}, u32[]{:S(2)}, u32[]{:S(2)}) %all-to-all-start.1) | async-done | bytes 2592 | tf_op jit(solution)/shard_map/all_to_all | solution.py:54
  35.8 135.6 %while.20 = (s32[]{:T(128)}, f32[8,32,128]{2,1,0:T(8,128)S(1)}, f32[8,32,128]{2,1,0:T(8,128)S(1)}, f32[5,8,8]{2,1,0:T(8,128)S(1)}, f32[1,32,128]{2,1,0:T(8,128)S...) while((s32[]{:T(128)}, f32[8,32,128]{2,1,0:T(8,128)S(1)}, ...), condition=%wide.region_2.0_spmd.clone, body=%wide.region_0.3_spmd.clone.sunk | while | flops 44994944 | bytes 15770289 | solution.py:95
  36.1 0.7 gather_fusion.1
  36.8 6.5 %gather_fusion = bf16[128,128,128]{2,1,0:T(8,128)(2,1)} fusion(bf16[128,2,128,128]{3,2,1,0:T(8,128)(2,1)} %get-tuple-element.546, s32[128]{0:T(128)S(1)} %or_bitcast_fusion.2), kind=kCustom, calls=%fused_computation.2.clone.clone.1 | custom fusion | bytes 8389632 | tf_op jit(solution)/shard_map/while/body/eval_jaxpr/jit(take_along_axis)/gather | solution.py:74
  43.2 4.2 %fusion.55 = bf16[128,1,8,128]{3,2,1,0:T(8,128)(2,1)} fusion(bf16[128,128,128]{2,1,0:T(8,128)(2,1)} %gather_fusion, pred[128]{0:T(512)(128)(4,1)S(1)} %get-tuple-element.506, bf16[128,8,128]{2,1,0:T(8,128)(2,1)S(1)} %gather_fusion.1, pred[128]{0:T(512)(128)(4,1)S(1)} %get-tuple-element.508), kind=kOutput, calls=%fused_computation.11.clone.1 | convolution fusion | flops 35913728 | bytes 4718848 | tf_op jit(solution)/shard_map/while/body/eval_jaxpr/tcrn,tcnm->tcrm/dot_general | solution.py:76
  47.4 4.3 %all-to-all-start = ((bf16[128,1,8,128]{3,2,1,0:T(8,128)(2,1)}), bf16[128,1,8,128]{3,2,1,0:T(8,128)(2,1)S(1)}, u32[]{:S(2)}, u32[]{:S(2)}) async-start(bf16[128,1,8,128]{3,2,1,0:T(8,128)(2,1)} %fusion.55), calls=%async_computation | async-start | bytes 524288 | tf_op jit(solution)/shard_map/while/body/eval_jaxpr/all_to_all | solution.py:79
  51.6 0.2 fusion.56
  51.9 11.1 %all-to-all-done = bf16[128,1,8,128]{3,2,1,0:T(8,128)(2,1)S(1)} async-done(((bf16[128,1,8,128]{3,2,1,0:T(8,128)(2,1)}), bf16[128,1,8,128]{3,2,1,0:T(8,128)(2,1)S(1)}, u32[]{:S(2)}, u32[]{:S(2)}) %all-to-all-start) | async-done | bytes 262176 | tf_op jit(solution)/shard_map/while/body/eval_jaxpr/all_to_all | solution.py:79
  63.5 0.7 gather_fusion.1
  64.1 6.5 %gather_fusion = bf16[128,128,128]{2,1,0:T(8,128)(2,1)} fusion(bf16[128,2,128,128]{3,2,1,0:T(8,128)(2,1)} %get-tuple-element.546, s32[128]{0:T(128)S(1)} %or_bitcast_fusion.2), kind=kCustom, calls=%fused_computation.2.clone.clone.1 | custom fusion | bytes 8389632 | tf_op jit(solution)/shard_map/while/body/eval_jaxpr/jit(take_along_axis)/gather | solution.py:74
  70.6 4.2 %fusion.55 = bf16[128,1,8,128]{3,2,1,0:T(8,128)(2,1)} fusion(bf16[128,128,128]{2,1,0:T(8,128)(2,1)} %gather_fusion, pred[128]{0:T(512)(128)(4,1)S(1)} %get-tuple-element.506, bf16[128,8,128]{2,1,0:T(8,128)(2,1)S(1)} %gather_fusion.1, pred[128]{0:T(512)(128)(4,1)S(1)} %get-tuple-element.508), kind=kOutput, calls=%fused_computation.11.clone.1 | convolution fusion | flops 35913728 | bytes 4718848 | tf_op jit(solution)/shard_map/while/body/eval_jaxpr/tcrn,tcnm->tcrm/dot_general | solution.py:76
  74.8 3.9 %all-to-all-start = ((bf16[128,1,8,128]{3,2,1,0:T(8,128)(2,1)}), bf16[128,1,8,128]{3,2,1,0:T(8,128)(2,1)S(1)}, u32[]{:S(2)}, u32[]{:S(2)}) async-start(bf16[128,1,8,128]{3,2,1,0:T(8,128)(2,1)} %fusion.55), calls=%async_computation | async-start | bytes 524288 | tf_op jit(solution)/shard_map/while/body/eval_jaxpr/all_to_all | solution.py:79
  78.7 0.2 fusion.56
  78.9 11.1 %all-to-all-done = bf16[128,1,8,128]{3,2,1,0:T(8,128)(2,1)S(1)} async-done(((bf16[128,1,8,128]{3,2,1,0:T(8,128)(2,1)}), bf16[128,1,8,128]{3,2,1,0:T(8,128)(2,1)S(1)}, u32[]{:S(2)}, u32[]{:S(2)}) %all-to-all-start) | async-done | bytes 262176 | tf_op jit(solution)/shard_map/while/body/eval_jaxpr/all_to_all | solution.py:79
  90.0 0.2 multiply_subtract_fusion.2
  90.5 0.7 gather_fusion.1
  91.2 6.5 %gather_fusion = bf16[128,128,128]{2,1,0:T(8,128)(2,1)} fusion(bf16[128,2,128,128]{3,2,1,0:T(8,128)(2,1)} %get-tuple-element.546, s32[128]{0:T(128)S(1)} %or_bitcast_fusion.2), kind=kCustom, calls=%fused_computation.2.clone.clone.1 | custom fusion | bytes 8389632 | tf_op jit(solution)/shard_map/while/body/eval_jaxpr/jit(take_along_axis)/gather | solution.py:74
  97.7 4.2 %fusion.55 = bf16[128,1,8,128]{3,2,1,0:T(8,128)(2,1)} fusion(bf16[128,128,128]{2,1,0:T(8,128)(2,1)} %gather_fusion, pred[128]{0:T(512)(128)(4,1)S(1)} %get-tuple-element.506, bf16[128,8,128]{2,1,0:T(8,128)(2,1)S(1)} %gather_fusion.1, pred[128]{0:T(512)(128)(4,1)S(1)} %get-tuple-element.508), kind=kOutput, calls=%fused_computation.11.clone.1 | convolution fusion | flops 35913728 | bytes 4718848 | tf_op jit(solution)/shard_map/while/body/eval_jaxpr/tcrn,tcnm->tcrm/dot_general | solution.py:76
  101.8 3.9 %all-to-all-start = ((bf16[128,1,8,128]{3,2,1,0:T(8,128)(2,1)}), bf16[128,1,8,128]{3,2,1,0:T(8,128)(2,1)S(1)}, u32[]{:S(2)}, u32[]{:S(2)}) async-start(bf16[128,1,8,128]{3,2,1,0:T(8,128)(2,1)} %fusion.55), calls=%async_computation | async-start | bytes 524288 | tf_op jit(solution)/shard_map/while/body/eval_jaxpr/all_to_all | solution.py:79
  105.8 0.2 fusion.56
  106.0 11.1 %all-to-all-done = bf16[128,1,8,128]{3,2,1,0:T(8,128)(2,1)S(1)} async-done(((bf16[128,1,8,128]{3,2,1,0:T(8,128)(2,1)}), bf16[128,1,8,128]{3,2,1,0:T(8,128)(2,1)S(1)}, u32[]{:S(2)}, u32[]{:S(2)}) %all-to-all-start) | async-done | bytes 262176 | tf_op jit(solution)/shard_map/while/body/eval_jaxpr/all_to_all | solution.py:79
  117.1 0.2 multiply_subtract_fusion.2
  117.6 0.7 gather_fusion.1
  118.3 6.5 %gather_fusion = bf16[128,128,128]{2,1,0:T(8,128)(2,1)} fusion(bf16[128,2,128,128]{3,2,1,0:T(8,128)(2,1)} %get-tuple-element.546, s32[128]{0:T(128)S(1)} %or_bitcast_fusion.2), kind=kCustom, calls=%fused_computation.2.clone.clone.1 | custom fusion | bytes 8389632 | tf_op jit(solution)/shard_map/while/body/eval_jaxpr/jit(take_along_axis)/gather | solution.py:74
  124.7 4.2 %fusion.55 = bf16[128,1,8,128]{3,2,1,0:T(8,128)(2,1)} fusion(bf16[128,128,128]{2,1,0:T(8,128)(2,1)} %gather_fusion, pred[128]{0:T(512)(128)(4,1)S(1)} %get-tuple-element.506, bf16[128,8,128]{2,1,0:T(8,128)(2,1)S(1)} %gather_fusion.1, pred[128]{0:T(512)(128)(4,1)S(1)} %get-tuple-element.508), kind=kOutput, calls=%fused_computation.11.clone.1 | convolution fusion | flops 35913728 | bytes 4718848 | tf_op jit(solution)/shard_map/while/body/eval_jaxpr/tcrn,tcnm->tcrm/dot_general | solution.py:76
  128.9 3.9 %all-to-all-start = ((bf16[128,1,8,128]{3,2,1,0:T(8,128)(2,1)}), bf16[128,1,8,128]{3,2,1,0:T(8,128)(2,1)S(1)}, u32[]{:S(2)}, u32[]{:S(2)}) async-start(bf16[128,1,8,128]{3,2,1,0:T(8,128)(2,1)} %fusion.55), calls=%async_computation | async-start | bytes 524288 | tf_op jit(solution)/shard_map/while/body/eval_jaxpr/all_to_all | solution.py:79
  132.8 0.2 fusion.56
  133.1 11.1 %all-to-all-done = bf16[128,1,8,128]{3,2,1,0:T(8,128)(2,1)S(1)} async-done(((bf16[128,1,8,128]{3,2,1,0:T(8,128)(2,1)}), bf16[128,1,8,128]{3,2,1,0:T(8,128)(2,1)S(1)}, u32[]{:S(2)}, u32[]{:S(2)}) %all-to-all-start) | async-done | bytes 262176 | tf_op jit(solution)/shard_map/while/body/eval_jaxpr/all_to_all | solution.py:79
  144.7 0.7 gather_fusion.1
  145.3 6.5 %gather_fusion = bf16[128,128,128]{2,1,0:T(8,128)(2,1)} fusion(bf16[128,2,128,128]{3,2,1,0:T(8,128)(2,1)} %get-tuple-element.546, s32[128]{0:T(128)S(1)} %or_bitcast_fusion.2), kind=kCustom, calls=%fused_computation.2.clone.clone.1 | custom fusion | bytes 8389632 | tf_op jit(solution)/shard_map/while/body/eval_jaxpr/jit(take_along_axis)/gather | solution.py:74
  151.8 4.2 %fusion.55 = bf16[128,1,8,128]{3,2,1,0:T(8,128)(2,1)} fusion(bf16[128,128,128]{2,1,0:T(8,128)(2,1)} %gather_fusion, pred[128]{0:T(512)(128)(4,1)S(1)} %get-tuple-element.506, bf16[128,8,128]{2,1,0:T(8,128)(2,1)S(1)} %gather_fusion.1, pred[128]{0:T(512)(128)(4,1)S(1)} %get-tuple-element.508), kind=kOutput, calls=%fused_computation.11.clone.1 | convolution fusion | flops 35913728 | bytes 4718848 | tf_op jit(solution)/shard_map/while/body/eval_jaxpr/tcrn,tcnm->tcrm/dot_general | solution.py:76
  156.0 3.9 %all-to-all-start = ((bf16[128,1,8,128]{3,2,1,0:T(8,128)(2,1)}), bf16[128,1,8,128]{3,2,1,0:T(8,128)(2,1)S(1)}, u32[]{:S(2)}, u32[]{:S(2)}) async-start(bf16[128,1,8,128]{3,2,1,0:T(8,128)(2,1)} %fusion.55), calls=%async_computation | async-start | bytes 524288 | tf_op jit(solution)/shard_map/while/body/eval_jaxpr/all_to_all | solution.py:79
  159.9 0.2 fusion.56
  160.1 11.1 %all-to-all-done = bf16[128,1,8,128]{3,2,1,0:T(8,128)(2,1)S(1)} async-done(((bf16[128,1,8,128]{3,2,1,0:T(8,128)(2,1)}), bf16[128,1,8,128]{3,2,1,0:T(8,128)(2,1)S(1)}, u32[]{:S(2)}, u32[]{:S(2)}) %all-to-all-start) | async-done | bytes 262176 | tf_op jit(solution)/shard_map/while/body/eval_jaxpr/all_to_all | solution.py:79
  171.5 0.7 reshape.391
  172.2 3.2 %all-to-all-start.2 = ((f32[4,1,320]{2,1,0:T(1,128)}), f32[4,1,320]{2,1,0:T(1,128)S(1)}, u32[]{:S(2)}, u32[]{:S(2)}) async-start(f32[4,1,320]{2,1,0:T(1,128)} %reshape.391), calls=%async_computation.2 | async-start | bytes 12288 | tf_op jit(solution)/shard_map/all_to_all | solution.py:16
  175.4 0.7 copy.82
  176.1 0.7 copy.83
  176.9 2.7 %all-to-all-done.2 = f32[4,1,320]{2,1,0:T(1,128)S(1)} async-done(((f32[4,1,320]{2,1,0:T(1,128)}), f32[4,1,320]{2,1,0:T(1,128)S(1)}, u32[]{:S(2)}, u32[]{:S(2)}) %all-to-all-start.2) | async-done | bytes 5152 | tf_op jit(solution)/shard_map/all_to_all | solution.py:16
  179.5 0.5 broadcast.389
  180.0 0.7 reduce.2
  180.8 0.6 multiply_bitcast_fusion
  (95 shorter events, 2.2 us)
Async XLA Ops:
  0.6 7.3 %copy-start.6 = (s32[1,128,2]{1,2,0:T(2,128)S(1)}, s32[1,128,2]{1,2,0:T(2,128)}, u32[]{:S(2)}) copy-start(s32[1,128,2]{1,2,0:T(2,128)} %param.22) | copy-start | bytes 3076
  2.2 11.5 %copy-start.5 = (s32[5,1,128]{2,1,0:T(1,128)S(1)}, s32[5,1,128]{2,1,0:T(1,128)}, u32[]{:S(2)}) copy-start(s32[5,1,128]{2,1,0:T(1,128)} %param.25) | copy-start | bytes 7684
  2.2 11.6 %copy-start.4 = (s32[5,1,128,1]{2,3,1,0:T(1,128)S(1)}, s32[5,1,128,1]{2,3,1,0:T(1,128)}, u32[]{:S(2)}) copy-start(s32[5,1,128,1]{2,3,1,0:T(1,128)} %param.24) | copy-start | bytes 7684
  2.2 23.8 %copy-start.2 = (f32[8,4096]{1,0:T(8,128)S(1)}, f32[8,4096]{1,0:T(8,128)}, u32[]{:S(2)}) copy-start(f32[8,4096]{1,0:T(8,128)} %param.17) | copy-start | bytes 393220
  2.3 23.8 %copy-start.3 = (f32[8,4096]{1,0:T(8,128)S(1)}, f32[8,4096]{1,0:T(8,128)}, u32[]{:S(2)}) copy-start(f32[8,4096]{1,0:T(8,128)} %param.16) | copy-start | bytes 393220
  2.3 23.9 %copy-start.1 = (f32[8,4096]{1,0:T(8,128)S(1)}, f32[8,4096]{1,0:T(8,128)}, u32[]{:S(2)}) copy-start(f32[8,4096]{1,0:T(8,128)} %param.15) | copy-start | bytes 393220
  2.3 33.5 %copy-start = (f32[4096]{0:T(1024)S(1)}, f32[4096]{0:T(1024)}, u32[]{:S(2)}) copy-start(f32[4096]{0:T(1024)} %param.19) | copy-start | bytes 49156
  2.3 33.5 %copy-start.7 = (f32[4096]{0:T(1024)S(1)}, f32[4096]{0:T(1024)}, u32[]{:S(2)}) copy-start(f32[4096]{0:T(1024)} %param.18) | copy-start | bytes 49156
  2.3 33.5 %copy-start.8 = (s32[32]{0:T(128)S(1)}, s32[32]{0:T(128)}, u32[]{:S(2)}) copy-start(s32[32]{0:T(128)} %param.23) | copy-start | bytes 388
  14.6 21.1 %all-to-all-start.1 = ((s32[5,128,1]{0,2,1:T(1,128)}), s32[5,128,1]{0,2,1:T(1,128)S(1)}, u32[]{:S(2)}, u32[]{:S(2)}) async-start(s32[5,128,1]{0,2,1:T(1,128)} %copy.58), calls=%async_computation.1 | async-start | bytes 131072 | tf_op jit(solution)/shard_map/all_to_all | solution.py:54
  47.4 15.6 %all-to-all-start = ((bf16[128,1,8,128]{3,2,1,0:T(8,128)(2,1)}), bf16[128,1,8,128]{3,2,1,0:T(8,128)(2,1)S(1)}, u32[]{:S(2)}, u32[]{:S(2)}) async-start(bf16[128,1,8,128]{3,2,1,0:T(8,128)(2,1)} %fusion.55), calls=%async_computation | async-start | bytes 524288 | tf_op jit(solution)/shard_map/while/body/eval_jaxpr/all_to_all | solution.py:79
  74.8 15.3 %all-to-all-start = ((bf16[128,1,8,128]{3,2,1,0:T(8,128)(2,1)}), bf16[128,1,8,128]{3,2,1,0:T(8,128)(2,1)S(1)}, u32[]{:S(2)}, u32[]{:S(2)}) async-start(bf16[128,1,8,128]{3,2,1,0:T(8,128)(2,1)} %fusion.55), calls=%async_computation | async-start | bytes 524288 | tf_op jit(solution)/shard_map/while/body/eval_jaxpr/all_to_all | solution.py:79
  101.8 15.3 %all-to-all-start = ((bf16[128,1,8,128]{3,2,1,0:T(8,128)(2,1)}), bf16[128,1,8,128]{3,2,1,0:T(8,128)(2,1)S(1)}, u32[]{:S(2)}, u32[]{:S(2)}) async-start(bf16[128,1,8,128]{3,2,1,0:T(8,128)(2,1)} %fusion.55), calls=%async_computation | async-start | bytes 524288 | tf_op jit(solution)/shard_map/while/body/eval_jaxpr/all_to_all | solution.py:79
  128.9 15.3 %all-to-all-start = ((bf16[128,1,8,128]{3,2,1,0:T(8,128)(2,1)}), bf16[128,1,8,128]{3,2,1,0:T(8,128)(2,1)S(1)}, u32[]{:S(2)}, u32[]{:S(2)}) async-start(bf16[128,1,8,128]{3,2,1,0:T(8,128)(2,1)} %fusion.55), calls=%async_computation | async-start | bytes 524288 | tf_op jit(solution)/shard_map/while/body/eval_jaxpr/all_to_all | solution.py:79
  156.0 15.3 %all-to-all-start = ((bf16[128,1,8,128]{3,2,1,0:T(8,128)(2,1)}), bf16[128,1,8,128]{3,2,1,0:T(8,128)(2,1)S(1)}, u32[]{:S(2)}, u32[]{:S(2)}) async-start(bf16[128,1,8,128]{3,2,1,0:T(8,128)(2,1)} %fusion.55), calls=%async_computation | async-start | bytes 524288 | tf_op jit(solution)/shard_map/while/body/eval_jaxpr/all_to_all | solution.py:79
  172.2 7.4 %all-to-all-start.2 = ((f32[4,1,320]{2,1,0:T(1,128)}), f32[4,1,320]{2,1,0:T(1,128)S(1)}, u32[]{:S(2)}, u32[]{:S(2)}) async-start(f32[4,1,320]{2,1,0:T(1,128)} %reshape.391), calls=%async_computation.2 | async-start | bytes 12288 | tf_op jit(solution)/shard_map/all_to_all | solution.py:16
where the time goes:
time: 182 us; the launch traced here: 181 us
  waiting for transfers between devices  67.8 us (37%)
  local copies, waits for them, and re-layouts  51.9 us (29%)
  starting transfers between devices  34.7 us (19%)
  matrix products  22.6 us (12%)
  other arithmetic  3.01 us (2%)
    all_to_all x5, waiting for transfers between devices, advance(): lax.all_to_all(outgoing, ('area', 'local'), split_axis=0, concat_axis=0,...  55.6 us
    gather x5, local copies, waits for them, and re-layouts, advance(): picked = jnp.take_along_axis(tile_table, chosen[:, :, None, None], axis=1)  32.3 us
    dot_general x5, matrix products, advance(): jnp.einsum('tcrn,tcnm->tcrm', senders, picked, preferred_element_type=jnp...  20.8 us
    all_to_all x5, starting transfers between devices, advance(): lax.all_to_all(outgoing, ('area', 'local'), split_axis=0, concat_axis=0,...  20 us
    all_to_all x1, starting transfers between devices, shards(): lax.all_to_all(dst_ids, ('area', 'local'), split_axis=1, concat_axis=1, t...  11.5 us
    all_to_all x1, waiting for transfers between devices, shards(): lax.all_to_all(dst_ids, ('area', 'local'), split_axis=1, concat_axis=1, t...  9.51 us
    gather x2, local copies, waits for them, and re-layouts, shards(): jnp.take_along_axis(jnp.broadcast_to(tile_src[0][None], table_shape), rou...  5.64 us
    gather x2, local copies, waits for them, and re-layouts, shards(): jnp.take_along_axis(jnp.broadcast_to(tile_dst[0][None], table_shape), rou...  5.64 us
  transfers between devices with their start and end apart: 7, of which 7 were waited for; matrix products, arithmetic and copies ran while one was open for 1% of the time, Pallas kernels for 0%

commit v1 on v0

v1 whole, which is shorter than its diff:
```python
import functools

import jax
import jax.numpy as jnp
from jax import lax
from jax.experimental import pallas as pl
from jax.experimental.pallas import tpu as pltpu
from jax.sharding import PartitionSpec as P

POPS = 8
BLOCK = 128
TRIALS = 8
NO_BLOCK = 64
GROUP = 8

spike_gain = 4.0
threshold = 1.0
reset_size = 0.5

VMEM = pl.BlockSpec(memory_space=pltpu.VMEM)
SMEM = pl.BlockSpec(memory_space=pltpu.SMEM)
HBM = pl.BlockSpec(memory_space=pltpu.HBM)


def params(mib, **more):
    return pltpu.CompilerParams(vmem_limit_bytes=mib << 20, **more)


def lanes(block):
    return slice(block * BLOCK, (block + 1) * BLOCK)


def spike_of(volts):
    return jax.nn.sigmoid(spike_gain * (volts - threshold))


def send_tiles(step, devs, route_ref, src_ref, blocks_ref, table_ref, tiles_ref, sems, out_ref):
    def one_round(g, carry):
        for j in range(GROUP):
            d = g * GROUP + j
            pltpu.make_async_copy(table_ref.at[d], tiles_ref.at[d], sems.at[d]).wait()
        for j in range(GROUP):
            d = g * GROUP + j
            spikes = blocks_ref[src_ref[route_ref[step, 0, d], d]]
            current = jnp.dot(spikes, tiles_ref[d], preferred_element_type=jnp.float32)
            out_ref[d, 0:TRIALS, :] = current.astype(jnp.bfloat16)
        return carry

    lax.fori_loop(0, devs // GROUP, one_round, 0)


def fetch_tiles(step, devs, tpt, route_ref, table_ref, tiles_ref, sems):
    def one(d, carry):
        pltpu.make_async_copy(
            table_ref.at[d * tpt + route_ref[step, 0, d]], tiles_ref.at[d], sems.at[d]
        ).start()
        return carry

    lax.fori_loop(0, devs, one, 0, unroll=8)


def first_kernel(
    route_ref, src_ref, volts_ref, dst_ref, routes_ref, counts_ref, table_ref,
    out_ref, spikes_ref, tiles_ref, blocks_ref, sems,
):
    devs = out_ref.shape[0]
    tpt = dst_ref.shape[0]
    steps = routes_ref.shape[0]

    fetch_tiles(0, devs, tpt, route_ref, table_ref, tiles_ref, sems)

    for b in range(blocks_ref.shape[0]):
        spikes = spike_of(volts_ref[:, lanes(b)])
        spikes_ref[:, lanes(b)] = spikes
        blocks_ref[b] = spikes.astype(jnp.bfloat16)

    step = lax.broadcasted_iota(jnp.int32, (BLOCK, devs), 0)
    targets = jnp.zeros((BLOCK, devs), jnp.int32)
    for t in range(steps):
        target = jnp.where(routes_ref[t] == 0, dst_ref[0:1, :], dst_ref[1:2, :])
        target = jnp.where(counts_ref[t] > 0, target, NO_BLOCK)
        targets = jnp.where(step == t, target, targets)
    targets = targets.astype(jnp.float32).astype(jnp.bfloat16)
    rows = lax.broadcasted_iota(jnp.int32, (devs * TRIALS, devs), 0) // TRIALS
    cols = lax.broadcasted_iota(jnp.int32, (devs * TRIALS, devs), 1)
    spread = jnp.where(rows == cols, 1.0, 0.0).astype(jnp.bfloat16)
    tails = lax.dot_general(
        spread, targets, (((1,), (1,)), ((), ())), preferred_element_type=jnp.float32
    )
    tails = tails.astype(jnp.bfloat16)
    for d in range(devs):
        out_ref[d, TRIALS:, :] = tails[d * TRIALS : (d + 1) * TRIALS, :]

    send_tiles(0, devs, route_ref, src_ref, blocks_ref, table_ref, tiles_ref, sems, out_ref)


def codes_of(tail, first):
    pick = jnp.where(
        lax.broadcasted_iota(jnp.int32, (8, BLOCK), 0)
        == lax.broadcasted_iota(jnp.int32, (8, BLOCK), 1),
        1.0,
        0.0,
    ).astype(jnp.bfloat16)
    blocks = lax.dot_general(
        pick, tail, (((1,), (1,)), ((), ())), preferred_element_type=jnp.float32
    ).astype(jnp.int32)
    trial = lax.broadcasted_iota(jnp.int32, blocks.shape, 1) % TRIALS
    return blocks * TRIALS + trial


def inflow_of(code, arrived, rows):
    row = lax.broadcasted_iota(jnp.int32, (rows, code.shape[1]), 0)
    deliver = jnp.where(row == code, 1.0, 0.0).astype(jnp.bfloat16)
    return jnp.dot(deliver, arrived, preferred_element_type=jnp.float32)


def update(b, inflow, volts_ref, cur_ref, ext_ref, spikes_ref, dsyn_ref, dmem_ref):
    at = lanes(b)
    dsyn = dsyn_ref[b : b + 1, :]
    dmem = dmem_ref[b : b + 1, :]
    cur = dsyn * cur_ref[:, at] + inflow[b * TRIALS : (b + 1) * TRIALS, :]
    volts = (
        dmem * volts_ref[:, at]
        + (1.0 - dmem) * (cur + ext_ref[:, at])
        - reset_size * spikes_ref[:, at]
    )
    return volts, cur


def step_kernel(step, *refs):
    (route_ref, src_ref, arrived_ref, codes_ref, volts_ref, cur_ref, ext_ref,
     spikes_ref, dsyn_ref, dmem_ref, table_ref) = refs[:11]
    if step == 1:
        volts_out, cur_out, spikes_out, out_ref, codes_out, tiles_ref, blocks_ref, sems = refs[11:]
    else:
        volts_out, cur_out, spikes_out, out_ref, tiles_ref, blocks_ref, sems = refs[11:]
    devs = out_ref.shape[0]
    count = blocks_ref.shape[0]
    tpt = table_ref.shape[0] // devs
    fetch_tiles(step, devs, tpt, route_ref, table_ref, tiles_ref, sems)
    if step == 1:
        tail = arrived_ref[:, TRIALS:, :].reshape(devs * TRIALS, BLOCK)
        codes = codes_of(tail, True)
        codes_out[...] = codes
        arrived = arrived_ref[:, :TRIALS, :].reshape(devs * TRIALS, BLOCK)
    else:
        codes = codes_ref[...]
        arrived = arrived_ref[...].reshape(devs * TRIALS, BLOCK)
    inflow = inflow_of(codes[step - 1 : step, :], arrived, count * TRIALS)
    for b in range(count):
        volts, cur = update(
            b, inflow, volts_ref, cur_ref, ext_ref, spikes_ref, dsyn_ref, dmem_ref
        )
        volts_out[:, lanes(b)] = volts
        cur_out[:, lanes(b)] = cur
        spikes = spike_of(volts)
        spikes_out[:, lanes(b)] = spikes
        blocks_ref[b] = spikes.astype(jnp.bfloat16)
    send_tiles(step, devs, route_ref, src_ref, blocks_ref, table_ref, tiles_ref, sems, out_ref)


def last_kernel(step, arrived_ref, codes_ref, volts_ref, cur_ref, ext_ref, spikes_ref,
                dsyn_ref, dmem_ref, volts_out, cur_out):
    devs = arrived_ref.shape[0]
    count = dsyn_ref.shape[0]
    arrived = arrived_ref[...].reshape(devs * TRIALS, BLOCK)
    inflow = inflow_of(codes_ref[step - 1 : step, :], arrived, count * TRIALS)
    for b in range(count):
        volts, cur = update(
            b, inflow, volts_ref, cur_ref, ext_ref, spikes_ref, dsyn_ref, dmem_ref
        )
        volts_out[:, lanes(b)] = volts
        cur_out[:, lanes(b)] = cur


def shards(
    potential,
    current,
    ext_drive,
    decay_syn,
    decay_mem,
    weights,
    tile_src,
    tile_dst,
    blk_pop,
    tile_route,
    counts,
):
    devs, tpt = weights.shape[1:3]
    count = blk_pop.shape[0]
    steps = tile_route.shape[0]
    f32, bf16 = jnp.float32, jnp.bfloat16
    table = weights.reshape(devs * tpt, BLOCK, BLOCK)
    src = tile_src[0].T
    dst = tile_dst[0].T
    route = tile_route.reshape(steps, 1, devs)
    used = counts.reshape(steps, 1, devs)
    dsyn = decay_syn.reshape(count, BLOCK)
    dmem = decay_mem.reshape(count, BLOCK)
    state = jax.ShapeDtypeStruct((TRIALS, count * BLOCK), f32)
    sent = jax.ShapeDtypeStruct((devs, TRIALS, BLOCK), bf16)
    scratch = [
        pltpu.VMEM((devs, BLOCK, BLOCK), bf16),
        pltpu.VMEM((count, TRIALS, BLOCK), bf16),
        pltpu.SemaphoreType.DMA((devs,)),
    ]

    def exchange(out):
        return lax.all_to_all(out, ("area", "local"), 0, 0, tiled=True)

    out, spikes = pl.pallas_call(
        first_kernel,
        out_shape=(jax.ShapeDtypeStruct((devs, 2 * TRIALS, BLOCK), bf16), state),
        in_specs=[SMEM, SMEM, VMEM, VMEM, VMEM, VMEM, HBM],
        out_specs=(VMEM, VMEM),
        scratch_shapes=scratch,
        compiler_params=params(48),
        name="first",
    )(route, src, potential, dst, route, used, table)
    arrived = exchange(out)
    volts, cur = potential, current
    codes = jnp.zeros((8, devs * TRIALS), jnp.int32)
    history = [spikes]
    for step in range(1, steps):
        outs = [state, state, state, sent]
        if step == 1:
            outs.append(jax.ShapeDtypeStruct((8, devs * TRIALS), jnp.int32))
        results = pl.pallas_call(
            functools.partial(step_kernel, step),
            out_shape=tuple(outs),
            in_specs=[SMEM, SMEM] + [VMEM] * 8 + [HBM],
            out_specs=(VMEM,) * len(outs),
            scratch_shapes=scratch,
            compiler_params=params(48),
            name=f"step{step}",
        )(route, src, arrived, codes, volts, cur, ext_drive, spikes, dsyn, dmem, table)
        volts, cur, spikes, out = results[:4]
        if step == 1:
            codes = results[4]
        history.append(spikes)
        arrived = exchange(out)
    pop_table = (blk_pop[:, None] == jnp.arange(POPS, dtype=jnp.int32)[None, :]).astype(f32)
    activity = jnp.stack([h.reshape(TRIALS, count, BLOCK).sum(axis=2) for h in history])
    rates = jnp.einsum("trb,bp->trp", activity, pop_table, precision=lax.Precision.HIGHEST)
    n_local = lax.axis_size("local")
    parts = [rates] + [
        lax.ppermute(rates, "local", [(i, (i + shift) % n_local) for i in range(n_local)])
        for shift in range(1, n_local)
    ]
    total = (parts[0] + parts[2]) + (parts[1] + parts[3])
    total = total / (BLOCK * count)
    volts, cur = pl.pallas_call(
        functools.partial(last_kernel, steps),
        out_shape=(state, state),
        in_specs=[VMEM] * 8,
        out_specs=(VMEM, VMEM),
        compiler_params=params(48),
        name="last",
    )(arrived, codes, volts, cur, ext_drive, spikes, dsyn, dmem)
    return volts, cur, total[None]


def solution(mesh):
    both = ("area", "local")
    in_specs = (
        P(None, both),
        P(None, both),
        P(None, both),
        P(both),
        P(both),
        P(both, None, None, None, None),
        P(both, None, None),
        P(both, None, None),
        P(both),
        P(None, both, None, None),
        P(None, both, None),
    )
    out_specs = (P(None, both), P(None, both), P("area", None, None, None))
    return jax.shard_map(shards, mesh=mesh, in_specs=in_specs, out_specs=out_specs, check_vma=False)
```

time: 182 us -> 125 us (0.69)
  local copies, waits for them, and re-layouts: 51.9 us -> 4.04 us
  Pallas kernels: 0 us -> 33.6 us
  matrix products: 22.6 us -> 0.14 us
  waiting for transfers between devices: 67.8 us -> 53.3 us
  starting transfers between devices: 34.7 us -> 31.6 us
  other arithmetic: 3.01 us -> 1.13 us
    gather x14 -> x0, local copies, waits for them, and re-layouts: 47 us -> none  [the longest x5 32.3 us: advance(): picked = jnp.take_along_axis(tile_table, chosen[:, :, None, None], axis=1)]
    pallas_call x0 -> x6, Pallas kernels: none -> 33.6 us  [the longest x4 26.1 us: shards(): pl.pallas_call(functools.partial(step_kernel, step), out_shape=tuple(outs...]
    dot_general x15 -> x1, matrix products: 22.6 us -> 0.14 us  [shards(): jnp.einsum('trb,bp->trp', activity, pop_table, precision=lax.Precision.HI...]
    all_to_all x7 -> x5, waiting for transfers between devices: 67.8 us -> 50.5 us  [exchange(): return lax.all_to_all(out, ('area', 'local'), 0, 0, tiled=True)]
    all_to_all x7 -> x5, starting transfers between devices: 34.7 us -> 27.2 us  [exchange(): return lax.all_to_all(out, ('area', 'local'), 0, 0, tiled=True)]
    ppermute x0 -> x3, starting transfers between devices: none -> 4.39 us  [shards(): lax.ppermute(rates, 'local', [(i, (i + shift) % n_local) for i in range(n...]
    ppermute x0 -> x3, waiting for transfers between devices: none -> 2.81 us  [shards(): lax.ppermute(rates, 'local', [(i, (i + shift) % n_local) for i in range(n...]
    unnamed x25 -> x30, local copies, waits for them, and re-layouts: 2.42 us -> 3.71 us
  transfers between devices with their start and end apart: 7 -> 8, of which waited for: 7 -> 7; matrix products, arithmetic and copies ran while one was open for 1% -> 1% of each run, Pallas kernels for 0% -> 0%
where the time goes in v1:
time: 125 us
  waiting for transfers between devices  53.3 us (43%)
  Pallas kernels  33.6 us (27%)
  starting transfers between devices  31.6 us (25%)
  local copies, waits for them, and re-layouts  4.04 us (3%)
    all_to_all x5, waiting for transfers between devices, exchange(): return lax.all_to_all(out, ('area', 'local'), 0, 0, tiled=True)  50.5 us
    all_to_all x5, starting transfers between devices, exchange(): return lax.all_to_all(out, ('area', 'local'), 0, 0, tiled=True)  27.2 us
    pallas_call x4, Pallas kernels, shards(): pl.pallas_call(functools.partial(step_kernel, step), out_shape=tuple(outs...  26.1 us
    pallas_call x1, Pallas kernels, shards(): pl.pallas_call(first_kernel, out_shape=(jax.ShapeDtypeStruct((devs, 2 * T...  6.52 us
    ppermute x3, starting transfers between devices, shards(): lax.ppermute(rates, 'local', [(i, (i + shift) % n_local) for i in range(n...  4.39 us
    unnamed x30, local copies, waits for them, and re-layouts  3.71 us
    ppermute x3, waiting for transfers between devices, shards(): lax.ppermute(rates, 'local', [(i, (i + shift) % n_local) for i in range(n...  2.81 us
  transfers between devices with their start and end apart: 8, of which 7 were waited for; matrix products, arithmetic and copies ran while one was open for 1% of the time, Pallas kernels for 0%

profile of v1, /device:TPU:1, one launch (start us, length us, event | category | flops | bytes accessed | tf_op | source)
XLA Modules:
  0.0 124.7 jit_solution(5904091869783069736)
XLA Ops:
  0.6 0.0 copy-start
  0.6 0.0 copy-start.1
  0.7 0.9 copy-done.1
  1.6 0.7 copy-done.6
  2.3 0.7 copy-done.8
  2.9 0.7 copy-done.10
  3.6 0.7 copy-done.11
  4.3 0.0 copy-start.7
  4.3 0.0 copy-start.9
  4.3 6.5 %first.1 = (bf16[128,16,128]{2,1,0:T(8,128)(2,1)}, f32[8,4096]{1,0:T(8,128)S(1)}) custom-call(s32[5,1,128]{2,1,0:T(1,128)S(1)} %bitcast.46, s32[2,128]{1,0:T(2,128)S(1)} %bitcast.52, f32[8,4096]{1,0:T(8,128)S(1)} %copy-done.1, s32[2,128]{1,0:T(2,128)S(1)} %bitcast.57, s32[5,1,128]{2,1,0:T(1,128)S(1)} %bitcast.47, s32[5,1,128]{2,1,0:T(1,128)S(1)} %copy-done.10, ...), custom_call_target="tpu_custom_call" | custom-call | tf_op jit(solution)/shard_map/first/pallas_call | solution.py:211
  10.9 11.5 %all-to-all-start = ((bf16[128,16,128]{2,1,0:T(8,128)(2,1)}), bf16[128,16,128]{2,1,0:T(8,128)(2,1)S(1)}, u32[]{:S(2)}, u32[]{:S(2)}) async-start(bf16[128,16,128]{2,1,0:T(8,128)(2,1)} %get-tuple-element.24), calls=%async_computation | async-start | bytes 1048576 | tf_op jit(solution)/shard_map/all_to_all | solution.py:209
  22.4 0.1 bitcast_reduce_fusion.4
  22.5 0.1 copy.14
  22.6 13.7 %all-to-all-done.refs_2_ = bf16[128,16,128]{2,1,0:T(8,128)(2,1)S(1)} async-done(((bf16[128,16,128]{2,1,0:T(8,128)(2,1)}), bf16[128,16,128]{2,1,0:T(8,128)(2,1)S(1)}, u32[]{:S(2)}, u32[]{:S(2)}) %all-to-all-start) | async-done | bytes 524320 | tf_op jit(solution)/shard_map/all_to_all | solution.py:209
  36.3 0.0 copy-done
  36.3 0.0 copy-done.3
  36.3 0.0 copy-done.4
  36.3 0.0 copy-done.5
  36.3 0.0 copy-done.7
  36.3 6.6 %step1.1 = (f32[8,4096]{1,0:T(8,128)S(1)}, f32[8,4096]{1,0:T(8,128)S(1)}, f32[8,4096]{1,0:T(8,128)S(1)}, bf16[128,8,128]{2,1,0:T(8,128)(2,1)}, s32[8,1024]{1,0:T(8,128)S(1)}) custom-call(s32[5,1,128]{2,1,0:T(1,128)S(1)} %bitcast.48, s32[2,128]{1,0:T(2,128)S(1)} %bitcast.53, bf16[128,16,128]{2,1,0:T(8,128)(2,1)S(1)} %all-to-all-done.refs_2_, ...), custom_call_target="tpu_custom_call" | custom-call | tf_op jit(solution)/shard_map/step1/pallas_call | solution.py:228
  43.0 3.9 %all-to-all-start.1 = ((bf16[128,8,128]{2,1,0:T(8,128)(2,1)}), bf16[128,8,128]{2,1,0:T(8,128)(2,1)S(1)}, u32[]{:S(2)}, u32[]{:S(2)}) async-start(bf16[128,8,128]{2,1,0:T(8,128)(2,1)} %get-tuple-element.26), calls=%async_computation.1 | async-start | bytes 524288 | tf_op jit(solution)/shard_map/all_to_all | solution.py:209
  46.9 0.1 bitcast_reduce_fusion.3
  47.0 0.1 copy.15
  47.0 11.2 %all-to-all-done.1.refs_2_ = bf16[128,8,128]{2,1,0:T(8,128)(2,1)S(1)} async-done(((bf16[128,8,128]{2,1,0:T(8,128)(2,1)}), bf16[128,8,128]{2,1,0:T(8,128)(2,1)S(1)}, u32[]{:S(2)}, u32[]{:S(2)}) %all-to-all-start.1) | async-done | bytes 262176 | tf_op jit(solution)/shard_map/all_to_all | solution.py:209
  58.3 6.5 %step2.1 = (f32[8,4096]{1,0:T(8,128)S(1)}, f32[8,4096]{1,0:T(8,128)S(1)}, f32[8,4096]{1,0:T(8,128)S(1)}, bf16[128,8,128]{2,1,0:T(8,128)(2,1)}) custom-call(s32[5,1,128]{2,1,0:T(1,128)S(1)} %bitcast.49, s32[2,128]{1,0:T(2,128)S(1)} %bitcast.54, bf16[128,8,128]{2,1,0:T(8,128)(2,1)S(1)} %all-to-all-done.1.refs_2_, ...), custom_call_target="tpu_custom_call" | custom-call | tf_op jit(solution)/shard_map/step2/pallas_call | solution.py:228
  64.8 3.9 %all-to-all-start.2 = ((bf16[128,8,128]{2,1,0:T(8,128)(2,1)}), bf16[128,8,128]{2,1,0:T(8,128)(2,1)S(1)}, u32[]{:S(2)}, u32[]{:S(2)}) async-start(bf16[128,8,128]{2,1,0:T(8,128)(2,1)} %get-tuple-element.31), calls=%async_computation.2 | async-start | bytes 524288 | tf_op jit(solution)/shard_map/all_to_all | solution.py:209
  68.7 0.1 bitcast_reduce_fusion.2
  68.8 0.1 copy.16
  68.9 11.2 %all-to-all-done.2.refs_2_ = bf16[128,8,128]{2,1,0:T(8,128)(2,1)S(1)} async-done(((bf16[128,8,128]{2,1,0:T(8,128)(2,1)}), bf16[128,8,128]{2,1,0:T(8,128)(2,1)S(1)}, u32[]{:S(2)}, u32[]{:S(2)}) %all-to-all-start.2) | async-done | bytes 262176 | tf_op jit(solution)/shard_map/all_to_all | solution.py:209
  80.1 6.5 %step3.1 = (f32[8,4096]{1,0:T(8,128)S(1)}, f32[8,4096]{1,0:T(8,128)S(1)}, f32[8,4096]{1,0:T(8,128)S(1)}, bf16[128,8,128]{2,1,0:T(8,128)(2,1)}) custom-call(s32[5,1,128]{2,1,0:T(1,128)S(1)} %bitcast.50, s32[2,128]{1,0:T(2,128)S(1)} %bitcast.55, bf16[128,8,128]{2,1,0:T(8,128)(2,1)S(1)} %all-to-all-done.2.refs_2_, ...), custom_call_target="tpu_custom_call" | custom-call | tf_op jit(solution)/shard_map/step3/pallas_call | solution.py:228
  86.5 3.9 %all-to-all-start.3 = ((bf16[128,8,128]{2,1,0:T(8,128)(2,1)}), bf16[128,8,128]{2,1,0:T(8,128)(2,1)S(1)}, u32[]{:S(2)}, u32[]{:S(2)}) async-start(bf16[128,8,128]{2,1,0:T(8,128)(2,1)} %get-tuple-element.35), calls=%async_computation.3 | async-start | bytes 524288 | tf_op jit(solution)/shard_map/all_to_all | solution.py:209
  90.5 0.1 bitcast_reduce_fusion.1
  90.6 0.1 copy.17
  90.7 11.2 %all-to-all-done.3.refs_2_ = bf16[128,8,128]{2,1,0:T(8,128)(2,1)S(1)} async-done(((bf16[128,8,128]{2,1,0:T(8,128)(2,1)}), bf16[128,8,128]{2,1,0:T(8,128)(2,1)S(1)}, u32[]{:S(2)}, u32[]{:S(2)}) %all-to-all-start.3) | async-done | bytes 262176 | tf_op jit(solution)/shard_map/all_to_all | solution.py:209
  101.8 6.5 %step4.1 = (f32[8,4096]{1,0:T(8,128)S(1)}, f32[8,4096]{1,0:T(8,128)S(1)}, f32[8,4096]{1,0:T(8,128)S(1)}, bf16[128,8,128]{2,1,0:T(8,128)(2,1)}) custom-call(s32[5,1,128]{2,1,0:T(1,128)S(1)} %bitcast.51, s32[2,128]{1,0:T(2,128)S(1)} %bitcast.56, bf16[128,8,128]{2,1,0:T(8,128)(2,1)S(1)} %all-to-all-done.3.refs_2_, ...), custom_call_target="tpu_custom_call" | custom-call | tf_op jit(solution)/shard_map/step4/pallas_call | solution.py:228
  108.3 3.9 %all-to-all-start.4 = ((bf16[128,8,128]{2,1,0:T(8,128)(2,1)}), bf16[128,8,128]{2,1,0:T(8,128)(2,1)S(1)}, u32[]{:S(2)}, u32[]{:S(2)}) async-start(bf16[128,8,128]{2,1,0:T(8,128)(2,1)} %get-tuple-element.39), calls=%async_computation.4 | async-start | bytes 524288 | tf_op jit(solution)/shard_map/all_to_all | solution.py:209
  112.3 0.1 bitcast_reduce_fusion
  112.4 0.1 copy.18
  112.5 0.1 fusion.1
  112.6 2.6 %collective-permute-start.2 = (f32[5,8,8]{2,1,0:T(8,128)S(1)}, f32[5,8,8]{2,1,0:T(8,128)S(1)}, u32[]{:S(2)}, u32[]{:S(2)}) collective-permute-start(f32[5,8,8]{2,1,0:T(8,128)S(1)} %fusion.1), channel_id=1, source_target_pairs={{0,3},{1,0},{2,1},{3,2},{4,7},{5,4},{6,5},{7,6},{8,11},{9,8},{10,9... | collective-permute-start | bytes 3848 | tf_op jit(solution)/shard_map/ppermute | solution.py:247
  115.3 0.0 collective-permute-start.1
  115.3 1.8 %collective-permute-start = (f32[5,8,8]{2,1,0:T(8,128)S(1)}, f32[5,8,8]{2,1,0:T(8,128)S(1)}, u32[]{:S(2)}, u32[]{:S(2)}) collective-permute-start(f32[5,8,8]{2,1,0:T(8,128)S(1)} %fusion.1), channel_id=1, source_target_pairs={{0,2},{1,3},{2,0},{3,1},{4,6},{5,7},{6,4},{7,5},{8,10},{9,11},{10,... | collective-permute-start | bytes 3848 | tf_op jit(solution)/shard_map/ppermute | solution.py:247
  117.0 0.0 collective-permute-done.2
  117.0 2.4 %collective-permute-done.1 = f32[5,8,8]{2,1,0:T(8,128)S(1)} collective-permute-done((f32[5,8,8]{2,1,0:T(8,128)S(1)}, f32[5,8,8]{2,1,0:T(8,128)S(1)}, u32[]{:S(2)}, u32[]{:S(2)}) %collective-permute-start.1) | collective-permute-done | bytes 1312 | tf_op jit(solution)/shard_map/ppermute | solution.py:247
  119.4 0.4 collective-permute-done
  119.8 0.6 multiply_bitcast_fusion
  120.4 3.2 %all-to-all-done.4.arrived_ref = bf16[128,8,128]{2,1,0:T(8,128)(2,1)S(1)} async-done(((bf16[128,8,128]{2,1,0:T(8,128)(2,1)}), bf16[128,8,128]{2,1,0:T(8,128)(2,1)S(1)}, u32[]{:S(2)}, u32[]{:S(2)}) %all-to-all-start.4) | async-done | bytes 262176 | tf_op jit(solution)/shard_map/all_to_all | solution.py:209
  123.6 1.0 last.1
  (18 shorter events, 0.0 us)
Async XLA Ops:
  0.6 35.7 %copy-start = (f32[8,4096]{1,0:T(8,128)S(1)}, f32[8,4096]{1,0:T(8,128)}, u32[]{:S(2)}) copy-start(f32[8,4096]{1,0:T(8,128)} %ext_ref.1) | copy-start | bytes 393220
  0.6 0.9 copy-start.1
  1.6 0.7 copy-start.6
  2.3 0.7 copy-start.8
  2.9 0.7 copy-start.10
  3.6 0.7 copy-start.11
  4.3 32.0 %copy-start.2 = (f32[8,4096]{1,0:T(8,128)S(1)}, f32[8,4096]{1,0:T(8,128)}, u32[]{:S(2)}) copy-start(f32[8,4096]{1,0:T(8,128)} %refs_4_.1) | copy-start | bytes 393220
  4.3 32.0 %copy-start.3 = (f32[4096]{0:T(1024)S(1)}, f32[4096]{0:T(1024)}, u32[]{:S(2)}) copy-start(f32[4096]{0:T(1024)} %param.14) | copy-start | bytes 49156
  4.3 32.0 %copy-start.4 = (f32[4096]{0:T(1024)S(1)}, f32[4096]{0:T(1024)}, u32[]{:S(2)}) copy-start(f32[4096]{0:T(1024)} %param.15) | copy-start | bytes 49156
  4.3 32.0 %copy-start.5 = (f32[8,4096]{1,0:T(8,128)S(1)}, f32[8,4096]{1,0:T(8,128)}, u32[]{:S(2)}) copy-start(f32[8,4096]{1,0:T(8,128)} %refs_5_.1) | copy-start | bytes 393220
  4.3 32.0 %copy-start.7 = (s32[5,1,128,1]{2,3,1,0:T(1,128)S(1)}, s32[5,1,128,1]{2,3,1,0:T(1,128)}, u32[]{:S(2)}) copy-start(s32[5,1,128,1]{2,3,1,0:T(1,128)} %param.20) | copy-start | bytes 7684
  4.3 32.0 %copy-start.9 = (s32[1,128,2]{1,2,0:T(2,128)S(1)}, s32[1,128,2]{1,2,0:T(2,128)}, u32[]{:S(2)}) copy-start(s32[1,128,2]{1,2,0:T(2,128)} %param.17) | copy-start | bytes 3076
  10.9 25.4 %all-to-all-start = ((bf16[128,16,128]{2,1,0:T(8,128)(2,1)}), bf16[128,16,128]{2,1,0:T(8,128)(2,1)S(1)}, u32[]{:S(2)}, u32[]{:S(2)}) async-start(bf16[128,16,128]{2,1,0:T(8,128)(2,1)} %get-tuple-element.24), calls=%async_computation | async-start | bytes 1048576 | tf_op jit(solution)/shard_map/all_to_all | solution.py:209
  43.0 15.3 %all-to-all-start.1 = ((bf16[128,8,128]{2,1,0:T(8,128)(2,1)}), bf16[128,8,128]{2,1,0:T(8,128)(2,1)S(1)}, u32[]{:S(2)}, u32[]{:S(2)}) async-start(bf16[128,8,128]{2,1,0:T(8,128)(2,1)} %get-tuple-element.26), calls=%async_computation.1 | async-start | bytes 524288 | tf_op jit(solution)/shard_map/all_to_all | solution.py:209
  64.8 15.3 %all-to-all-start.2 = ((bf16[128,8,128]{2,1,0:T(8,128)(2,1)}), bf16[128,8,128]{2,1,0:T(8,128)(2,1)S(1)}, u32[]{:S(2)}, u32[]{:S(2)}) async-start(bf16[128,8,128]{2,1,0:T(8,128)(2,1)} %get-tuple-element.31), calls=%async_computation.2 | async-start | bytes 524288 | tf_op jit(solution)/shard_map/all_to_all | solution.py:209
  80.1 32.4 %copy-start.12 = (s32[32]{0:T(128)S(1)}, s32[32]{0:T(128)}, u32[]{:S(2)}) copy-start(s32[32]{0:T(128)} %param.19) | copy-start | bytes 388
  86.5 15.3 %all-to-all-start.3 = ((bf16[128,8,128]{2,1,0:T(8,128)(2,1)}), bf16[128,8,128]{2,1,0:T(8,128)(2,1)S(1)}, u32[]{:S(2)}, u32[]{:S(2)}) async-start(bf16[128,8,128]{2,1,0:T(8,128)(2,1)} %get-tuple-element.35), calls=%async_computation.3 | async-start | bytes 524288 | tf_op jit(solution)/shard_map/all_to_all | solution.py:209
  108.3 15.3 %all-to-all-start.4 = ((bf16[128,8,128]{2,1,0:T(8,128)(2,1)}), bf16[128,8,128]{2,1,0:T(8,128)(2,1)S(1)}, u32[]{:S(2)}, u32[]{:S(2)}) async-start(bf16[128,8,128]{2,1,0:T(8,128)(2,1)} %get-tuple-element.39), calls=%async_computation.4 | async-start | bytes 524288 | tf_op jit(solution)/shard_map/all_to_all | solution.py:209
  112.6 4.4 %collective-permute-start.2 = (f32[5,8,8]{2,1,0:T(8,128)S(1)}, f32[5,8,8]{2,1,0:T(8,128)S(1)}, u32[]{:S(2)}, u32[]{:S(2)}) collective-permute-start(f32[5,8,8]{2,1,0:T(8,128)S(1)} %fusion.1), channel_id=1, source_target_pairs={{0,3},{1,0},{2,1},{3,2},{4,7},{5,4},{6,5},{7,6},{8,11},{9,8},{10,9... | collective-permute-start | bytes 3848 | tf_op jit(solution)/shard_map/ppermute | solution.py:247
  115.3 4.1 %collective-permute-start.1 = (f32[5,8,8]{2,1,0:T(8,128)S(1)}, f32[5,8,8]{2,1,0:T(8,128)S(1)}, u32[]{:S(2)}, u32[]{:S(2)}) collective-permute-start(f32[5,8,8]{2,1,0:T(8,128)S(1)} %fusion.1), channel_id=1, source_target_pairs={{0,1},{1,2},{2,3},{3,0},{4,5},{5,6},{6,7},{7,4},{8,9},{9,10},{10,1... | collective-permute-start | bytes 3848 | tf_op jit(solution)/shard_map/ppermute | solution.py:247
  115.3 4.6 %collective-permute-start = (f32[5,8,8]{2,1,0:T(8,128)S(1)}, f32[5,8,8]{2,1,0:T(8,128)S(1)}, u32[]{:S(2)}, u32[]{:S(2)}) collective-permute-start(f32[5,8,8]{2,1,0:T(8,128)S(1)} %fusion.1), channel_id=1, source_target_pairs={{0,2},{1,3},{2,0},{3,1},{4,6},{5,7},{6,4},{7,5},{8,10},{9,11},{10,... | collective-permute-start | bytes 3848 | tf_op jit(solution)/shard_map/ppermute | solution.py:247

commit v2 on v1

v2 whole, which is shorter than its diff:
```python
import functools

import jax
import jax.numpy as jnp
from jax import lax
from jax.experimental import pallas as pl
from jax.experimental.pallas import tpu as pltpu
from jax.sharding import PartitionSpec as P

POPS = 8
BLOCK = 128
TRIALS = 8
NO_BLOCK = 64
GROUP = 8
CHUNKS = 8

spike_gain = 4.0
threshold = 1.0
reset_size = 0.5

VMEM = pl.BlockSpec(memory_space=pltpu.VMEM)
HBM = pl.BlockSpec(memory_space=pltpu.HBM)


def params(mib, **more):
    return pltpu.CompilerParams(vmem_limit_bytes=mib << 20, **more)


def lanes(block):
    return slice(block * BLOCK, (block + 1) * BLOCK)


def spike_of(volts):
    return jax.nn.sigmoid(spike_gain * (volts - threshold))


def send_tiles(first, last, tpt, row, route_ref, src_ref, blocks_ref, table_ref, out_ref):
    def one_round(g, carry):
        for j in range(GROUP):
            d = g * GROUP + j
            k = route_ref[row, 0, d]
            spikes = blocks_ref[src_ref[k, d]]
            current = jnp.dot(
                spikes, table_ref[d * tpt + k], preferred_element_type=jnp.float32
            )
            out_ref[d, 0:TRIALS, :] = current.astype(jnp.bfloat16)
        return carry

    lax.fori_loop(first // GROUP, last // GROUP, one_round, 0)


def one_hot(row, col):
    return jnp.where(row == col, 1.0, 0.0).astype(jnp.bfloat16)


def population_rows(pops):
    count = pops.shape[1]
    spread = one_hot(
        lax.broadcasted_iota(jnp.int32, (count, count * TRIALS), 0),
        lax.broadcasted_iota(jnp.int32, (count, count * TRIALS), 1) // TRIALS,
    )
    pops = jnp.broadcast_to(pops.astype(jnp.float32), (TRIALS, count)).astype(jnp.bfloat16)
    pops = jnp.dot(pops, spread, preferred_element_type=jnp.float32)[0:1, :].astype(jnp.int32)
    trial = lax.broadcasted_iota(jnp.int32, pops.shape, 1) % TRIALS
    row = lax.broadcasted_iota(jnp.int32, (TRIALS * POPS, count * TRIALS), 0)
    return one_hot(row, trial * POPS + pops)


def activity_of(member, spikes):
    high = spikes.astype(jnp.bfloat16)
    low = (spikes - high.astype(jnp.float32)).astype(jnp.bfloat16)
    return jnp.dot(member, high, preferred_element_type=jnp.float32) + jnp.dot(
        member, low, preferred_element_type=jnp.float32
    )


def first_kernel(
    route_hbm, src_hbm, dst_hbm, counts_hbm, volts_hbm, pops_hbm, table_hbm,
    out_ref, spikes_ref, table_ref, act_ref,
    route_s, src_s, routes_ref, dst_ref, counts_ref, volts_ref, pops_ref,
    blocks_ref, rows_ref, sems, chunk_sems,
):
    devs = out_ref.shape[0]
    tpt = dst_ref.shape[0]
    steps = routes_ref.shape[0]
    size = table_ref.shape[0] // CHUNKS
    copies = [
        pltpu.make_async_copy(a, b, sems.at[i])
        for i, (a, b) in enumerate(
            (
                (volts_hbm, volts_ref),
                (route_hbm, routes_ref),
                (dst_hbm, dst_ref),
                (counts_hbm, counts_ref),
                (route_hbm.at[0:1], route_s),
                (src_hbm, src_s),
                (pops_hbm, pops_ref),
            )
        )
    ]
    for copy in copies:
        copy.start()
    chunks = [
        pltpu.make_async_copy(
            table_hbm.at[pl.ds(c * size, size)], table_ref.at[pl.ds(c * size, size)], chunk_sems.at[c]
        )
        for c in range(CHUNKS)
    ]
    for copy in chunks:
        copy.start()
    copies[1].wait()
    copies[2].wait()
    copies[3].wait()

    step = lax.broadcasted_iota(jnp.int32, (BLOCK, devs), 0)
    targets = jnp.zeros((BLOCK, devs), jnp.int32)
    for t in range(steps):
        target = jnp.where(routes_ref[t] == 0, dst_ref[0:1, :], dst_ref[1:2, :])
        target = jnp.where(counts_ref[t] > 0, target, NO_BLOCK)
        targets = jnp.where(step == t, target, targets)
    targets = targets.astype(jnp.float32).astype(jnp.bfloat16)
    rows = lax.broadcasted_iota(jnp.int32, (devs * TRIALS, devs), 0) // TRIALS
    cols = lax.broadcasted_iota(jnp.int32, (devs * TRIALS, devs), 1)
    tails = lax.dot_general(
        one_hot(rows, cols), targets, (((1,), (1,)), ((), ())), preferred_element_type=jnp.float32
    )
    tails = tails.astype(jnp.bfloat16)
    for d in range(devs):
        out_ref[d, TRIALS:, :] = tails[d * TRIALS : (d + 1) * TRIALS, :]

    copies[0].wait()
    for b in range(blocks_ref.shape[0]):
        spikes = spike_of(volts_ref[:, lanes(b)])
        spikes_ref[:, lanes(b)] = spikes
        rows_ref[b * TRIALS : (b + 1) * TRIALS, :] = spikes
        blocks_ref[b] = spikes.astype(jnp.bfloat16)
    copies[6].wait()
    act_ref[...] = activity_of(population_rows(pops_ref[...]), rows_ref[...])

    copies[4].wait()
    copies[5].wait()
    per_chunk = devs // CHUNKS
    for c in range(CHUNKS):
        chunks[c].wait()
        send_tiles(
            c * per_chunk, (c + 1) * per_chunk, tpt, 0, route_s, src_s, blocks_ref, table_ref, out_ref
        )


def codes_of(tail):
    pick = one_hot(
        lax.broadcasted_iota(jnp.int32, (8, BLOCK), 0),
        lax.broadcasted_iota(jnp.int32, (8, BLOCK), 1),
    )
    blocks = lax.dot_general(
        pick, tail, (((1,), (1,)), ((), ())), preferred_element_type=jnp.float32
    ).astype(jnp.int32)
    trial = lax.broadcasted_iota(jnp.int32, blocks.shape, 1) % TRIALS
    return blocks * TRIALS + trial


def inflow_of(code, arrived, rows):
    row = lax.broadcasted_iota(jnp.int32, (rows, code.shape[1]), 0)
    return jnp.dot(one_hot(row, code), arrived, preferred_element_type=jnp.float32)


def update(b, inflow, volts_ref, cur_ref, ext_ref, spikes_ref, dsyn_ref, dmem_ref):
    at = lanes(b)
    dsyn = dsyn_ref[b : b + 1, :]
    dmem = dmem_ref[b : b + 1, :]
    cur = dsyn * cur_ref[:, at] + inflow[b * TRIALS : (b + 1) * TRIALS, :]
    volts = (
        dmem * volts_ref[:, at]
        + (1.0 - dmem) * (cur + ext_ref[:, at])
        - reset_size * spikes_ref[:, at]
    )
    return volts, cur


def step_kernel(step, *refs):
    (route_ref, src_ref, arrived_ref, codes_ref, volts_ref, cur_ref, ext_ref,
     spikes_ref, dsyn_ref, dmem_ref, pops_ref, table_ref) = refs[:12]
    volts_out, cur_out, spikes_out, out_ref, act_ref = refs[12:17]
    route_s, src_s, blocks_ref, rows_ref, sems = refs[-5:]
    devs = out_ref.shape[0]
    count = blocks_ref.shape[0]
    tpt = table_ref.shape[0] // devs
    to_smem = (
        pltpu.make_async_copy(route_ref.at[step : step + 1], route_s, sems.at[0]),
        pltpu.make_async_copy(src_ref, src_s, sems.at[1]),
    )
    for copy in to_smem:
        copy.start()
    if step == 1:
        codes = codes_of(arrived_ref[:, TRIALS:, :].reshape(devs * TRIALS, BLOCK))
        refs[17][...] = codes
        arrived = arrived_ref[:, :TRIALS, :].reshape(devs * TRIALS, BLOCK)
    else:
        codes = codes_ref[...]
        arrived = arrived_ref[...].reshape(devs * TRIALS, BLOCK)
    inflow = inflow_of(codes[step - 1 : step, :], arrived, count * TRIALS)
    for b in range(count):
        volts, cur = update(
            b, inflow, volts_ref, cur_ref, ext_ref, spikes_ref, dsyn_ref, dmem_ref
        )
        volts_out[:, lanes(b)] = volts
        cur_out[:, lanes(b)] = cur
        spikes = spike_of(volts)
        spikes_out[:, lanes(b)] = spikes
        rows_ref[b * TRIALS : (b + 1) * TRIALS, :] = spikes
        blocks_ref[b] = spikes.astype(jnp.bfloat16)
    act_ref[...] = activity_of(population_rows(pops_ref[...]), rows_ref[...])
    for copy in to_smem:
        copy.wait()
    send_tiles(0, devs, tpt, 0, route_s, src_s, blocks_ref, table_ref, out_ref)


def last_kernel(step, arrived_ref, codes_ref, volts_ref, cur_ref, ext_ref, spikes_ref,
                dsyn_ref, dmem_ref, volts_out, cur_out):
    devs = arrived_ref.shape[0]
    count = dsyn_ref.shape[0]
    arrived = arrived_ref[...].reshape(devs * TRIALS, BLOCK)
    inflow = inflow_of(codes_ref[step - 1 : step, :], arrived, count * TRIALS)
    for b in range(count):
        volts, cur = update(
            b, inflow, volts_ref, cur_ref, ext_ref, spikes_ref, dsyn_ref, dmem_ref
        )
        volts_out[:, lanes(b)] = volts
        cur_out[:, lanes(b)] = cur


def shards(
    potential,
    current,
    ext_drive,
    decay_syn,
    decay_mem,
    weights,
    tile_src,
    tile_dst,
    blk_pop,
    tile_route,
    counts,
):
    devs, tpt = weights.shape[1:3]
    count = blk_pop.shape[0]
    steps = tile_route.shape[0]
    f32, bf16, i32 = jnp.float32, jnp.bfloat16, jnp.int32
    table = weights.reshape(devs * tpt, BLOCK, BLOCK)
    src = tile_src[0].T
    dst = tile_dst[0].T
    route = tile_route.reshape(steps, 1, devs)
    used = counts.reshape(steps, 1, devs)
    dsyn = decay_syn.reshape(count, BLOCK)
    dmem = decay_mem.reshape(count, BLOCK)
    pops = blk_pop.reshape(1, count)
    state = jax.ShapeDtypeStruct((TRIALS, count * BLOCK), f32)
    sent = jax.ShapeDtypeStruct((devs, TRIALS, BLOCK), bf16)
    act = jax.ShapeDtypeStruct((POPS * TRIALS, BLOCK), f32)
    scratch = [
        pltpu.SMEM((1, 1, devs), i32),
        pltpu.SMEM((tpt, devs), i32),
    ]
    blocks = [
        pltpu.VMEM((count, TRIALS, BLOCK), bf16),
        pltpu.VMEM((count * TRIALS, BLOCK), f32),
    ]

    def exchange(out):
        return lax.all_to_all(out, ("area", "local"), 0, 0, tiled=True)

    def in_hbm(array):
        return pltpu.with_memory_space_constraint(array, pltpu.HBM)

    out, spikes, local_table, activity = pl.pallas_call(
        first_kernel,
        out_shape=(
            jax.ShapeDtypeStruct((devs, 2 * TRIALS, BLOCK), bf16),
            state,
            pltpu.VMEM(table.shape, bf16),
            act,
        ),
        in_specs=[HBM] * 7,
        out_specs=(VMEM,) * 4,
        scratch_shapes=scratch
        + [
            pltpu.VMEM((steps, 1, devs), i32),
            pltpu.VMEM((tpt, devs), i32),
            pltpu.VMEM((steps, 1, devs), i32),
            pltpu.VMEM(state.shape, f32),
            pltpu.VMEM((1, count), i32),
        ]
        + blocks
        + [pltpu.SemaphoreType.DMA((7,)), pltpu.SemaphoreType.DMA((CHUNKS,))],
        compiler_params=params(8),
        name="first",
    )(*[in_hbm(a) for a in (route, src, dst, used, potential, pops, table)])
    arrived = exchange(out)
    volts, cur = potential, current
    codes = jnp.zeros((8, devs * TRIALS), i32)
    history = [activity]
    for step in range(1, steps):
        outs = [state, state, state, sent, act]
        if step == 1:
            outs.append(jax.ShapeDtypeStruct((8, devs * TRIALS), i32))
        results = pl.pallas_call(
            functools.partial(step_kernel, step),
            out_shape=tuple(outs),
            in_specs=[VMEM] * 12,
            out_specs=(VMEM,) * len(outs),
            scratch_shapes=scratch + blocks + [pltpu.SemaphoreType.DMA((2,))],
            compiler_params=params(8),
            name=f"step{step}",
        )(route, src, arrived, codes, volts, cur, ext_drive, spikes, dsyn, dmem, pops, local_table)
        volts, cur, spikes, out, activity = results[:5]
        if step == 1:
            codes = results[5]
        history.append(activity)
        if step == steps - 1:
            history, out = lax.optimization_barrier((history, out))
        arrived = exchange(out)
    rates = jnp.stack(history).sum(axis=2).reshape(steps, TRIALS, POPS)
    n_local = lax.axis_size("local")
    parts = [rates] + [
        lax.ppermute(rates, "local", [(i, (i + shift) % n_local) for i in range(n_local)])
        for shift in range(1, n_local)
    ]
    total = (parts[0] + parts[2]) + (parts[1] + parts[3])
    total = total / (BLOCK * count)
    volts, cur = pl.pallas_call(
        functools.partial(last_kernel, steps),
        out_shape=(state, state),
        in_specs=[VMEM] * 8,
        out_specs=(VMEM, VMEM),
        compiler_params=params(8),
        name="last",
    )(arrived, codes, volts, cur, ext_drive, spikes, dsyn, dmem)
    return volts, cur, total[None]


def solution(mesh):
    both = ("area", "local")
    in_specs = (
        P(None, both),
        P(None, both),
        P(None, both),
        P(both),
        P(both),
        P(both, None, None, None, None),
        P(both, None, None),
        P(both, None, None),
        P(both),
        P(None, both, None, None),
        P(None, both, None),
    )
    out_specs = (P(None, both), P(None, both), P("area", None, None, None))
    return jax.shard_map(shards, mesh=mesh, in_specs=in_specs, out_specs=out_specs, check_vma=False)
```

time: 125 us -> 110 us (0.88)
  blocking collectives: 0 us -> 70.4 us
  waiting for transfers between devices: 53.3 us -> 6.27 us
  starting transfers between devices: 31.6 us -> 8.28 us
  Pallas kernels: 33.6 us -> 23.6 us
  local copies, waits for them, and re-layouts: 4.04 us -> 0.13 us
    all_to_all x0 -> x4, blocking collectives: none -> 70.4 us  [exchange(): return lax.all_to_all(out, ('area', 'local'), 0, 0, tiled=True)]
    all_to_all x5 -> x1, waiting for transfers between devices: 50.5 us -> 3.46 us  [exchange(): return lax.all_to_all(out, ('area', 'local'), 0, 0, tiled=True)]
    all_to_all x5 -> x1, starting transfers between devices: 27.2 us -> 3.95 us  [exchange(): return lax.all_to_all(out, ('area', 'local'), 0, 0, tiled=True)]
    pallas_call x4, Pallas kernels: 26.1 us -> 16.2 us  [shards(): pl.pallas_call(functools.partial(step_kernel, step), out_shape=tuple(outs...]
    unnamed x30 -> x20, local copies, waits for them, and re-layouts: 3.71 us -> 0.05 us
  transfers between devices with their start and end apart: 8 -> 4, of which waited for: 7 -> 3; matrix products, arithmetic and copies ran while one was open for 1% -> 1% of each run, Pallas kernels for 0% -> 0%
where the time goes in v2:
time: 110 us
  blocking collectives  70.4 us (64%)
  Pallas kernels  23.6 us (21%)
  starting transfers between devices  8.28 us (8%)
  waiting for transfers between devices  6.27 us (6%)
    all_to_all x4, blocking collectives, exchange(): return lax.all_to_all(out, ('area', 'local'), 0, 0, tiled=True)  70.4 us
    pallas_call x4, Pallas kernels, shards(): pl.pallas_call(functools.partial(step_kernel, step), out_shape=tuple(outs...  16.2 us
    pallas_call x1, Pallas kernels, shards(): pl.pallas_call(first_kernel, out_shape=(jax.ShapeDtypeStruct((devs, 2 * T...  6.41 us
    ppermute x3, starting transfers between devices, shards(): lax.ppermute(rates, 'local', [(i, (i + shift) % n_local) for i in range(n...  4.34 us
    all_to_all x1, starting transfers between devices, exchange(): return lax.all_to_all(out, ('area', 'local'), 0, 0, tiled=True)  3.95 us
    all_to_all x1, waiting for transfers between devices, exchange(): return lax.all_to_all(out, ('area', 'local'), 0, 0, tiled=True)  3.46 us
    ppermute x3, waiting for transfers between devices, shards(): lax.ppermute(rates, 'local', [(i, (i + shift) % n_local) for i in range(n...  2.81 us
  transfers between devices with their start and end apart: 4, of which 3 were waited for; matrix products, arithmetic and copies ran while one was open for 1% of the time, Pallas kernels for 0%

profile of v2, /device:TPU:1, one launch (start us, length us, event | category | flops | bytes accessed | tf_op | source)
XLA Modules:
  0.0 110.3 jit_solution(12461116710547148424)
XLA Ops:
  0.6 0.0 copy-start.1
  0.6 0.0 copy-start.5
  0.7 0.0 copy-start.7
  0.7 0.0 copy-start.6
  0.7 0.0 copy-start
  0.7 0.0 copy-start.3
  0.7 0.0 copy-start.2
  0.7 0.0 copy-start.4
  0.7 6.4 %first.1 = (bf16[128,16,128]{2,1,0:T(8,128)(2,1)S(1)}, f32[8,4096]{1,0:T(8,128)S(1)}, bf16[256,128,128]{2,1,0:T(8,128)(2,1)S(1)}, f32[64,128]{1,0:T(8,128)S(1)}) custom-call(s32[5,1,128]{2,1,0:T(1,128)} %bitcast.33, s32[2,128]{1,0:T(2,128)} %bitcast.38, s32[2,128]{1,0:T(2,128)} %bitcast.49, s32[5,1,128]{2,1,0:T(1,128)} %counts_hbm.1, f32[8,4096]{1,0:T(8,128)} %refs_4_.1, ...), custom_call_target="tpu_custom_call" | custom-call | tf_op jit(solution)/shard_map/first/pallas_call | solution.py:275
  7.1 25.2 %all_to_all.25.refs_2_ = bf16[128,16,128]{2,1,0:T(8,128)(2,1)S(1)} all-to-all(bf16[128,16,128]{2,1,0:T(8,128)(2,1)S(1)} %get-tuple-element.37), channel_id=1, replica_groups=mesh['area'=32,'local'=4] {'area','local'}, dimensions={0} | all-to-all | bytes 1048576 | tf_op jit(solution)/shard_map/all_to_all | solution.py:270
  32.3 0.0 copy-done.1
  32.3 0.0 copy-done.5
  32.3 0.0 copy-done.7
  32.4 0.0 copy-done.6
  32.4 0.0 copy-done
  32.4 0.0 copy-done.3
  32.4 0.0 copy-done.2
  32.4 0.0 copy-done.4
  32.4 4.0 %step1.1 = (f32[8,4096]{1,0:T(8,128)S(1)}, f32[8,4096]{1,0:T(8,128)S(1)}, f32[8,4096]{1,0:T(8,128)S(1)}, bf16[128,8,128]{2,1,0:T(8,128)(2,1)S(1)}, f32[64,128]{1,0:T(8,128)S(1)}, /*index=5*/s32[8,1024]{1,0:T(8,128)S(1)}) custom-call(s32[5,1,128]{2,1,0:T(1,128)S(1)} %bitcast.34, s32[2,128]{1,0:T(2,128)S(1)} %bitcast.39, ...), custom_call_target="tpu_custom_call" | custom-call | tf_op jit(solution)/shard_map/step1/pallas_call | solution.py:306
  36.4 15.0 %all_to_all.26.refs_2_ = bf16[128,8,128]{2,1,0:T(8,128)(2,1)S(1)} all-to-all(bf16[128,8,128]{2,1,0:T(8,128)(2,1)S(1)} %get-tuple-element.41), channel_id=1, replica_groups=mesh['area'=32,'local'=4] {'area','local'}, dimensions={0} | all-to-all | bytes 524288 | tf_op jit(solution)/shard_map/all_to_all | solution.py:270
  51.4 3.8 %step2.1 = (f32[8,4096]{1,0:T(8,128)S(1)}, f32[8,4096]{1,0:T(8,128)S(1)}, f32[8,4096]{1,0:T(8,128)S(1)}, bf16[128,8,128]{2,1,0:T(8,128)(2,1)S(1)}, f32[64,128]{1,0:T(8,128)S(1)}) custom-call(s32[5,1,128]{2,1,0:T(1,128)S(1)} %bitcast.35, s32[2,128]{1,0:T(2,128)S(1)} %bitcast.40, bf16[128,8,128]{2,1,0:T(8,128)(2,1)S(1)} %all_to_all.26.refs_2_, ...), custom_call_target="tpu_custom_call" | custom-call | tf_op jit(solution)/shard_map/step2/pallas_call | solution.py:306
  55.2 15.1 %all_to_all.27.refs_2_ = bf16[128,8,128]{2,1,0:T(8,128)(2,1)S(1)} all-to-all(bf16[128,8,128]{2,1,0:T(8,128)(2,1)S(1)} %get-tuple-element.47), channel_id=1, replica_groups=mesh['area'=32,'local'=4] {'area','local'}, dimensions={0} | all-to-all | bytes 524288 | tf_op jit(solution)/shard_map/all_to_all | solution.py:270
  70.3 3.8 %step3.1 = (f32[8,4096]{1,0:T(8,128)S(1)}, f32[8,4096]{1,0:T(8,128)S(1)}, f32[8,4096]{1,0:T(8,128)S(1)}, bf16[128,8,128]{2,1,0:T(8,128)(2,1)S(1)}, f32[64,128]{1,0:T(8,128)S(1)}) custom-call(s32[5,1,128]{2,1,0:T(1,128)S(1)} %bitcast.36, s32[2,128]{1,0:T(2,128)S(1)} %bitcast.41, bf16[128,8,128]{2,1,0:T(8,128)(2,1)S(1)} %all_to_all.27.refs_2_, ...), custom_call_target="tpu_custom_call" | custom-call | tf_op jit(solution)/shard_map/step3/pallas_call | solution.py:306
  74.2 15.1 %all_to_all.28.refs_2_ = bf16[128,8,128]{2,1,0:T(8,128)(2,1)S(1)} all-to-all(bf16[128,8,128]{2,1,0:T(8,128)(2,1)S(1)} %get-tuple-element.52), channel_id=1, replica_groups=mesh['area'=32,'local'=4] {'area','local'}, dimensions={0} | all-to-all | bytes 524288 | tf_op jit(solution)/shard_map/all_to_all | solution.py:270
  89.3 4.5 %step4.1 = (f32[8,4096]{1,0:T(8,128)S(1)}, f32[8,4096]{1,0:T(8,128)S(1)}, f32[8,4096]{1,0:T(8,128)S(1)}, bf16[128,8,128]{2,1,0:T(8,128)(2,1)}, f32[64,128]{1,0:T(8,128)S(1)}) custom-call(s32[5,1,128]{2,1,0:T(1,128)S(1)} %bitcast.37, s32[2,128]{1,0:T(2,128)S(1)} %bitcast.42, bf16[128,8,128]{2,1,0:T(8,128)(2,1)S(1)} %all_to_all.28.refs_2_, ...), custom_call_target="tpu_custom_call" | custom-call | tf_op jit(solution)/shard_map/step4/pallas_call | solution.py:306
  93.8 3.9 %all-to-all-start.4 = ((bf16[128,8,128]{2,1,0:T(8,128)(2,1)}), bf16[128,8,128]{2,1,0:T(8,128)(2,1)S(1)}, u32[]{:S(2)}, u32[]{:S(2)}) async-start(bf16[128,8,128]{2,1,0:T(8,128)(2,1)} %get-tuple-element.58), calls=%async_computation.4 | async-start | bytes 524288 | tf_op jit(solution)/shard_map/all_to_all | solution.py:270
  97.8 0.1 reduce_sum.9
  97.9 0.1 reshape.29
  98.0 2.6 %collective-permute-start.2 = (f32[5,8,8]{2,1,0:T(8,128)S(1)}, f32[5,8,8]{2,1,0:T(8,128)S(1)}, u32[]{:S(2)}, u32[]{:S(2)}) collective-permute-start(f32[5,8,8]{2,1,0:T(8,128)S(1)} %reshape.29), channel_id=1, source_target_pairs={{0,3},{1,0},{2,1},{3,2},{4,7},{5,4},{6,5},{7,6},{8,11},{9,8},{10,9... | collective-permute-start | bytes 3848 | tf_op jit(solution)/shard_map/ppermute | solution.py:325
  100.6 0.0 collective-permute-start.1
  100.6 1.8 %collective-permute-start = (f32[5,8,8]{2,1,0:T(8,128)S(1)}, f32[5,8,8]{2,1,0:T(8,128)S(1)}, u32[]{:S(2)}, u32[]{:S(2)}) collective-permute-start(f32[5,8,8]{2,1,0:T(8,128)S(1)} %reshape.29), channel_id=1, source_target_pairs={{0,2},{1,3},{2,0},{3,1},{4,6},{5,7},{6,4},{7,5},{8,10},{9,11},{10,... | collective-permute-start | bytes 3848 | tf_op jit(solution)/shard_map/ppermute | solution.py:325
  102.4 0.0 collective-permute-done.2
  102.4 2.4 %collective-permute-done.1 = f32[5,8,8]{2,1,0:T(8,128)S(1)} collective-permute-done((f32[5,8,8]{2,1,0:T(8,128)S(1)}, f32[5,8,8]{2,1,0:T(8,128)S(1)}, u32[]{:S(2)}, u32[]{:S(2)}) %collective-permute-start.1) | collective-permute-done | bytes 1312 | tf_op jit(solution)/shard_map/ppermute | solution.py:325
  104.7 0.4 collective-permute-done
  105.2 0.6 multiply_bitcast_fusion
  105.8 3.5 %all-to-all-done.4.arrived_ref = bf16[128,8,128]{2,1,0:T(8,128)(2,1)S(1)} async-done(((bf16[128,8,128]{2,1,0:T(8,128)(2,1)}), bf16[128,8,128]{2,1,0:T(8,128)(2,1)S(1)}, u32[]{:S(2)}, u32[]{:S(2)}) %all-to-all-start.4) | async-done | bytes 262176 | tf_op jit(solution)/shard_map/all_to_all | solution.py:270
  109.2 1.0 last.1
  (6 shorter events, 0.0 us)
Async XLA Ops:
  0.6 31.7 %copy-start.1 = (f32[8,4096]{1,0:T(8,128)S(1)}, f32[8,4096]{1,0:T(8,128)}, u32[]{:S(2)}) copy-start(f32[8,4096]{1,0:T(8,128)} %refs_4_.1) | copy-start | bytes 393220
  0.6 31.7 %copy-start.5 = (s32[5,1,128,1]{2,3,1,0:T(1,128)S(1)}, s32[5,1,128,1]{2,3,1,0:T(1,128)}, u32[]{:S(2)}) copy-start(s32[5,1,128,1]{2,3,1,0:T(1,128)} %param.20) | copy-start | bytes 7684
  0.7 31.7 %copy-start.7 = (s32[32]{0:T(128)S(1)}, s32[32]{0:T(128)}, u32[]{:S(2)}) copy-start(s32[32]{0:T(128)} %param.19) | copy-start | bytes 388
  0.7 31.7 %copy-start.6 = (s32[1,128,2]{1,2,0:T(2,128)S(1)}, s32[1,128,2]{1,2,0:T(2,128)}, u32[]{:S(2)}) copy-start(s32[1,128,2]{1,2,0:T(2,128)} %param.17) | copy-start | bytes 3076
  0.7 31.7 %copy-start = (f32[8,4096]{1,0:T(8,128)S(1)}, f32[8,4096]{1,0:T(8,128)}, u32[]{:S(2)}) copy-start(f32[8,4096]{1,0:T(8,128)} %ext_ref.1) | copy-start | bytes 393220
  0.7 31.7 %copy-start.3 = (f32[4096]{0:T(1024)S(1)}, f32[4096]{0:T(1024)}, u32[]{:S(2)}) copy-start(f32[4096]{0:T(1024)} %param.15) | copy-start | bytes 49156
  0.7 31.7 %copy-start.2 = (f32[4096]{0:T(1024)S(1)}, f32[4096]{0:T(1024)}, u32[]{:S(2)}) copy-start(f32[4096]{0:T(1024)} %param.14) | copy-start | bytes 49156
  0.7 31.7 %copy-start.4 = (f32[8,4096]{1,0:T(8,128)S(1)}, f32[8,4096]{1,0:T(8,128)}, u32[]{:S(2)}) copy-start(f32[8,4096]{1,0:T(8,128)} %refs_5_.1) | copy-start | bytes 393220
  93.8 15.4 %all-to-all-start.4 = ((bf16[128,8,128]{2,1,0:T(8,128)(2,1)}), bf16[128,8,128]{2,1,0:T(8,128)(2,1)S(1)}, u32[]{:S(2)}, u32[]{:S(2)}) async-start(bf16[128,8,128]{2,1,0:T(8,128)(2,1)} %get-tuple-element.58), calls=%async_computation.4 | async-start | bytes 524288 | tf_op jit(solution)/shard_map/all_to_all | solution.py:270
  98.0 4.3 %collective-permute-start.2 = (f32[5,8,8]{2,1,0:T(8,128)S(1)}, f32[5,8,8]{2,1,0:T(8,128)S(1)}, u32[]{:S(2)}, u32[]{:S(2)}) collective-permute-start(f32[5,8,8]{2,1,0:T(8,128)S(1)} %reshape.29), channel_id=1, source_target_pairs={{0,3},{1,0},{2,1},{3,2},{4,7},{5,4},{6,5},{7,6},{8,11},{9,8},{10,9... | collective-permute-start | bytes 3848 | tf_op jit(solution)/shard_map/ppermute | solution.py:325
  100.6 4.1 %collective-permute-start.1 = (f32[5,8,8]{2,1,0:T(8,128)S(1)}, f32[5,8,8]{2,1,0:T(8,128)S(1)}, u32[]{:S(2)}, u32[]{:S(2)}) collective-permute-start(f32[5,8,8]{2,1,0:T(8,128)S(1)} %reshape.29), channel_id=1, source_target_pairs={{0,1},{1,2},{2,3},{3,0},{4,5},{5,6},{6,7},{7,4},{8,9},{9,10},{10,1... | collective-permute-start | bytes 3848 | tf_op jit(solution)/shard_map/ppermute | solution.py:325
  100.6 4.6 %collective-permute-start = (f32[5,8,8]{2,1,0:T(8,128)S(1)}, f32[5,8,8]{2,1,0:T(8,128)S(1)}, u32[]{:S(2)}, u32[]{:S(2)}) collective-permute-start(f32[5,8,8]{2,1,0:T(8,128)S(1)} %reshape.29), channel_id=1, source_target_pairs={{0,2},{1,3},{2,0},{3,1},{4,6},{5,7},{6,4},{7,5},{8,10},{9,11},{10,... | collective-permute-start | bytes 3848 | tf_op jit(solution)/shard_map/ppermute | solution.py:325

commit v3 on v2

--- a/solution.py
+++ b/solution.py
@@ -11,7 +11,6 @@
 BLOCK = 128
 TRIALS = 8
 NO_BLOCK = 64
-GROUP = 8
 CHUNKS = 8
 
 spike_gain = 4.0
@@ -35,18 +34,13 @@
 
 
 def send_tiles(first, last, tpt, row, route_ref, src_ref, blocks_ref, table_ref, out_ref):
-    def one_round(g, carry):
-        for j in range(GROUP):
-            d = g * GROUP + j
-            k = route_ref[row, 0, d]
-            spikes = blocks_ref[src_ref[k, d]]
-            current = jnp.dot(
-                spikes, table_ref[d * tpt + k], preferred_element_type=jnp.float32
-            )
-            out_ref[d, 0:TRIALS, :] = current.astype(jnp.bfloat16)
-        return carry
-
-    lax.fori_loop(first // GROUP, last // GROUP, one_round, 0)
+    for d in range(first, last, 2):
+        k, l = route_ref[row, 0, d], route_ref[row, 0, d + 1]
+        spikes = jnp.concatenate([blocks_ref[src_ref[k, d]], blocks_ref[src_ref[l, d + 1]]], axis=0)
+        tiles = jnp.concatenate([table_ref[d * tpt + k], table_ref[(d + 1) * tpt + l]], axis=1)
+        current = jnp.dot(spikes, tiles, preferred_element_type=jnp.float32).astype(jnp.bfloat16)
+        out_ref[d, 0:TRIALS, :] = current[:TRIALS, :BLOCK]
+        out_ref[d + 1, 0:TRIALS, :] = current[TRIALS:, BLOCK:]
 
 
 def one_hot(row, col):
@@ -100,14 +94,16 @@
     ]
     for copy in copies:
         copy.start()
-    chunks = [
-        pltpu.make_async_copy(
-            table_hbm.at[pl.ds(c * size, size)], table_ref.at[pl.ds(c * size, size)], chunk_sems.at[c]
-        )
-        for c in range(CHUNKS)
-    ]
-    for copy in chunks:
-        copy.start()
+
+    def chunk(c):
+        at = pl.ds(c * size, size)
+        return pltpu.make_async_copy(table_hbm.at[at], table_ref.at[at], chunk_sems.at[c])
+
+    def start(c, carry):
+        chunk(c).start()
+        return carry
+
+    lax.fori_loop(0, CHUNKS, start, 0)
     copies[1].wait()
     copies[2].wait()
     copies[3].wait()
@@ -141,7 +137,7 @@
     copies[5].wait()
     per_chunk = devs // CHUNKS
     for c in range(CHUNKS):
-        chunks[c].wait()
+        chunk(c).wait()
         send_tiles(
             c * per_chunk, (c + 1) * per_chunk, tpt, 0, route_s, src_s, blocks_ref, table_ref, out_ref
         )

time: 110 us -> 99 us (0.900)
  Pallas kernels: 23.6 us -> 12.1 us
    pallas_call x4, Pallas kernels: 16.2 us -> 7.15 us  [shards(): pl.pallas_call(functools.partial(step_kernel, step), out_shape=tuple(outs...]
    pallas_call x1, Pallas kernels: 6.41 us -> 3.95 us  [shards(): pl.pallas_call(first_kernel, out_shape=(jax.ShapeDtypeStruct((devs, 2 * T...]
where the time goes in v3:
time: 99 us; the launch traced here: 98.7 us
  blocking collectives  70.4 us (71%)
  Pallas kernels  12.1 us (12%)
  starting transfers between devices  8.28 us (8%)
  waiting for transfers between devices  6.27 us (6%)
    all_to_all x4, blocking collectives, exchange(): return lax.all_to_all(out, ('area', 'local'), 0, 0, tiled=True)  70.4 us
    pallas_call x4, Pallas kernels, shards(): pl.pallas_call(functools.partial(step_kernel, step), out_shape=tuple(outs...  7.15 us
    ppermute x3, starting transfers between devices, shards(): lax.ppermute(rates, 'local', [(i, (i + shift) % n_local) for i in range(n...  4.34 us
    pallas_call x1, Pallas kernels, shards(): pl.pallas_call(first_kernel, out_shape=(jax.ShapeDtypeStruct((devs, 2 * T...  3.95 us
    all_to_all x1, starting transfers between devices, exchange(): return lax.all_to_all(out, ('area', 'local'), 0, 0, tiled=True)  3.94 us
    all_to_all x1, waiting for transfers between devices, exchange(): return lax.all_to_all(out, ('area', 'local'), 0, 0, tiled=True)  3.46 us
    ppermute x3, waiting for transfers between devices, shards(): lax.ppermute(rates, 'local', [(i, (i + shift) % n_local) for i in range(n...  2.81 us
  transfers between devices with their start and end apart: 4, of which 3 were waited for; matrix products, arithmetic and copies ran while one was open for 1% of the time, Pallas kernels for 0%

profile of v3, /device:TPU:1, one launch (start us, length us, event | category | flops | bytes accessed | tf_op | source)
XLA Modules:
  0.0 98.7 jit_solution(13708490589235023493)
XLA Ops:
  0.6 0.0 copy-start.1
  0.6 0.0 copy-start.5
  0.7 0.0 copy-start.7
  0.7 0.0 copy-start.6
  0.7 0.0 copy-start
  0.7 0.0 copy-start.3
  0.7 0.0 copy-start.2
  0.7 0.0 copy-start.4
  0.7 3.9 %first.1 = (bf16[128,16,128]{2,1,0:T(8,128)(2,1)S(1)}, f32[8,4096]{1,0:T(8,128)S(1)}, bf16[256,128,128]{2,1,0:T(8,128)(2,1)S(1)}, f32[64,128]{1,0:T(8,128)S(1)}) custom-call(s32[5,1,128]{2,1,0:T(1,128)} %bitcast.33, s32[2,128]{1,0:T(2,128)} %bitcast.38, s32[2,128]{1,0:T(2,128)} %bitcast.49, s32[5,1,128]{2,1,0:T(1,128)} %counts_hbm.1, f32[8,4096]{1,0:T(8,128)} %refs_4_.1, ...), custom_call_target="tpu_custom_call" | custom-call | tf_op jit(solution)/shard_map/first/pallas_call | solution.py:271
  4.7 25.2 %all_to_all.25.refs_2_ = bf16[128,16,128]{2,1,0:T(8,128)(2,1)S(1)} all-to-all(bf16[128,16,128]{2,1,0:T(8,128)(2,1)S(1)} %get-tuple-element.37), channel_id=1, replica_groups=mesh['area'=32,'local'=4] {'area','local'}, dimensions={0} | all-to-all | bytes 1048576 | tf_op jit(solution)/shard_map/all_to_all | solution.py:266
  29.9 0.0 copy-done.1
  29.9 0.0 copy-done.5
  29.9 0.0 copy-done.7
  29.9 0.0 copy-done.6
  29.9 0.0 copy-done
  29.9 0.0 copy-done.3
  29.9 0.0 copy-done.2
  29.9 0.0 copy-done.4
  29.9 1.7 %step1.1 = (f32[8,4096]{1,0:T(8,128)S(1)}, f32[8,4096]{1,0:T(8,128)S(1)}, f32[8,4096]{1,0:T(8,128)S(1)}, bf16[128,8,128]{2,1,0:T(8,128)(2,1)S(1)}, f32[64,128]{1,0:T(8,128)S(1)}, /*index=5*/s32[8,1024]{1,0:T(8,128)S(1)}) custom-call(s32[5,1,128]{2,1,0:T(1,128)S(1)} %bitcast.34, s32[2,128]{1,0:T(2,128)S(1)} %bitcast.39, ...), custom_call_target="tpu_custom_call" | custom-call | tf_op jit(solution)/shard_map/step1/pallas_call | solution.py:302
  31.7 15.0 %all_to_all.26.refs_2_ = bf16[128,8,128]{2,1,0:T(8,128)(2,1)S(1)} all-to-all(bf16[128,8,128]{2,1,0:T(8,128)(2,1)S(1)} %get-tuple-element.41), channel_id=1, replica_groups=mesh['area'=32,'local'=4] {'area','local'}, dimensions={0} | all-to-all | bytes 524288 | tf_op jit(solution)/shard_map/all_to_all | solution.py:266
  46.7 1.6 %step2.1 = (f32[8,4096]{1,0:T(8,128)S(1)}, f32[8,4096]{1,0:T(8,128)S(1)}, f32[8,4096]{1,0:T(8,128)S(1)}, bf16[128,8,128]{2,1,0:T(8,128)(2,1)S(1)}, f32[64,128]{1,0:T(8,128)S(1)}) custom-call(s32[5,1,128]{2,1,0:T(1,128)S(1)} %bitcast.35, s32[2,128]{1,0:T(2,128)S(1)} %bitcast.40, bf16[128,8,128]{2,1,0:T(8,128)(2,1)S(1)} %all_to_all.26.refs_2_, ...), custom_call_target="tpu_custom_call" | custom-call | tf_op jit(solution)/shard_map/step2/pallas_call | solution.py:302
  48.3 15.1 %all_to_all.27.refs_2_ = bf16[128,8,128]{2,1,0:T(8,128)(2,1)S(1)} all-to-all(bf16[128,8,128]{2,1,0:T(8,128)(2,1)S(1)} %get-tuple-element.47), channel_id=1, replica_groups=mesh['area'=32,'local'=4] {'area','local'}, dimensions={0} | all-to-all | bytes 524288 | tf_op jit(solution)/shard_map/all_to_all | solution.py:266
  63.3 1.6 %step3.1 = (f32[8,4096]{1,0:T(8,128)S(1)}, f32[8,4096]{1,0:T(8,128)S(1)}, f32[8,4096]{1,0:T(8,128)S(1)}, bf16[128,8,128]{2,1,0:T(8,128)(2,1)S(1)}, f32[64,128]{1,0:T(8,128)S(1)}) custom-call(s32[5,1,128]{2,1,0:T(1,128)S(1)} %bitcast.36, s32[2,128]{1,0:T(2,128)S(1)} %bitcast.41, bf16[128,8,128]{2,1,0:T(8,128)(2,1)S(1)} %all_to_all.27.refs_2_, ...), custom_call_target="tpu_custom_call" | custom-call | tf_op jit(solution)/shard_map/step3/pallas_call | solution.py:302
  64.9 15.1 %all_to_all.28.refs_2_ = bf16[128,8,128]{2,1,0:T(8,128)(2,1)S(1)} all-to-all(bf16[128,8,128]{2,1,0:T(8,128)(2,1)S(1)} %get-tuple-element.52), channel_id=1, replica_groups=mesh['area'=32,'local'=4] {'area','local'}, dimensions={0} | all-to-all | bytes 524288 | tf_op jit(solution)/shard_map/all_to_all | solution.py:266
  80.0 2.3 %step4.1 = (f32[8,4096]{1,0:T(8,128)S(1)}, f32[8,4096]{1,0:T(8,128)S(1)}, f32[8,4096]{1,0:T(8,128)S(1)}, bf16[128,8,128]{2,1,0:T(8,128)(2,1)}, f32[64,128]{1,0:T(8,128)S(1)}) custom-call(s32[5,1,128]{2,1,0:T(1,128)S(1)} %bitcast.37, s32[2,128]{1,0:T(2,128)S(1)} %bitcast.42, bf16[128,8,128]{2,1,0:T(8,128)(2,1)S(1)} %all_to_all.28.refs_2_, ...), custom_call_target="tpu_custom_call" | custom-call | tf_op jit(solution)/shard_map/step4/pallas_call | solution.py:302
  82.3 3.9 %all-to-all-start.4 = ((bf16[128,8,128]{2,1,0:T(8,128)(2,1)}), bf16[128,8,128]{2,1,0:T(8,128)(2,1)S(1)}, u32[]{:S(2)}, u32[]{:S(2)}) async-start(bf16[128,8,128]{2,1,0:T(8,128)(2,1)} %get-tuple-element.58), calls=%async_computation.4 | async-start | bytes 524288 | tf_op jit(solution)/shard_map/all_to_all | solution.py:266
  86.3 0.1 reduce_sum.9
  86.4 0.1 reshape.29
  86.5 2.6 %collective-permute-start.2 = (f32[5,8,8]{2,1,0:T(8,128)S(1)}, f32[5,8,8]{2,1,0:T(8,128)S(1)}, u32[]{:S(2)}, u32[]{:S(2)}) collective-permute-start(f32[5,8,8]{2,1,0:T(8,128)S(1)} %reshape.29), channel_id=1, source_target_pairs={{0,3},{1,0},{2,1},{3,2},{4,7},{5,4},{6,5},{7,6},{8,11},{9,8},{10,9... | collective-permute-start | bytes 3848 | tf_op jit(solution)/shard_map/ppermute | solution.py:321
  89.1 0.0 collective-permute-start.1
  89.1 1.8 %collective-permute-start = (f32[5,8,8]{2,1,0:T(8,128)S(1)}, f32[5,8,8]{2,1,0:T(8,128)S(1)}, u32[]{:S(2)}, u32[]{:S(2)}) collective-permute-start(f32[5,8,8]{2,1,0:T(8,128)S(1)} %reshape.29), channel_id=1, source_target_pairs={{0,2},{1,3},{2,0},{3,1},{4,6},{5,7},{6,4},{7,5},{8,10},{9,11},{10,... | collective-permute-start | bytes 3848 | tf_op jit(solution)/shard_map/ppermute | solution.py:321
  90.8 0.0 collective-permute-done.2
  90.8 2.4 %collective-permute-done.1 = f32[5,8,8]{2,1,0:T(8,128)S(1)} collective-permute-done((f32[5,8,8]{2,1,0:T(8,128)S(1)}, f32[5,8,8]{2,1,0:T(8,128)S(1)}, u32[]{:S(2)}, u32[]{:S(2)}) %collective-permute-start.1) | collective-permute-done | bytes 1312 | tf_op jit(solution)/shard_map/ppermute | solution.py:321
  93.2 0.4 collective-permute-done
  93.6 0.6 multiply_bitcast_fusion
  94.3 3.5 %all-to-all-done.4.arrived_ref = bf16[128,8,128]{2,1,0:T(8,128)(2,1)S(1)} async-done(((bf16[128,8,128]{2,1,0:T(8,128)(2,1)}), bf16[128,8,128]{2,1,0:T(8,128)(2,1)S(1)}, u32[]{:S(2)}, u32[]{:S(2)}) %all-to-all-start.4) | async-done | bytes 262176 | tf_op jit(solution)/shard_map/all_to_all | solution.py:266
  97.7 1.0 %last.1 = (f32[8,4096]{1,0:T(8,128)}, f32[8,4096]{1,0:T(8,128)}) custom-call(bf16[128,8,128]{2,1,0:T(8,128)(2,1)S(1)} %all-to-all-done.4.arrived_ref, s32[8,1024]{1,0:T(8,128)S(1)} %get-tuple-element.42.refs_3_.codes_ref, f32[8,4096]{1,0:T(8,128)S(1)} %get-tuple-element.59.volts_ref, f32[8,4096]{1,0:T(8,128)S(1)} %get-tuple-element.60.cur_ref, ...), custom_call_target="tpu_custom_call" | custom-call | tf_op jit(solution)/shard_map/last/pallas_call | solution.py:326
  (6 shorter events, 0.0 us)
Async XLA Ops:
  0.6 29.2 %copy-start.1 = (f32[8,4096]{1,0:T(8,128)S(1)}, f32[8,4096]{1,0:T(8,128)}, u32[]{:S(2)}) copy-start(f32[8,4096]{1,0:T(8,128)} %refs_4_.1) | copy-start | bytes 393220
  0.6 29.2 %copy-start.5 = (s32[5,1,128,1]{2,3,1,0:T(1,128)S(1)}, s32[5,1,128,1]{2,3,1,0:T(1,128)}, u32[]{:S(2)}) copy-start(s32[5,1,128,1]{2,3,1,0:T(1,128)} %param.20) | copy-start | bytes 7684
  0.7 29.2 %copy-start.7 = (s32[32]{0:T(128)S(1)}, s32[32]{0:T(128)}, u32[]{:S(2)}) copy-start(s32[32]{0:T(128)} %param.19) | copy-start | bytes 388
  0.7 29.2 %copy-start.6 = (s32[1,128,2]{1,2,0:T(2,128)S(1)}, s32[1,128,2]{1,2,0:T(2,128)}, u32[]{:S(2)}) copy-start(s32[1,128,2]{1,2,0:T(2,128)} %param.17) | copy-start | bytes 3076
  0.7 29.2 %copy-start = (f32[8,4096]{1,0:T(8,128)S(1)}, f32[8,4096]{1,0:T(8,128)}, u32[]{:S(2)}) copy-start(f32[8,4096]{1,0:T(8,128)} %ext_ref.1) | copy-start | bytes 393220
  0.7 29.2 %copy-start.3 = (f32[4096]{0:T(1024)S(1)}, f32[4096]{0:T(1024)}, u32[]{:S(2)}) copy-start(f32[4096]{0:T(1024)} %param.15) | copy-start | bytes 49156
  0.7 29.2 %copy-start.2 = (f32[4096]{0:T(1024)S(1)}, f32[4096]{0:T(1024)}, u32[]{:S(2)}) copy-start(f32[4096]{0:T(1024)} %param.14) | copy-start | bytes 49156
  0.7 29.2 %copy-start.4 = (f32[8,4096]{1,0:T(8,128)S(1)}, f32[8,4096]{1,0:T(8,128)}, u32[]{:S(2)}) copy-start(f32[8,4096]{1,0:T(8,128)} %refs_5_.1) | copy-start | bytes 393220
  82.3 15.4 %all-to-all-start.4 = ((bf16[128,8,128]{2,1,0:T(8,128)(2,1)}), bf16[128,8,128]{2,1,0:T(8,128)(2,1)S(1)}, u32[]{:S(2)}, u32[]{:S(2)}) async-start(bf16[128,8,128]{2,1,0:T(8,128)(2,1)} %get-tuple-element.58), calls=%async_computation.4 | async-start | bytes 524288 | tf_op jit(solution)/shard_map/all_to_all | solution.py:266
  86.5 4.3 %collective-permute-start.2 = (f32[5,8,8]{2,1,0:T(8,128)S(1)}, f32[5,8,8]{2,1,0:T(8,128)S(1)}, u32[]{:S(2)}, u32[]{:S(2)}) collective-permute-start(f32[5,8,8]{2,1,0:T(8,128)S(1)} %reshape.29), channel_id=1, source_target_pairs={{0,3},{1,0},{2,1},{3,2},{4,7},{5,4},{6,5},{7,6},{8,11},{9,8},{10,9... | collective-permute-start | bytes 3848 | tf_op jit(solution)/shard_map/ppermute | solution.py:321
  89.1 4.1 %collective-permute-start.1 = (f32[5,8,8]{2,1,0:T(8,128)S(1)}, f32[5,8,8]{2,1,0:T(8,128)S(1)}, u32[]{:S(2)}, u32[]{:S(2)}) collective-permute-start(f32[5,8,8]{2,1,0:T(8,128)S(1)} %reshape.29), channel_id=1, source_target_pairs={{0,1},{1,2},{2,3},{3,0},{4,5},{5,6},{6,7},{7,4},{8,9},{9,10},{10,1... | collective-permute-start | bytes 3848 | tf_op jit(solution)/shard_map/ppermute | solution.py:321
  89.1 4.6 %collective-permute-start = (f32[5,8,8]{2,1,0:T(8,128)S(1)}, f32[5,8,8]{2,1,0:T(8,128)S(1)}, u32[]{:S(2)}, u32[]{:S(2)}) collective-permute-start(f32[5,8,8]{2,1,0:T(8,128)S(1)} %reshape.29), channel_id=1, source_target_pairs={{0,2},{1,3},{2,0},{3,1},{4,6},{5,7},{6,4},{7,5},{8,10},{9,11},{10,... | collective-permute-start | bytes 3848 | tf_op jit(solution)/shard_map/ppermute | solution.py:321

commit v4 on v3

--- a/solution.py
+++ b/solution.py
@@ -11,7 +11,9 @@
 BLOCK = 128
 TRIALS = 8
 NO_BLOCK = 64
-CHUNKS = 8
+EXTRA = 2
+CHUNK = 16
+WHOLE = 32
 
 spike_gain = 4.0
 threshold = 1.0
@@ -33,14 +35,14 @@
     return jax.nn.sigmoid(spike_gain * (volts - threshold))
 
 
-def send_tiles(first, last, tpt, row, route_ref, src_ref, blocks_ref, table_ref, out_ref):
+def send_tiles(first, last, tile_of, route_ref, src_ref, blocks_ref, tiles_ref, store):
     for d in range(first, last, 2):
-        k, l = route_ref[row, 0, d], route_ref[row, 0, d + 1]
+        k, l = route_ref[0, 0, d], route_ref[0, 0, d + 1]
         spikes = jnp.concatenate([blocks_ref[src_ref[k, d]], blocks_ref[src_ref[l, d + 1]]], axis=0)
-        tiles = jnp.concatenate([table_ref[d * tpt + k], table_ref[(d + 1) * tpt + l]], axis=1)
+        tiles = jnp.concatenate([tiles_ref[tile_of(d, k)], tiles_ref[tile_of(d + 1, l)]], axis=1)
         current = jnp.dot(spikes, tiles, preferred_element_type=jnp.float32).astype(jnp.bfloat16)
-        out_ref[d, 0:TRIALS, :] = current[:TRIALS, :BLOCK]
-        out_ref[d + 1, 0:TRIALS, :] = current[TRIALS:, BLOCK:]
+        store(d, current[:TRIALS, :BLOCK])
+        store(d + 1, current[TRIALS:, BLOCK:])
 
 
 def one_hot(row, col):
@@ -70,24 +72,22 @@
 
 def first_kernel(
     route_hbm, src_hbm, dst_hbm, counts_hbm, volts_hbm, pops_hbm, table_hbm,
-    out_ref, spikes_ref, table_ref, act_ref,
-    route_s, src_s, routes_ref, dst_ref, counts_ref, volts_ref, pops_ref,
-    blocks_ref, rows_ref, sems, chunk_sems,
+    out_ref, spikes_ref, act_ref,
+    route_s, src_s, routes_ref, dst_ref, counts_ref, volts_ref, pops_ref, tiles_ref,
+    blocks_ref, rows_ref, sems, whole_sems, routed_sems,
 ):
-    devs = out_ref.shape[0]
-    tpt = dst_ref.shape[0]
+    tpt, devs = dst_ref.shape
     steps = routes_ref.shape[0]
-    size = table_ref.shape[0] // CHUNKS
     copies = [
         pltpu.make_async_copy(a, b, sems.at[i])
         for i, (a, b) in enumerate(
             (
+                (route_hbm.at[0:1], route_s),
+                (src_hbm, src_s),
                 (volts_hbm, volts_ref),
                 (route_hbm, routes_ref),
                 (dst_hbm, dst_ref),
                 (counts_hbm, counts_ref),
-                (route_hbm.at[0:1], route_s),
-                (src_hbm, src_s),
                 (pops_hbm, pops_ref),
             )
         )
@@ -95,18 +95,30 @@
     for copy in copies:
         copy.start()
 
-    def chunk(c):
-        at = pl.ds(c * size, size)
-        return pltpu.make_async_copy(table_hbm.at[at], table_ref.at[at], chunk_sems.at[c])
-
-    def start(c, carry):
-        chunk(c).start()
+    def whole(c):
+        at = pl.ds(c * CHUNK * tpt, CHUNK * tpt)
+        return pltpu.make_async_copy(table_hbm.at[at], tiles_ref.at[at], whole_sems.at[c])
+
+    def start_whole(c, carry):
+        whole(c).start()
         return carry
 
-    lax.fori_loop(0, CHUNKS, start, 0)
-    copies[1].wait()
-    copies[2].wait()
-    copies[3].wait()
+    lax.fori_loop(0, WHOLE // CHUNK, start_whole, 0)
+    copies[0].wait()
+
+    base = WHOLE * tpt - WHOLE
+
+    def start_routed(c, carry):
+        for j in range(CHUNK):
+            d = WHOLE + c * CHUNK + j
+            pltpu.make_async_copy(
+                table_hbm.at[d * tpt + route_s[0, 0, d]], tiles_ref.at[base + d], routed_sems.at[c]
+            ).start()
+        return carry
+
+    lax.fori_loop(0, (devs - WHOLE) // CHUNK, start_routed, 0)
+    for copy in copies[3:6]:
+        copy.wait()
 
     step = lax.broadcasted_iota(jnp.int32, (BLOCK, devs), 0)
     targets = jnp.zeros((BLOCK, devs), jnp.int32)
@@ -115,16 +127,17 @@
         target = jnp.where(counts_ref[t] > 0, target, NO_BLOCK)
         targets = jnp.where(step == t, target, targets)
     targets = targets.astype(jnp.float32).astype(jnp.bfloat16)
-    rows = lax.broadcasted_iota(jnp.int32, (devs * TRIALS, devs), 0) // TRIALS
-    cols = lax.broadcasted_iota(jnp.int32, (devs * TRIALS, devs), 1)
-    tails = lax.dot_general(
+    rows = lax.broadcasted_iota(jnp.int32, (devs * EXTRA, devs), 0) // EXTRA
+    cols = lax.broadcasted_iota(jnp.int32, (devs * EXTRA, devs), 1)
+    extra = lax.dot_general(
         one_hot(rows, cols), targets, (((1,), (1,)), ((), ())), preferred_element_type=jnp.float32
     )
-    tails = tails.astype(jnp.bfloat16)
+    extra = extra.astype(jnp.bfloat16)
+    long = TRIALS + EXTRA
     for d in range(devs):
-        out_ref[d, TRIALS:, :] = tails[d * TRIALS : (d + 1) * TRIALS, :]
-
-    copies[0].wait()
+        out_ref[d * long + TRIALS : (d + 1) * long, :] = extra[d * EXTRA : (d + 1) * EXTRA, :]
+
+    copies[2].wait()
     for b in range(blocks_ref.shape[0]):
         spikes = spike_of(volts_ref[:, lanes(b)])
         spikes_ref[:, lanes(b)] = spikes
@@ -132,27 +145,53 @@
         blocks_ref[b] = spikes.astype(jnp.bfloat16)
     copies[6].wait()
     act_ref[...] = activity_of(population_rows(pops_ref[...]), rows_ref[...])
-
-    copies[4].wait()
-    copies[5].wait()
-    per_chunk = devs // CHUNKS
-    for c in range(CHUNKS):
-        chunk(c).wait()
+    copies[1].wait()
+
+    def store(d, current):
+        out_ref[d * long : d * long + TRIALS, :] = current
+
+    for c in range(WHOLE // CHUNK):
+        whole(c).wait()
         send_tiles(
-            c * per_chunk, (c + 1) * per_chunk, tpt, 0, route_s, src_s, blocks_ref, table_ref, out_ref
+            c * CHUNK, (c + 1) * CHUNK, lambda d, k: d * tpt + k, route_s, src_s, blocks_ref, tiles_ref, store
         )
-
-
-def codes_of(tail):
-    pick = one_hot(
-        lax.broadcasted_iota(jnp.int32, (8, BLOCK), 0),
-        lax.broadcasted_iota(jnp.int32, (8, BLOCK), 1),
-    )
-    blocks = lax.dot_general(
-        pick, tail, (((1,), (1,)), ((), ())), preferred_element_type=jnp.float32
-    ).astype(jnp.int32)
-    trial = lax.broadcasted_iota(jnp.int32, blocks.shape, 1) % TRIALS
-    return blocks * TRIALS + trial
+    for c in range((devs - WHOLE) // CHUNK):
+        at = WHOLE + c * CHUNK
+        pltpu.make_async_copy(
+            table_hbm.at[pl.ds(0, CHUNK)], tiles_ref.at[pl.ds(base + at, CHUNK)], routed_sems.at[c]
+        ).wait()
+        send_tiles(
+            at, at + CHUNK, lambda d, k: base + d, route_s, src_s, blocks_ref, tiles_ref, store
+        )
+
+
+def iotas(shape):
+    return lax.broadcasted_iota(jnp.int32, shape, 0), lax.broadcasted_iota(jnp.int32, shape, 1)
+
+
+def codes_of(message, devs):
+    long = TRIALS + EXTRA
+    read = lax.dot_general(
+        one_hot(*iotas((8, BLOCK))), message, (((1,), (1,)), ((), ())), preferred_element_type=jnp.float32
+    )
+    place = lax.broadcasted_iota(jnp.int32, read.shape, 1) % long
+    blocks = jnp.where(place >= TRIALS, read, 0.0)
+    near = blocks
+    width = near.shape[1]
+    near = pltpu.roll(near, width - 2, 1)
+    near = near + pltpu.roll(near, width - 2, 1)
+    near = near + pltpu.roll(near, width - 4, 1)
+    here = jnp.where(place < TRIALS, near.astype(jnp.int32) * TRIALS + place, -1)
+    row, col = iotas((devs * long, devs))
+    one = jnp.dot(
+        jnp.where(place == TRIALS, blocks, 0.0).astype(jnp.bfloat16),
+        one_hot(row // long, col),
+        preferred_element_type=jnp.float32,
+    ).astype(jnp.bfloat16)
+    row, col = iotas((devs, devs * TRIALS))
+    later = jnp.dot(one, one_hot(row, col // TRIALS), preferred_element_type=jnp.float32)
+    trial = lax.broadcasted_iota(jnp.int32, later.shape, 1) % TRIALS
+    return here, later.astype(jnp.int32) * TRIALS + trial
 
 
 def inflow_of(code, arrived, rows):
@@ -188,9 +227,9 @@
     for copy in to_smem:
         copy.start()
     if step == 1:
-        codes = codes_of(arrived_ref[:, TRIALS:, :].reshape(devs * TRIALS, BLOCK))
-        refs[17][...] = codes
-        arrived = arrived_ref[:, :TRIALS, :].reshape(devs * TRIALS, BLOCK)
+        arrived = arrived_ref[...]
+        codes, later = codes_of(arrived, devs)
+        refs[17][...] = later
     else:
         codes = codes_ref[...]
         arrived = arrived_ref[...].reshape(devs * TRIALS, BLOCK)
@@ -208,7 +247,11 @@
     act_ref[...] = activity_of(population_rows(pops_ref[...]), rows_ref[...])
     for copy in to_smem:
         copy.wait()
-    send_tiles(0, devs, tpt, 0, route_s, src_s, blocks_ref, table_ref, out_ref)
+
+    def store(d, current):
+        out_ref[d] = current
+
+    send_tiles(0, devs, lambda d, k: d * tpt + k, route_s, src_s, blocks_ref, table_ref, store)
 
 
 def last_kernel(step, arrived_ref, codes_ref, volts_ref, cur_ref, ext_ref, spikes_ref,
@@ -268,16 +311,12 @@
     def in_hbm(array):
         return pltpu.with_memory_space_constraint(array, pltpu.HBM)
 
-    out, spikes, local_table, activity = pl.pallas_call(
+    long = TRIALS + EXTRA
+    out, spikes, activity = pl.pallas_call(
         first_kernel,
-        out_shape=(
-            jax.ShapeDtypeStruct((devs, 2 * TRIALS, BLOCK), bf16),
-            state,
-            pltpu.VMEM(table.shape, bf16),
-            act,
-        ),
+        out_shape=(jax.ShapeDtypeStruct((devs * long, BLOCK), bf16), state, act),
         in_specs=[HBM] * 7,
-        out_specs=(VMEM,) * 4,
+        out_specs=(VMEM,) * 3,
         scratch_shapes=scratch
         + [
             pltpu.VMEM((steps, 1, devs), i32),
@@ -285,18 +324,26 @@
             pltpu.VMEM((steps, 1, devs), i32),
             pltpu.VMEM(state.shape, f32),
             pltpu.VMEM((1, count), i32),
+            pltpu.VMEM((devs + WHOLE * (tpt - 1), BLOCK, BLOCK), bf16),
         ]
         + blocks
-        + [pltpu.SemaphoreType.DMA((7,)), pltpu.SemaphoreType.DMA((CHUNKS,))],
-        compiler_params=params(8),
+        + [
+            pltpu.SemaphoreType.DMA((7,)),
+            pltpu.SemaphoreType.DMA((WHOLE // CHUNK,)),
+            pltpu.SemaphoreType.DMA(((devs - WHOLE) // CHUNK,)),
+        ],
+        compiler_params=params(16),
         name="first",
     )(*[in_hbm(a) for a in (route, src, dst, used, potential, pops, table)])
-    arrived = exchange(out)
+    arrived = exchange(out.reshape(devs, long // 2, 2, BLOCK)).reshape(devs * long, BLOCK)
+    local_table = table
     volts, cur = potential, current
     codes = jnp.zeros((8, devs * TRIALS), i32)
     history = [activity]
     for step in range(1, steps):
         outs = [state, state, state, sent, act]
+        if step == steps - 1:
+            outs[3] = pltpu.VMEM(sent.shape, bf16)
         if step == 1:
             outs.append(jax.ShapeDtypeStruct((8, devs * TRIALS), i32))
         results = pl.pallas_call(

time: 99 us -> 96.8 us (0.978)
  blocking collectives: 70.4 us -> 68.5 us
    all_to_all x4, blocking collectives: 70.4 us -> 68.5 us  [exchange(): return lax.all_to_all(out, ('area', 'local'), 0, 0, tiled=True)]
where the time goes in v4:
time: 96.8 us; the launch traced here: 96.6 us
  blocking collectives  68.5 us (71%)
  Pallas kernels  11.8 us (12%)
  starting transfers between devices  8.28 us (9%)
  waiting for transfers between devices  6.28 us (6%)
    all_to_all x4, blocking collectives, exchange(): return lax.all_to_all(out, ('area', 'local'), 0, 0, tiled=True)  68.5 us
    pallas_call x4, Pallas kernels, shards(): pl.pallas_call(functools.partial(step_kernel, step), out_shape=tuple(outs...  7.18 us
    ppermute x3, starting transfers between devices, shards(): lax.ppermute(rates, 'local', [(i, (i + shift) % n_local) for i in range(n...  4.34 us
    all_to_all x1, starting transfers between devices, exchange(): return lax.all_to_all(out, ('area', 'local'), 0, 0, tiled=True)  3.94 us
    pallas_call x1, Pallas kernels, shards(): pl.pallas_call(first_kernel, out_shape=(jax.ShapeDtypeStruct((devs * long...  3.61 us
    all_to_all x1, waiting for transfers between devices, exchange(): return lax.all_to_all(out, ('area', 'local'), 0, 0, tiled=True)  3.47 us
    ppermute x3, waiting for transfers between devices, shards(): lax.ppermute(rates, 'local', [(i, (i + shift) % n_local) for i in range(n...  2.81 us
  transfers between devices with their start and end apart: 4, of which 3 were waited for; matrix products, arithmetic and copies ran while one was open for 1% of the time, Pallas kernels for 0%

profile of v4, /device:TPU:1, one launch (start us, length us, event | category | flops | bytes accessed | tf_op | source)
XLA Modules:
  0.0 96.6 jit_solution(7838809120565931213)
XLA Ops:
  0.6 0.0 copy-start.2
  0.6 0.0 copy-start.6
  0.7 0.0 copy-start.8
  0.7 0.0 copy-start.7
  0.7 0.0 copy-start
  0.7 0.0 copy-start.1
  0.7 0.0 copy-start.4
  0.7 0.0 copy-start.3
  0.7 0.0 copy-start.5
  0.7 3.6 %first.1 = (bf16[1280,128]{1,0:T(8,128)(2,1)S(1)}, f32[8,4096]{1,0:T(8,128)S(1)}, f32[64,128]{1,0:T(8,128)S(1)}) custom-call(s32[5,1,128]{2,1,0:T(1,128)} %bitcast.42, s32[2,128]{1,0:T(2,128)} %bitcast.47, s32[2,128]{1,0:T(2,128)} %bitcast.57, s32[5,1,128]{2,1,0:T(1,128)} %counts_hbm.1, f32[8,4096]{1,0:T(8,128)} %refs_4_.1, s32[1,32]{1,0:T(1,128)} %bitcast.52, ...), custom_call_target="tpu_custom_call" | custom-call | tf_op jit(solution)/shard_map/first/pallas_call | solution.py:315
  4.3 23.3 %all_to_all.25 = bf16[128,5,2,128]{3,2,1,0:T(2,128)(2,1)S(1)} all-to-all(bf16[128,5,2,128]{3,2,1,0:T(2,128)(2,1)S(1)} %bitcast.41), channel_id=1, replica_groups=mesh['area'=32,'local'=4] {'area','local'}, dimensions={0} | all-to-all | bytes 655360 | tf_op jit(solution)/shard_map/all_to_all | solution.py:309
  27.6 0.0 copy-done.2
  27.6 0.0 copy-done.6
  27.6 0.0 copy-done.8
  27.6 0.0 copy-done.7
  27.6 0.0 copy-done
  27.6 0.0 copy-done.1
  27.7 0.0 copy-done.4
  27.7 0.0 copy-done.3
  27.7 0.0 copy-done.5
  27.7 1.7 %step1.1 = (f32[8,4096]{1,0:T(8,128)S(1)}, f32[8,4096]{1,0:T(8,128)S(1)}, f32[8,4096]{1,0:T(8,128)S(1)}, bf16[128,8,128]{2,1,0:T(8,128)(2,1)S(1)}, f32[64,128]{1,0:T(8,128)S(1)}, /*index=5*/s32[8,1024]{1,0:T(8,128)S(1)}) custom-call(s32[5,1,128]{2,1,0:T(1,128)S(1)} %bitcast.43, s32[2,128]{1,0:T(2,128)S(1)} %bitcast.48, bf16[1280,128]{1,0:T(8,128)(2,1)S(1)} %bitcast.30, ...), custom_call_target="tpu_custom_call" | custom-call | tf_op jit(solution)/shard_map/step1/pallas_call | solution.py:349
  29.4 15.1 %all_to_all.26.refs_2_ = bf16[128,8,128]{2,1,0:T(8,128)(2,1)S(1)} all-to-all(bf16[128,8,128]{2,1,0:T(8,128)(2,1)S(1)} %get-tuple-element.39), channel_id=1, replica_groups=mesh['area'=32,'local'=4] {'area','local'}, dimensions={0} | all-to-all | bytes 524288 | tf_op jit(solution)/shard_map/all_to_all | solution.py:309
  44.5 1.6 %step2.1 = (f32[8,4096]{1,0:T(8,128)S(1)}, f32[8,4096]{1,0:T(8,128)S(1)}, f32[8,4096]{1,0:T(8,128)S(1)}, bf16[128,8,128]{2,1,0:T(8,128)(2,1)S(1)}, f32[64,128]{1,0:T(8,128)S(1)}) custom-call(s32[5,1,128]{2,1,0:T(1,128)S(1)} %bitcast.44, s32[2,128]{1,0:T(2,128)S(1)} %bitcast.49, bf16[128,8,128]{2,1,0:T(8,128)(2,1)S(1)} %all_to_all.26.refs_2_, ...), custom_call_target="tpu_custom_call" | custom-call | tf_op jit(solution)/shard_map/step2/pallas_call | solution.py:349
  46.1 15.1 %all_to_all.27.refs_2_ = bf16[128,8,128]{2,1,0:T(8,128)(2,1)S(1)} all-to-all(bf16[128,8,128]{2,1,0:T(8,128)(2,1)S(1)} %get-tuple-element.45), channel_id=1, replica_groups=mesh['area'=32,'local'=4] {'area','local'}, dimensions={0} | all-to-all | bytes 524288 | tf_op jit(solution)/shard_map/all_to_all | solution.py:309
  61.2 1.6 %step3.1 = (f32[8,4096]{1,0:T(8,128)S(1)}, f32[8,4096]{1,0:T(8,128)S(1)}, f32[8,4096]{1,0:T(8,128)S(1)}, bf16[128,8,128]{2,1,0:T(8,128)(2,1)S(1)}, f32[64,128]{1,0:T(8,128)S(1)}) custom-call(s32[5,1,128]{2,1,0:T(1,128)S(1)} %bitcast.45, s32[2,128]{1,0:T(2,128)S(1)} %bitcast.50, bf16[128,8,128]{2,1,0:T(8,128)(2,1)S(1)} %all_to_all.27.refs_2_, ...), custom_call_target="tpu_custom_call" | custom-call | tf_op jit(solution)/shard_map/step3/pallas_call | solution.py:349
  62.8 15.1 %all_to_all.28.refs_2_ = bf16[128,8,128]{2,1,0:T(8,128)(2,1)S(1)} all-to-all(bf16[128,8,128]{2,1,0:T(8,128)(2,1)S(1)} %get-tuple-element.50), channel_id=1, replica_groups=mesh['area'=32,'local'=4] {'area','local'}, dimensions={0} | all-to-all | bytes 524288 | tf_op jit(solution)/shard_map/all_to_all | solution.py:309
  77.8 2.3 %step4.1 = (f32[8,4096]{1,0:T(8,128)S(1)}, f32[8,4096]{1,0:T(8,128)S(1)}, f32[8,4096]{1,0:T(8,128)S(1)}, bf16[128,8,128]{2,1,0:T(8,128)(2,1)}, f32[64,128]{1,0:T(8,128)S(1)}) custom-call(s32[5,1,128]{2,1,0:T(1,128)S(1)} %bitcast.46, s32[2,128]{1,0:T(2,128)S(1)} %bitcast.51, bf16[128,8,128]{2,1,0:T(8,128)(2,1)S(1)} %all_to_all.28.refs_2_, ...), custom_call_target="tpu_custom_call" | custom-call | tf_op jit(solution)/shard_map/step4/pallas_call | solution.py:349
  80.1 3.9 %all-to-all-start.4 = ((bf16[128,8,128]{2,1,0:T(8,128)(2,1)}), bf16[128,8,128]{2,1,0:T(8,128)(2,1)S(1)}, u32[]{:S(2)}, u32[]{:S(2)}) async-start(bf16[128,8,128]{2,1,0:T(8,128)(2,1)} %get-tuple-element.56), calls=%async_computation.4 | async-start | bytes 524288 | tf_op jit(solution)/shard_map/all_to_all | solution.py:309
  84.1 0.1 reduce_sum.9
  84.2 0.1 reshape.37
  84.3 2.6 %collective-permute-start.2 = (f32[5,8,8]{2,1,0:T(8,128)S(1)}, f32[5,8,8]{2,1,0:T(8,128)S(1)}, u32[]{:S(2)}, u32[]{:S(2)}) collective-permute-start(f32[5,8,8]{2,1,0:T(8,128)S(1)} %reshape.37), channel_id=1, source_target_pairs={{0,3},{1,0},{2,1},{3,2},{4,7},{5,4},{6,5},{7,6},{8,11},{9,8},{10,9... | collective-permute-start | bytes 3848 | tf_op jit(solution)/shard_map/ppermute | solution.py:368
  86.9 0.0 collective-permute-start.1
  86.9 1.8 %collective-permute-start = (f32[5,8,8]{2,1,0:T(8,128)S(1)}, f32[5,8,8]{2,1,0:T(8,128)S(1)}, u32[]{:S(2)}, u32[]{:S(2)}) collective-permute-start(f32[5,8,8]{2,1,0:T(8,128)S(1)} %reshape.37), channel_id=1, source_target_pairs={{0,2},{1,3},{2,0},{3,1},{4,6},{5,7},{6,4},{7,5},{8,10},{9,11},{10,... | collective-permute-start | bytes 3848 | tf_op jit(solution)/shard_map/ppermute | solution.py:368
  88.7 0.0 collective-permute-done.2
  88.7 2.4 %collective-permute-done.1 = f32[5,8,8]{2,1,0:T(8,128)S(1)} collective-permute-done((f32[5,8,8]{2,1,0:T(8,128)S(1)}, f32[5,8,8]{2,1,0:T(8,128)S(1)}, u32[]{:S(2)}, u32[]{:S(2)}) %collective-permute-start.1) | collective-permute-done | bytes 1312 | tf_op jit(solution)/shard_map/ppermute | solution.py:368
  91.0 0.4 collective-permute-done
  91.5 0.6 multiply_bitcast_fusion
  92.1 3.5 %all-to-all-done.4.arrived_ref = bf16[128,8,128]{2,1,0:T(8,128)(2,1)S(1)} async-done(((bf16[128,8,128]{2,1,0:T(8,128)(2,1)}), bf16[128,8,128]{2,1,0:T(8,128)(2,1)S(1)}, u32[]{:S(2)}, u32[]{:S(2)}) %all-to-all-start.4) | async-done | bytes 262176 | tf_op jit(solution)/shard_map/all_to_all | solution.py:309
  95.6 1.0 %last.1 = (f32[8,4096]{1,0:T(8,128)}, f32[8,4096]{1,0:T(8,128)}) custom-call(bf16[128,8,128]{2,1,0:T(8,128)(2,1)S(1)} %all-to-all-done.4.arrived_ref, s32[8,1024]{1,0:T(8,128)S(1)} %get-tuple-element.40.refs_3_.codes_ref, f32[8,4096]{1,0:T(8,128)S(1)} %get-tuple-element.57.volts_ref, f32[8,4096]{1,0:T(8,128)S(1)} %get-tuple-element.58.cur_ref, ...), custom_call_target="tpu_custom_call" | custom-call | tf_op jit(solution)/shard_map/last/pallas_call | solution.py:373
  (6 shorter events, 0.0 us)
Async XLA Ops:
  0.6 27.0 %copy-start.2 = (f32[8,4096]{1,0:T(8,128)S(1)}, f32[8,4096]{1,0:T(8,128)}, u32[]{:S(2)}) copy-start(f32[8,4096]{1,0:T(8,128)} %refs_4_.1) | copy-start | bytes 393220
  0.6 27.0 %copy-start.6 = (s32[5,1,128,1]{2,3,1,0:T(1,128)S(1)}, s32[5,1,128,1]{2,3,1,0:T(1,128)}, u32[]{:S(2)}) copy-start(s32[5,1,128,1]{2,3,1,0:T(1,128)} %param.20) | copy-start | bytes 7684
  0.7 27.0 %copy-start.8 = (s32[32]{0:T(128)S(1)}, s32[32]{0:T(128)}, u32[]{:S(2)}) copy-start(s32[32]{0:T(128)} %param.19) | copy-start | bytes 388
  0.7 27.0 %copy-start.7 = (s32[1,128,2]{1,2,0:T(2,128)S(1)}, s32[1,128,2]{1,2,0:T(2,128)}, u32[]{:S(2)}) copy-start(s32[1,128,2]{1,2,0:T(2,128)} %param.17) | copy-start | bytes 3076
  0.7 27.0 %copy-start = (bf16[1,128,2,128,128]{4,3,2,1,0:T(8,128)(2,1)S(1)}, bf16[1,128,2,128,128]{4,3,2,1,0:T(8,128)(2,1)}, u32[]{:S(2)}) copy-start(bf16[1,128,2,128,128]{4,3,2,1,0:T(8,128)(2,1)} %param.16) | copy-start | bytes 25165828
  0.7 27.0 %copy-start.1 = (f32[8,4096]{1,0:T(8,128)S(1)}, f32[8,4096]{1,0:T(8,128)}, u32[]{:S(2)}) copy-start(f32[8,4096]{1,0:T(8,128)} %ext_ref.1) | copy-start | bytes 393220
  0.7 27.0 %copy-start.4 = (f32[4096]{0:T(1024)S(1)}, f32[4096]{0:T(1024)}, u32[]{:S(2)}) copy-start(f32[4096]{0:T(1024)} %param.15) | copy-start | bytes 49156
  0.7 27.0 %copy-start.3 = (f32[4096]{0:T(1024)S(1)}, f32[4096]{0:T(1024)}, u32[]{:S(2)}) copy-start(f32[4096]{0:T(1024)} %param.14) | copy-start | bytes 49156
  0.7 27.0 %copy-start.5 = (f32[8,4096]{1,0:T(8,128)S(1)}, f32[8,4096]{1,0:T(8,128)}, u32[]{:S(2)}) copy-start(f32[8,4096]{1,0:T(8,128)} %refs_5_.1) | copy-start | bytes 393220
  80.1 15.4 %all-to-all-start.4 = ((bf16[128,8,128]{2,1,0:T(8,128)(2,1)}), bf16[128,8,128]{2,1,0:T(8,128)(2,1)S(1)}, u32[]{:S(2)}, u32[]{:S(2)}) async-start(bf16[128,8,128]{2,1,0:T(8,128)(2,1)} %get-tuple-element.56), calls=%async_computation.4 | async-start | bytes 524288 | tf_op jit(solution)/shard_map/all_to_all | solution.py:309
  84.3 4.3 %collective-permute-start.2 = (f32[5,8,8]{2,1,0:T(8,128)S(1)}, f32[5,8,8]{2,1,0:T(8,128)S(1)}, u32[]{:S(2)}, u32[]{:S(2)}) collective-permute-start(f32[5,8,8]{2,1,0:T(8,128)S(1)} %reshape.37), channel_id=1, source_target_pairs={{0,3},{1,0},{2,1},{3,2},{4,7},{5,4},{6,5},{7,6},{8,11},{9,8},{10,9... | collective-permute-start | bytes 3848 | tf_op jit(solution)/shard_map/ppermute | solution.py:368
  86.9 4.1 %collective-permute-start.1 = (f32[5,8,8]{2,1,0:T(8,128)S(1)}, f32[5,8,8]{2,1,0:T(8,128)S(1)}, u32[]{:S(2)}, u32[]{:S(2)}) collective-permute-start(f32[5,8,8]{2,1,0:T(8,128)S(1)} %reshape.37), channel_id=1, source_target_pairs={{0,1},{1,2},{2,3},{3,0},{4,5},{5,6},{6,7},{7,4},{8,9},{9,10},{10,1... | collective-permute-start | bytes 3848 | tf_op jit(solution)/shard_map/ppermute | solution.py:368
  86.9 4.6 %collective-permute-start = (f32[5,8,8]{2,1,0:T(8,128)S(1)}, f32[5,8,8]{2,1,0:T(8,128)S(1)}, u32[]{:S(2)}, u32[]{:S(2)}) collective-permute-start(f32[5,8,8]{2,1,0:T(8,128)S(1)} %reshape.37), channel_id=1, source_target_pairs={{0,2},{1,3},{2,0},{3,1},{4,6},{5,7},{6,4},{7,5},{8,10},{9,11},{10,... | collective-permute-start | bytes 3848 | tf_op jit(solution)/shard_map/ppermute | solution.py:368

commit v5 on v4

--- a/solution.py
+++ b/solution.py
@@ -20,6 +20,7 @@
 reset_size = 0.5
 
 VMEM = pl.BlockSpec(memory_space=pltpu.VMEM)
+ANY = pl.BlockSpec(memory_space=pl.ANY)
 HBM = pl.BlockSpec(memory_space=pltpu.HBM)
 
 
@@ -163,6 +164,10 @@
         send_tiles(
             at, at + CHUNK, lambda d, k: base + d, route_s, src_s, blocks_ref, tiles_ref, store
         )
+
+
+def gate_kernel(message_ref, out_ref):
+    pass
 
 
 def iotas(shape):
@@ -335,6 +340,17 @@
         compiler_params=params(16),
         name="first",
     )(*[in_hbm(a) for a in (route, src, dst, used, potential, pops, table)])
+    for i in range(2):
+        out = pl.pallas_call(
+            gate_kernel,
+            out_shape=jax.ShapeDtypeStruct(out.shape, out.dtype),
+            in_specs=[ANY],
+            out_specs=ANY,
+            input_output_aliases={0: 0},
+            cost_estimate=pl.CostEstimate(flops=6_000_000_000, bytes_accessed=0, transcendentals=0),
+            compiler_params=params(1),
+            name=f"gate{i}",
+        )(out)
     arrived = exchange(out.reshape(devs, long // 2, 2, BLOCK)).reshape(devs * long, BLOCK)
     local_table = table
     volts, cur = potential, current

time: 96.8 us -> 96.5 us (level)
  no operation moved by 1% of the time
where the time goes in v5:
time: 96.5 us; the launch traced here: 96.2 us
  blocking collectives  68.5 us (71%)
  Pallas kernels  11.4 us (12%)
  starting transfers between devices  8.28 us (9%)
  waiting for transfers between devices  6.27 us (6%)
    all_to_all x4, blocking collectives, exchange(): return lax.all_to_all(out, ('area', 'local'), 0, 0, tiled=True)  68.5 us
    pallas_call x4, Pallas kernels, shards(): pl.pallas_call(functools.partial(step_kernel, step), out_shape=tuple(outs...  7.19 us
    ppermute x3, starting transfers between devices, shards(): lax.ppermute(rates, 'local', [(i, (i + shift) % n_local) for i in range(n...  4.34 us
    all_to_all x1, starting transfers between devices, exchange(): return lax.all_to_all(out, ('area', 'local'), 0, 0, tiled=True)  3.95 us
    all_to_all x1, waiting for transfers between devices, exchange(): return lax.all_to_all(out, ('area', 'local'), 0, 0, tiled=True)  3.46 us
    pallas_call x1, Pallas kernels, shards(): pl.pallas_call(first_kernel, out_shape=(jax.ShapeDtypeStruct((devs * long...  3.16 us
    ppermute x3, waiting for transfers between devices, shards(): lax.ppermute(rates, 'local', [(i, (i + shift) % n_local) for i in range(n...  2.81 us
  transfers between devices with their start and end apart: 4, of which 3 were waited for; matrix products, arithmetic and copies ran while one was open for 1% of the time, Pallas kernels for 0%

profile of v5, /device:TPU:1, one launch (start us, length us, event | category | flops | bytes accessed | tf_op | source)
XLA Modules:
  0.0 96.2 jit_solution(12155766067655742726)
XLA Ops:
  0.6 3.2 %first.1 = (bf16[1280,128]{1,0:T(8,128)(2,1)S(1)}, f32[8,4096]{1,0:T(8,128)S(1)}, f32[64,128]{1,0:T(8,128)S(1)}) custom-call(s32[5,1,128]{2,1,0:T(1,128)} %bitcast.44, s32[2,128]{1,0:T(2,128)} %bitcast.49, s32[2,128]{1,0:T(2,128)} %bitcast.59, s32[5,1,128]{2,1,0:T(1,128)} %counts_hbm.1, f32[8,4096]{1,0:T(8,128)} %refs_4_.1, s32[1,32]{1,0:T(1,128)} %bitcast.54, ...), custom_call_target="tpu_custom_call" | custom-call | tf_op jit(solution)/shard_map/first/pallas_call | solution.py:320
  3.8 0.0 slice-start
  3.8 0.0 slice-start.1
  3.8 0.0 copy-start
  3.9 0.0 copy-start.1
  3.9 0.0 copy-start.2
  3.9 0.0 copy-start.3
  3.9 0.0 copy-start.4
  3.9 0.0 copy-start.5
  3.9 0.0 copy-start.6
  3.9 0.0 copy-start.7
  3.9 23.3 %all_to_all.25 = bf16[128,5,2,128]{3,2,1,0:T(2,128)(2,1)S(1)} all-to-all(bf16[128,5,2,128]{3,2,1,0:T(2,128)(2,1)S(1)} %bitcast.43), channel_id=1, replica_groups=mesh['area'=32,'local'=4] {'area','local'}, dimensions={0} | all-to-all | bytes 655360 | tf_op jit(solution)/shard_map/all_to_all | solution.py:314
  27.2 0.0 slice-done
  27.2 0.0 slice-done.1
  27.2 0.0 copy-done
  27.2 0.0 copy-done.1
  27.2 0.0 copy-done.2
  27.3 0.0 copy-done.3
  27.3 0.0 copy-done.4
  27.3 0.0 copy-done.5
  27.3 0.0 copy-done.6
  27.3 0.0 copy-done.7
  27.3 1.7 %step1.1 = (f32[8,4096]{1,0:T(8,128)S(1)}, f32[8,4096]{1,0:T(8,128)S(1)}, f32[8,4096]{1,0:T(8,128)S(1)}, bf16[128,8,128]{2,1,0:T(8,128)(2,1)S(1)}, f32[64,128]{1,0:T(8,128)S(1)}, /*index=5*/s32[8,1024]{1,0:T(8,128)S(1)}) custom-call(s32[5,1,128]{2,1,0:T(1,128)S(1)} %bitcast.45, s32[2,128]{1,0:T(2,128)S(1)} %bitcast.50, bf16[1280,128]{1,0:T(8,128)(2,1)S(1)} %bitcast.32, ...), custom_call_target="tpu_custom_call" | custom-call | tf_op jit(solution)/shard_map/step1/pallas_call | solution.py:365
  29.1 15.1 %all_to_all.26.refs_2_ = bf16[128,8,128]{2,1,0:T(8,128)(2,1)S(1)} all-to-all(bf16[128,8,128]{2,1,0:T(8,128)(2,1)S(1)} %get-tuple-element.39), channel_id=1, replica_groups=mesh['area'=32,'local'=4] {'area','local'}, dimensions={0} | all-to-all | bytes 524288 | tf_op jit(solution)/shard_map/all_to_all | solution.py:314
  44.1 1.6 %step2.1 = (f32[8,4096]{1,0:T(8,128)S(1)}, f32[8,4096]{1,0:T(8,128)S(1)}, f32[8,4096]{1,0:T(8,128)S(1)}, bf16[128,8,128]{2,1,0:T(8,128)(2,1)S(1)}, f32[64,128]{1,0:T(8,128)S(1)}) custom-call(s32[5,1,128]{2,1,0:T(1,128)S(1)} %bitcast.46, s32[2,128]{1,0:T(2,128)S(1)} %bitcast.51, bf16[128,8,128]{2,1,0:T(8,128)(2,1)S(1)} %all_to_all.26.refs_2_, ...), custom_call_target="tpu_custom_call" | custom-call | tf_op jit(solution)/shard_map/step2/pallas_call | solution.py:365
  45.7 15.1 %all_to_all.27.refs_2_ = bf16[128,8,128]{2,1,0:T(8,128)(2,1)S(1)} all-to-all(bf16[128,8,128]{2,1,0:T(8,128)(2,1)S(1)} %get-tuple-element.45), channel_id=1, replica_groups=mesh['area'=32,'local'=4] {'area','local'}, dimensions={0} | all-to-all | bytes 524288 | tf_op jit(solution)/shard_map/all_to_all | solution.py:314
  60.8 1.6 %step3.1 = (f32[8,4096]{1,0:T(8,128)S(1)}, f32[8,4096]{1,0:T(8,128)S(1)}, f32[8,4096]{1,0:T(8,128)S(1)}, bf16[128,8,128]{2,1,0:T(8,128)(2,1)S(1)}, f32[64,128]{1,0:T(8,128)S(1)}) custom-call(s32[5,1,128]{2,1,0:T(1,128)S(1)} %bitcast.47, s32[2,128]{1,0:T(2,128)S(1)} %bitcast.52, bf16[128,8,128]{2,1,0:T(8,128)(2,1)S(1)} %all_to_all.27.refs_2_, ...), custom_call_target="tpu_custom_call" | custom-call | tf_op jit(solution)/shard_map/step3/pallas_call | solution.py:365
  62.4 15.1 %all_to_all.28.refs_2_ = bf16[128,8,128]{2,1,0:T(8,128)(2,1)S(1)} all-to-all(bf16[128,8,128]{2,1,0:T(8,128)(2,1)S(1)} %get-tuple-element.50), channel_id=1, replica_groups=mesh['area'=32,'local'=4] {'area','local'}, dimensions={0} | all-to-all | bytes 524288 | tf_op jit(solution)/shard_map/all_to_all | solution.py:314
  77.5 2.3 %step4.1 = (f32[8,4096]{1,0:T(8,128)S(1)}, f32[8,4096]{1,0:T(8,128)S(1)}, f32[8,4096]{1,0:T(8,128)S(1)}, bf16[128,8,128]{2,1,0:T(8,128)(2,1)}, f32[64,128]{1,0:T(8,128)S(1)}) custom-call(s32[5,1,128]{2,1,0:T(1,128)S(1)} %bitcast.48, s32[2,128]{1,0:T(2,128)S(1)} %bitcast.53, bf16[128,8,128]{2,1,0:T(8,128)(2,1)S(1)} %all_to_all.28.refs_2_, ...), custom_call_target="tpu_custom_call" | custom-call | tf_op jit(solution)/shard_map/step4/pallas_call | solution.py:365
  79.8 3.9 %all-to-all-start.4 = ((bf16[128,8,128]{2,1,0:T(8,128)(2,1)}), bf16[128,8,128]{2,1,0:T(8,128)(2,1)S(1)}, u32[]{:S(2)}, u32[]{:S(2)}) async-start(bf16[128,8,128]{2,1,0:T(8,128)(2,1)} %get-tuple-element.56), calls=%async_computation.4 | async-start | bytes 524288 | tf_op jit(solution)/shard_map/all_to_all | solution.py:314
  83.8 0.1 reduce_sum.9
  83.9 0.1 reshape.37
  84.0 2.6 %collective-permute-start.2 = (f32[5,8,8]{2,1,0:T(8,128)S(1)}, f32[5,8,8]{2,1,0:T(8,128)S(1)}, u32[]{:S(2)}, u32[]{:S(2)}) collective-permute-start(f32[5,8,8]{2,1,0:T(8,128)S(1)} %reshape.37), channel_id=1, source_target_pairs={{0,3},{1,0},{2,1},{3,2},{4,7},{5,4},{6,5},{7,6},{8,11},{9,8},{10,9... | collective-permute-start | bytes 3848 | tf_op jit(solution)/shard_map/ppermute | solution.py:384
  86.6 0.0 collective-permute-start.1
  86.6 1.8 %collective-permute-start = (f32[5,8,8]{2,1,0:T(8,128)S(1)}, f32[5,8,8]{2,1,0:T(8,128)S(1)}, u32[]{:S(2)}, u32[]{:S(2)}) collective-permute-start(f32[5,8,8]{2,1,0:T(8,128)S(1)} %reshape.37), channel_id=1, source_target_pairs={{0,2},{1,3},{2,0},{3,1},{4,6},{5,7},{6,4},{7,5},{8,10},{9,11},{10,... | collective-permute-start | bytes 3848 | tf_op jit(solution)/shard_map/ppermute | solution.py:384
  88.3 0.0 collective-permute-done.2
  88.3 2.4 %collective-permute-done.1 = f32[5,8,8]{2,1,0:T(8,128)S(1)} collective-permute-done((f32[5,8,8]{2,1,0:T(8,128)S(1)}, f32[5,8,8]{2,1,0:T(8,128)S(1)}, u32[]{:S(2)}, u32[]{:S(2)}) %collective-permute-start.1) | collective-permute-done | bytes 1312 | tf_op jit(solution)/shard_map/ppermute | solution.py:384
  90.7 0.4 collective-permute-done
  91.1 0.6 multiply_bitcast_fusion
  91.7 3.5 %all-to-all-done.4.arrived_ref = bf16[128,8,128]{2,1,0:T(8,128)(2,1)S(1)} async-done(((bf16[128,8,128]{2,1,0:T(8,128)(2,1)}), bf16[128,8,128]{2,1,0:T(8,128)(2,1)S(1)}, u32[]{:S(2)}, u32[]{:S(2)}) %all-to-all-start.4) | async-done | bytes 262176 | tf_op jit(solution)/shard_map/all_to_all | solution.py:314
  95.2 1.0 %last.1 = (f32[8,4096]{1,0:T(8,128)}, f32[8,4096]{1,0:T(8,128)}) custom-call(bf16[128,8,128]{2,1,0:T(8,128)(2,1)S(1)} %all-to-all-done.4.arrived_ref, s32[8,1024]{1,0:T(8,128)S(1)} %get-tuple-element.40.refs_3_.codes_ref, f32[8,4096]{1,0:T(8,128)S(1)} %get-tuple-element.57.volts_ref, f32[8,4096]{1,0:T(8,128)S(1)} %get-tuple-element.58.cur_ref, ...), custom_call_target="tpu_custom_call" | custom-call | tf_op jit(solution)/shard_map/last/pallas_call | solution.py:389
  (9 shorter events, 0.0 us)
Async XLA Ops:
  3.8 23.4 %slice-start = ((s8[8388608]{0:T(1024)(128)(4,1)}), s8[4194304]{0:T(1024)(128)(4,1)S(1)}, s32[]{:S(2)}) async-start(s8[8388608]{0:T(1024)(128)(4,1)} %bitcast.26), calls=%async_computation.5 | async-start | bytes 8388608
  3.8 23.4 %slice-start.1 = ((s8[8388608]{0:T(1024)(128)(4,1)}), s8[4194304]{0:T(1024)(128)(4,1)S(1)}, s32[]{:S(2)}) async-start(s8[8388608]{0:T(1024)(128)(4,1)} %bitcast.26), calls=%async_computation.6 | async-start | bytes 8388608
  3.8 23.4 %copy-start = (f32[8,4096]{1,0:T(8,128)S(1)}, f32[8,4096]{1,0:T(8,128)}, u32[]{:S(2)}) copy-start(f32[8,4096]{1,0:T(8,128)} %ext_ref.1) | copy-start | bytes 393220
  3.9 23.4 %copy-start.1 = (f32[8,4096]{1,0:T(8,128)S(1)}, f32[8,4096]{1,0:T(8,128)}, u32[]{:S(2)}) copy-start(f32[8,4096]{1,0:T(8,128)} %refs_4_.1) | copy-start | bytes 393220
  3.9 23.4 %copy-start.2 = (f32[4096]{0:T(1024)S(1)}, f32[4096]{0:T(1024)}, u32[]{:S(2)}) copy-start(f32[4096]{0:T(1024)} %param.14) | copy-start | bytes 49156
  3.9 23.4 %copy-start.3 = (f32[4096]{0:T(1024)S(1)}, f32[4096]{0:T(1024)}, u32[]{:S(2)}) copy-start(f32[4096]{0:T(1024)} %param.15) | copy-start | bytes 49156
  3.9 23.4 %copy-start.4 = (f32[8,4096]{1,0:T(8,128)S(1)}, f32[8,4096]{1,0:T(8,128)}, u32[]{:S(2)}) copy-start(f32[8,4096]{1,0:T(8,128)} %refs_5_.1) | copy-start | bytes 393220
  3.9 23.4 %copy-start.5 = (s32[5,1,128,1]{2,3,1,0:T(1,128)S(1)}, s32[5,1,128,1]{2,3,1,0:T(1,128)}, u32[]{:S(2)}) copy-start(s32[5,1,128,1]{2,3,1,0:T(1,128)} %param.20) | copy-start | bytes 7684
  3.9 23.4 %copy-start.6 = (s32[1,128,2]{1,2,0:T(2,128)S(1)}, s32[1,128,2]{1,2,0:T(2,128)}, u32[]{:S(2)}) copy-start(s32[1,128,2]{1,2,0:T(2,128)} %param.17) | copy-start | bytes 3076
  3.9 23.4 %copy-start.7 = (s32[32]{0:T(128)S(1)}, s32[32]{0:T(128)}, u32[]{:S(2)}) copy-start(s32[32]{0:T(128)} %param.19) | copy-start | bytes 388
  79.8 15.4 %all-to-all-start.4 = ((bf16[128,8,128]{2,1,0:T(8,128)(2,1)}), bf16[128,8,128]{2,1,0:T(8,128)(2,1)S(1)}, u32[]{:S(2)}, u32[]{:S(2)}) async-start(bf16[128,8,128]{2,1,0:T(8,128)(2,1)} %get-tuple-element.56), calls=%async_computation.4 | async-start | bytes 524288 | tf_op jit(solution)/shard_map/all_to_all | solution.py:314
  84.0 4.3 %collective-permute-start.2 = (f32[5,8,8]{2,1,0:T(8,128)S(1)}, f32[5,8,8]{2,1,0:T(8,128)S(1)}, u32[]{:S(2)}, u32[]{:S(2)}) collective-permute-start(f32[5,8,8]{2,1,0:T(8,128)S(1)} %reshape.37), channel_id=1, source_target_pairs={{0,3},{1,0},{2,1},{3,2},{4,7},{5,4},{6,5},{7,6},{8,11},{9,8},{10,9... | collective-permute-start | bytes 3848 | tf_op jit(solution)/shard_map/ppermute | solution.py:384
  86.6 4.1 %collective-permute-start.1 = (f32[5,8,8]{2,1,0:T(8,128)S(1)}, f32[5,8,8]{2,1,0:T(8,128)S(1)}, u32[]{:S(2)}, u32[]{:S(2)}) collective-permute-start(f32[5,8,8]{2,1,0:T(8,128)S(1)} %reshape.37), channel_id=1, source_target_pairs={{0,1},{1,2},{2,3},{3,0},{4,5},{5,6},{6,7},{7,4},{8,9},{9,10},{10,1... | collective-permute-start | bytes 3848 | tf_op jit(solution)/shard_map/ppermute | solution.py:384
  86.6 4.6 %collective-permute-start = (f32[5,8,8]{2,1,0:T(8,128)S(1)}, f32[5,8,8]{2,1,0:T(8,128)S(1)}, u32[]{:S(2)}, u32[]{:S(2)}) collective-permute-start(f32[5,8,8]{2,1,0:T(8,128)S(1)} %reshape.37), channel_id=1, source_target_pairs={{0,2},{1,3},{2,0},{3,1},{4,6},{5,7},{6,4},{7,5},{8,10},{9,11},{10,... | collective-permute-start | bytes 3848 | tf_op jit(solution)/shard_map/ppermute | solution.py:384

commit v6 on v5

--- a/solution.py
+++ b/solution.py
@@ -12,7 +12,8 @@
 TRIALS = 8
 NO_BLOCK = 64
 EXTRA = 2
-CHUNK = 16
+PIECES = 4
+CHUNK = 32
 WHOLE = 32
 
 spike_gain = 4.0
@@ -36,11 +37,11 @@
     return jax.nn.sigmoid(spike_gain * (volts - threshold))
 
 
-def send_tiles(first, last, tile_of, route_ref, src_ref, blocks_ref, tiles_ref, store):
+def send_tiles(first, last, pick, blocks_ref, tiles_ref, store):
     for d in range(first, last, 2):
-        k, l = route_ref[0, 0, d], route_ref[0, 0, d + 1]
-        spikes = jnp.concatenate([blocks_ref[src_ref[k, d]], blocks_ref[src_ref[l, d + 1]]], axis=0)
-        tiles = jnp.concatenate([tiles_ref[tile_of(d, k)], tiles_ref[tile_of(d + 1, l)]], axis=1)
+        (block, tile), (block_b, tile_b) = pick(d), pick(d + 1)
+        spikes = jnp.concatenate([blocks_ref[block], blocks_ref[block_b]], axis=0)
+        tiles = jnp.concatenate([tiles_ref[tile], tiles_ref[tile_b]], axis=1)
         current = jnp.dot(spikes, tiles, preferred_element_type=jnp.float32).astype(jnp.bfloat16)
         store(d, current[:TRIALS, :BLOCK])
         store(d + 1, current[TRIALS:, BLOCK:])
@@ -73,8 +74,8 @@
 
 def first_kernel(
     route_hbm, src_hbm, dst_hbm, counts_hbm, volts_hbm, pops_hbm, table_hbm,
-    out_ref, spikes_ref, act_ref,
-    route_s, src_s, routes_ref, dst_ref, counts_ref, volts_ref, pops_ref, tiles_ref,
+    out_ref, spikes_ref, act_ref, chosen_ref,
+    route_s, src_s, routes_ref, from_ref, dst_ref, counts_ref, volts_ref, pops_ref, tiles_ref,
     blocks_ref, rows_ref, sems, whole_sems, routed_sems,
 ):
     tpt, devs = dst_ref.shape
@@ -89,6 +90,7 @@
                 (route_hbm, routes_ref),
                 (dst_hbm, dst_ref),
                 (counts_hbm, counts_ref),
+                (src_hbm, from_ref),
                 (pops_hbm, pops_ref),
             )
         )
@@ -118,7 +120,7 @@
         return carry
 
     lax.fori_loop(0, (devs - WHOLE) // CHUNK, start_routed, 0)
-    for copy in copies[3:6]:
+    for copy in copies[3:7]:
         copy.wait()
 
     step = lax.broadcasted_iota(jnp.int32, (BLOCK, devs), 0)
@@ -127,6 +129,9 @@
         target = jnp.where(routes_ref[t] == 0, dst_ref[0:1, :], dst_ref[1:2, :])
         target = jnp.where(counts_ref[t] > 0, target, NO_BLOCK)
         targets = jnp.where(step == t, target, targets)
+        device = lax.broadcasted_iota(jnp.int32, (1, devs), 1)
+        chosen_ref[t, 0:1, :] = device * tpt + routes_ref[t]
+        chosen_ref[t, 1:2, :] = jnp.where(routes_ref[t] == 0, from_ref[0:1, :], from_ref[1:2, :])
     targets = targets.astype(jnp.float32).astype(jnp.bfloat16)
     rows = lax.broadcasted_iota(jnp.int32, (devs * EXTRA, devs), 0) // EXTRA
     cols = lax.broadcasted_iota(jnp.int32, (devs * EXTRA, devs), 1)
@@ -144,26 +149,29 @@
         spikes_ref[:, lanes(b)] = spikes
         rows_ref[b * TRIALS : (b + 1) * TRIALS, :] = spikes
         blocks_ref[b] = spikes.astype(jnp.bfloat16)
-    copies[6].wait()
+    copies[7].wait()
     act_ref[...] = activity_of(population_rows(pops_ref[...]), rows_ref[...])
     copies[1].wait()
 
     def store(d, current):
         out_ref[d * long : d * long + TRIALS, :] = current
 
+    def pick_whole(d):
+        k = route_s[0, 0, d]
+        return src_s[k, d], d * tpt + k
+
+    def pick_routed(d):
+        return src_s[route_s[0, 0, d], d], base + d
+
     for c in range(WHOLE // CHUNK):
         whole(c).wait()
-        send_tiles(
-            c * CHUNK, (c + 1) * CHUNK, lambda d, k: d * tpt + k, route_s, src_s, blocks_ref, tiles_ref, store
-        )
+        send_tiles(c * CHUNK, (c + 1) * CHUNK, pick_whole, blocks_ref, tiles_ref, store)
     for c in range((devs - WHOLE) // CHUNK):
         at = WHOLE + c * CHUNK
         pltpu.make_async_copy(
             table_hbm.at[pl.ds(0, CHUNK)], tiles_ref.at[pl.ds(base + at, CHUNK)], routed_sems.at[c]
         ).wait()
-        send_tiles(
-            at, at + CHUNK, lambda d, k: base + d, route_s, src_s, blocks_ref, tiles_ref, store
-        )
+        send_tiles(at, at + CHUNK, pick_routed, blocks_ref, tiles_ref, store)
 
 
 def gate_kernel(message_ref, out_ref):
@@ -217,24 +225,20 @@
     return volts, cur
 
 
-def step_kernel(step, *refs):
-    (route_ref, src_ref, arrived_ref, codes_ref, volts_ref, cur_ref, ext_ref,
-     spikes_ref, dsyn_ref, dmem_ref, pops_ref, table_ref) = refs[:12]
-    volts_out, cur_out, spikes_out, out_ref, act_ref = refs[12:17]
-    route_s, src_s, blocks_ref, rows_ref, sems = refs[-5:]
+def step_kernel(step, last, *refs):
+    (chosen_ref, arrived_ref, codes_ref, volts_ref, cur_ref, ext_ref,
+     spikes_ref, dsyn_ref, dmem_ref, pops_ref, table_ref) = refs[:11]
+    volts_out, cur_out, spikes_out, out_ref, act_ref = refs[11:16]
+    chosen_s, blocks_ref, rows_ref, sems = refs[-5:-1]
+    sent_ref = refs[-1]
     devs = out_ref.shape[0]
     count = blocks_ref.shape[0]
-    tpt = table_ref.shape[0] // devs
-    to_smem = (
-        pltpu.make_async_copy(route_ref.at[step : step + 1], route_s, sems.at[0]),
-        pltpu.make_async_copy(src_ref, src_s, sems.at[1]),
-    )
-    for copy in to_smem:
-        copy.start()
+    to_smem = pltpu.make_async_copy(chosen_ref.at[step], chosen_s, sems.at[0])
+    to_smem.start()
     if step == 1:
         arrived = arrived_ref[...]
         codes, later = codes_of(arrived, devs)
-        refs[17][...] = later
+        refs[16][...] = later
     else:
         codes = codes_ref[...]
         arrived = arrived_ref[...].reshape(devs * TRIALS, BLOCK)
@@ -250,13 +254,31 @@
         rows_ref[b * TRIALS : (b + 1) * TRIALS, :] = spikes
         blocks_ref[b] = spikes.astype(jnp.bfloat16)
     act_ref[...] = activity_of(population_rows(pops_ref[...]), rows_ref[...])
-    for copy in to_smem:
-        copy.wait()
-
-    def store(d, current):
-        out_ref[d] = current
-
-    send_tiles(0, devs, lambda d, k: d * tpt + k, route_s, src_s, blocks_ref, table_ref, store)
+    to_smem.wait()
+
+    def pick(d):
+        return chosen_s[1, d], chosen_s[0, d]
+
+    if not last:
+
+        def store(d, current):
+            out_ref[d] = current
+
+        send_tiles(0, devs, pick, blocks_ref, table_ref, store)
+        return
+
+    def store_sent(d, current):
+        sent_ref[d] = current
+
+    size = devs // PIECES
+    pieces = []
+    for c in range(PIECES):
+        send_tiles(c * size, (c + 1) * size, pick, blocks_ref, table_ref, store_sent)
+        at = pl.ds(c * size, size)
+        pieces.append(pltpu.make_async_copy(sent_ref.at[at], out_ref.at[at], sems.at[1 + c]))
+        pieces[-1].start()
+    for piece in pieces:
+        piece.wait()
 
 
 def last_kernel(step, arrived_ref, codes_ref, volts_ref, cur_ref, ext_ref, spikes_ref,
@@ -317,14 +339,20 @@
         return pltpu.with_memory_space_constraint(array, pltpu.HBM)
 
     long = TRIALS + EXTRA
-    out, spikes, activity = pl.pallas_call(
+    out, spikes, activity, chosen = pl.pallas_call(
         first_kernel,
-        out_shape=(jax.ShapeDtypeStruct((devs * long, BLOCK), bf16), state, act),
+        out_shape=(
+            jax.ShapeDtypeStruct((devs * long, BLOCK), bf16),
+            state,
+            act,
+            jax.ShapeDtypeStruct((steps, 2, devs), i32),
+        ),
         in_specs=[HBM] * 7,
-        out_specs=(VMEM,) * 3,
+        out_specs=(VMEM,) * 4,
         scratch_shapes=scratch
         + [
             pltpu.VMEM((steps, 1, devs), i32),
+            pltpu.VMEM((tpt, devs), i32),
             pltpu.VMEM((tpt, devs), i32),
             pltpu.VMEM((steps, 1, devs), i32),
             pltpu.VMEM(state.shape, f32),
@@ -333,7 +361,7 @@
         ]
         + blocks
         + [
-            pltpu.SemaphoreType.DMA((7,)),
+            pltpu.SemaphoreType.DMA((8,)),
             pltpu.SemaphoreType.DMA((WHOLE // CHUNK,)),
             pltpu.SemaphoreType.DMA(((devs - WHOLE) // CHUNK,)),
         ],
@@ -358,24 +386,32 @@
     history = [activity]
     for step in range(1, steps):
         outs = [state, state, state, sent, act]
-        if step == steps - 1:
-            outs[3] = pltpu.VMEM(sent.shape, bf16)
+        last = step == steps - 1
+        out_specs = [VMEM] * len(outs)
         if step == 1:
             outs.append(jax.ShapeDtypeStruct((8, devs * TRIALS), i32))
+            out_specs.append(VMEM)
+        if last:
+            out_specs[3] = HBM
         results = pl.pallas_call(
-            functools.partial(step_kernel, step),
+            functools.partial(step_kernel, step, last),
             out_shape=tuple(outs),
-            in_specs=[VMEM] * 12,
-            out_specs=(VMEM,) * len(outs),
-            scratch_shapes=scratch + blocks + [pltpu.SemaphoreType.DMA((2,))],
+            in_specs=[VMEM] * 11,
+            out_specs=tuple(out_specs),
+            scratch_shapes=[pltpu.SMEM((2, devs), i32)]
+            + blocks
+            + [
+                pltpu.SemaphoreType.DMA((1 + PIECES,)),
+                pltpu.VMEM(sent.shape if last else (8, BLOCK), bf16),
+            ],
             compiler_params=params(8),
             name=f"step{step}",
-        )(route, src, arrived, codes, volts, cur, ext_drive, spikes, dsyn, dmem, pops, local_table)
+        )(chosen, arrived, codes, volts, cur, ext_drive, spikes, dsyn, dmem, pops, local_table)
         volts, cur, spikes, out, activity = results[:5]
         if step == 1:
             codes = results[5]
         history.append(activity)
-        if step == steps - 1:
+        if last:
             history, out = lax.optimization_barrier((history, out))
         arrived = exchange(out)
     rates = jnp.stack(history).sum(axis=2).reshape(steps, TRIALS, POPS)

time: 96.5 us -> 96.6 us (level)
  no operation moved by 1% of the time
where the time goes in v6:
time: 96.6 us; the launch traced here: 96.3 us
  blocking collectives  68.5 us (71%)
  Pallas kernels  11.5 us (12%)
  starting transfers between devices  8.28 us (9%)
  waiting for transfers between devices  6.27 us (6%)
    all_to_all x4, blocking collectives, exchange(): return lax.all_to_all(out, ('area', 'local'), 0, 0, tiled=True)  68.5 us
    pallas_call x4, Pallas kernels, shards(): pl.pallas_call(functools.partial(step_kernel, step, last), out_shape=tupl...  7.47 us
    ppermute x3, starting transfers between devices, shards(): lax.ppermute(rates, 'local', [(i, (i + shift) % n_local) for i in range(n...  4.34 us
    all_to_all x1, starting transfers between devices, exchange(): return lax.all_to_all(out, ('area', 'local'), 0, 0, tiled=True)  3.94 us
    all_to_all x1, waiting for transfers between devices, exchange(): return lax.all_to_all(out, ('area', 'local'), 0, 0, tiled=True)  3.46 us
    pallas_call x1, Pallas kernels, shards(): pl.pallas_call(first_kernel, out_shape=(jax.ShapeDtypeStruct((devs * long...  2.99 us
    ppermute x3, waiting for transfers between devices, shards(): lax.ppermute(rates, 'local', [(i, (i + shift) % n_local) for i in range(n...  2.81 us
  transfers between devices with their start and end apart: 4, of which 3 were waited for; matrix products, arithmetic and copies ran while one was open for 1% of the time, Pallas kernels for 0%

profile of v6, /device:TPU:1, one launch (start us, length us, event | category | flops | bytes accessed | tf_op | source)
XLA Modules:
  0.0 96.3 jit_solution(17092575017653816683)
XLA Ops:
  0.6 3.0 %first.1 = (bf16[1280,128]{1,0:T(8,128)(2,1)S(1)}, f32[8,4096]{1,0:T(8,128)S(1)}, f32[64,128]{1,0:T(8,128)S(1)}, s32[5,2,128]{2,1,0:T(2,128)S(1)}) custom-call(s32[5,1,128]{2,1,0:T(1,128)} %bitcast.49, s32[2,128]{1,0:T(2,128)} %bitcast.50, s32[2,128]{1,0:T(2,128)} %bitcast.51, s32[5,1,128]{2,1,0:T(1,128)} %counts_hbm.1, f32[8,4096]{1,0:T(8,128)} %refs_3_.1, ...), custom_call_target="tpu_custom_call" | custom-call | tf_op jit(solution)/shard_map/first/pallas_call | solution.py:342
  3.6 0.0 slice-start
  3.7 0.0 slice-start.1
  3.7 0.0 copy-start
  3.7 0.0 copy-start.1
  3.7 0.0 copy-start.2
  3.7 0.0 copy-start.3
  3.7 0.0 copy-start.4
  3.7 0.0 copy-start.5
  3.8 23.3 %all_to_all.25 = bf16[128,5,2,128]{3,2,1,0:T(2,128)(2,1)S(1)} all-to-all(bf16[128,5,2,128]{3,2,1,0:T(2,128)(2,1)S(1)} %bitcast.43), channel_id=1, replica_groups=mesh['area'=32,'local'=4] {'area','local'}, dimensions={0} | all-to-all | bytes 655360 | tf_op jit(solution)/shard_map/all_to_all | solution.py:336
  27.0 0.0 slice-done
  27.0 0.0 slice-done.1
  27.0 0.0 copy-done
  27.0 0.0 copy-done.1
  27.0 0.0 copy-done.2
  27.1 0.0 copy-done.3
  27.1 0.0 copy-done.4
  27.1 0.0 copy-done.5
  27.1 2.0 %step1.1 = (f32[8,4096]{1,0:T(8,128)S(1)}, f32[8,4096]{1,0:T(8,128)S(1)}, f32[8,4096]{1,0:T(8,128)S(1)}, bf16[128,8,128]{2,1,0:T(8,128)(2,1)S(1)}, f32[64,128]{1,0:T(8,128)S(1)}, /*index=5*/s32[8,1024]{1,0:T(8,128)S(1)}) custom-call(s32[5,2,128]{2,1,0:T(2,128)S(1)} %get-tuple-element.37.refs_0_, bf16[1280,128]{1,0:T(8,128)(2,1)S(1)} %bitcast.32, ...), custom_call_target="tpu_custom_call" | custom-call | tf_op jit(solution)/shard_map/step1/pallas_call | solution.py:396
  29.1 15.1 %all_to_all.26.refs_1_ = bf16[128,8,128]{2,1,0:T(8,128)(2,1)S(1)} all-to-all(bf16[128,8,128]{2,1,0:T(8,128)(2,1)S(1)} %get-tuple-element.41), channel_id=1, replica_groups=mesh['area'=32,'local'=4] {'area','local'}, dimensions={0} | all-to-all | bytes 524288 | tf_op jit(solution)/shard_map/all_to_all | solution.py:336
  44.2 1.6 %step2.1 = (f32[8,4096]{1,0:T(8,128)S(1)}, f32[8,4096]{1,0:T(8,128)S(1)}, f32[8,4096]{1,0:T(8,128)S(1)}, bf16[128,8,128]{2,1,0:T(8,128)(2,1)S(1)}, f32[64,128]{1,0:T(8,128)S(1)}) custom-call(s32[5,2,128]{2,1,0:T(2,128)S(1)} %get-tuple-element.37.refs_0_, bf16[128,8,128]{2,1,0:T(8,128)(2,1)S(1)} %all_to_all.26.refs_1_, ...), custom_call_target="tpu_custom_call" | custom-call | tf_op jit(solution)/shard_map/step2/pallas_call | solution.py:396
  45.8 15.1 %all_to_all.27.refs_1_ = bf16[128,8,128]{2,1,0:T(8,128)(2,1)S(1)} all-to-all(bf16[128,8,128]{2,1,0:T(8,128)(2,1)S(1)} %get-tuple-element.47), channel_id=1, replica_groups=mesh['area'=32,'local'=4] {'area','local'}, dimensions={0} | all-to-all | bytes 524288 | tf_op jit(solution)/shard_map/all_to_all | solution.py:336
  60.9 1.6 %step3.1 = (f32[8,4096]{1,0:T(8,128)S(1)}, f32[8,4096]{1,0:T(8,128)S(1)}, f32[8,4096]{1,0:T(8,128)S(1)}, bf16[128,8,128]{2,1,0:T(8,128)(2,1)S(1)}, f32[64,128]{1,0:T(8,128)S(1)}) custom-call(s32[5,2,128]{2,1,0:T(2,128)S(1)} %get-tuple-element.37.refs_0_, bf16[128,8,128]{2,1,0:T(8,128)(2,1)S(1)} %all_to_all.27.refs_1_, ...), custom_call_target="tpu_custom_call" | custom-call | tf_op jit(solution)/shard_map/step3/pallas_call | solution.py:396
  62.5 15.1 %all_to_all.28.refs_1_ = bf16[128,8,128]{2,1,0:T(8,128)(2,1)S(1)} all-to-all(bf16[128,8,128]{2,1,0:T(8,128)(2,1)S(1)} %get-tuple-element.52), channel_id=1, replica_groups=mesh['area'=32,'local'=4] {'area','local'}, dimensions={0} | all-to-all | bytes 524288 | tf_op jit(solution)/shard_map/all_to_all | solution.py:336
  77.6 2.2 %step4.1 = (f32[8,4096]{1,0:T(8,128)S(1)}, f32[8,4096]{1,0:T(8,128)S(1)}, f32[8,4096]{1,0:T(8,128)S(1)}, bf16[128,8,128]{2,1,0:T(8,128)(2,1)}, f32[64,128]{1,0:T(8,128)S(1)}) custom-call(s32[5,2,128]{2,1,0:T(2,128)S(1)} %get-tuple-element.37.refs_0_, bf16[128,8,128]{2,1,0:T(8,128)(2,1)S(1)} %all_to_all.28.refs_1_, ...), custom_call_target="tpu_custom_call" | custom-call | tf_op jit(solution)/shard_map/step4/pallas_call | solution.py:396
  79.8 3.9 %all-to-all-start.4 = ((bf16[128,8,128]{2,1,0:T(8,128)(2,1)}), bf16[128,8,128]{2,1,0:T(8,128)(2,1)S(1)}, u32[]{:S(2)}, u32[]{:S(2)}) async-start(bf16[128,8,128]{2,1,0:T(8,128)(2,1)} %get-tuple-element.58), calls=%async_computation.4 | async-start | bytes 524288 | tf_op jit(solution)/shard_map/all_to_all | solution.py:336
  83.8 0.1 reduce_sum.9
  84.0 0.1 reshape.37
  84.0 2.6 %collective-permute-start.2 = (f32[5,8,8]{2,1,0:T(8,128)S(1)}, f32[5,8,8]{2,1,0:T(8,128)S(1)}, u32[]{:S(2)}, u32[]{:S(2)}) collective-permute-start(f32[5,8,8]{2,1,0:T(8,128)S(1)} %reshape.37), channel_id=1, source_target_pairs={{0,3},{1,0},{2,1},{3,2},{4,7},{5,4},{6,5},{7,6},{8,11},{9,8},{10,9... | collective-permute-start | bytes 3848 | tf_op jit(solution)/shard_map/ppermute | solution.py:420
  86.6 0.0 collective-permute-start.1
  86.6 1.8 %collective-permute-start = (f32[5,8,8]{2,1,0:T(8,128)S(1)}, f32[5,8,8]{2,1,0:T(8,128)S(1)}, u32[]{:S(2)}, u32[]{:S(2)}) collective-permute-start(f32[5,8,8]{2,1,0:T(8,128)S(1)} %reshape.37), channel_id=1, source_target_pairs={{0,2},{1,3},{2,0},{3,1},{4,6},{5,7},{6,4},{7,5},{8,10},{9,11},{10,... | collective-permute-start | bytes 3848 | tf_op jit(solution)/shard_map/ppermute | solution.py:420
  88.4 0.0 collective-permute-done.2
  88.4 2.4 %collective-permute-done.1 = f32[5,8,8]{2,1,0:T(8,128)S(1)} collective-permute-done((f32[5,8,8]{2,1,0:T(8,128)S(1)}, f32[5,8,8]{2,1,0:T(8,128)S(1)}, u32[]{:S(2)}, u32[]{:S(2)}) %collective-permute-start.1) | collective-permute-done | bytes 1312 | tf_op jit(solution)/shard_map/ppermute | solution.py:420
  90.7 0.4 collective-permute-done
  91.2 0.6 multiply_bitcast_fusion
  91.8 3.5 %all-to-all-done.4.arrived_ref = bf16[128,8,128]{2,1,0:T(8,128)(2,1)S(1)} async-done(((bf16[128,8,128]{2,1,0:T(8,128)(2,1)}), bf16[128,8,128]{2,1,0:T(8,128)(2,1)S(1)}, u32[]{:S(2)}, u32[]{:S(2)}) %all-to-all-start.4) | async-done | bytes 262176 | tf_op jit(solution)/shard_map/all_to_all | solution.py:336
  95.3 1.0 %last.1 = (f32[8,4096]{1,0:T(8,128)}, f32[8,4096]{1,0:T(8,128)}) custom-call(bf16[128,8,128]{2,1,0:T(8,128)(2,1)S(1)} %all-to-all-done.4.arrived_ref, s32[8,1024]{1,0:T(8,128)S(1)} %get-tuple-element.42.refs_2_.codes_ref, f32[8,4096]{1,0:T(8,128)S(1)} %get-tuple-element.59.volts_ref, f32[8,4096]{1,0:T(8,128)S(1)} %get-tuple-element.60.cur_ref, ...), custom_call_target="tpu_custom_call" | custom-call | tf_op jit(solution)/shard_map/last/pallas_call | solution.py:425
  (9 shorter events, 0.0 us)
Async XLA Ops:
  3.6 23.4 %slice-start = ((s8[8388608]{0:T(1024)(128)(4,1)}), s8[4194304]{0:T(1024)(128)(4,1)S(1)}, s32[]{:S(2)}) async-start(s8[8388608]{0:T(1024)(128)(4,1)} %bitcast.26), calls=%async_computation.5 | async-start | bytes 8388608
  3.7 23.4 %slice-start.1 = ((s8[8388608]{0:T(1024)(128)(4,1)}), s8[4194304]{0:T(1024)(128)(4,1)S(1)}, s32[]{:S(2)}) async-start(s8[8388608]{0:T(1024)(128)(4,1)} %bitcast.26), calls=%async_computation.6 | async-start | bytes 8388608
  3.7 23.4 %copy-start = (f32[8,4096]{1,0:T(8,128)S(1)}, f32[8,4096]{1,0:T(8,128)}, u32[]{:S(2)}) copy-start(f32[8,4096]{1,0:T(8,128)} %ext_ref.1) | copy-start | bytes 393220
  3.7 23.4 %copy-start.1 = (f32[8,4096]{1,0:T(8,128)S(1)}, f32[8,4096]{1,0:T(8,128)}, u32[]{:S(2)}) copy-start(f32[8,4096]{1,0:T(8,128)} %refs_3_.1) | copy-start | bytes 393220
  3.7 23.4 %copy-start.2 = (f32[4096]{0:T(1024)S(1)}, f32[4096]{0:T(1024)}, u32[]{:S(2)}) copy-start(f32[4096]{0:T(1024)} %param.14) | copy-start | bytes 49156
  3.7 23.4 %copy-start.3 = (f32[4096]{0:T(1024)S(1)}, f32[4096]{0:T(1024)}, u32[]{:S(2)}) copy-start(f32[4096]{0:T(1024)} %param.15) | copy-start | bytes 49156
  3.7 23.4 %copy-start.4 = (f32[8,4096]{1,0:T(8,128)S(1)}, f32[8,4096]{1,0:T(8,128)}, u32[]{:S(2)}) copy-start(f32[8,4096]{1,0:T(8,128)} %refs_4_.1) | copy-start | bytes 393220
  3.7 23.3 %copy-start.5 = (s32[32]{0:T(128)S(1)}, s32[32]{0:T(128)}, u32[]{:S(2)}) copy-start(s32[32]{0:T(128)} %param.19) | copy-start | bytes 388
  79.8 15.4 %all-to-all-start.4 = ((bf16[128,8,128]{2,1,0:T(8,128)(2,1)}), bf16[128,8,128]{2,1,0:T(8,128)(2,1)S(1)}, u32[]{:S(2)}, u32[]{:S(2)}) async-start(bf16[128,8,128]{2,1,0:T(8,128)(2,1)} %get-tuple-element.58), calls=%async_computation.4 | async-start | bytes 524288 | tf_op jit(solution)/shard_map/all_to_all | solution.py:336
  84.0 4.3 %collective-permute-start.2 = (f32[5,8,8]{2,1,0:T(8,128)S(1)}, f32[5,8,8]{2,1,0:T(8,128)S(1)}, u32[]{:S(2)}, u32[]{:S(2)}) collective-permute-start(f32[5,8,8]{2,1,0:T(8,128)S(1)} %reshape.37), channel_id=1, source_target_pairs={{0,3},{1,0},{2,1},{3,2},{4,7},{5,4},{6,5},{7,6},{8,11},{9,8},{10,9... | collective-permute-start | bytes 3848 | tf_op jit(solution)/shard_map/ppermute | solution.py:420
  86.6 4.1 %collective-permute-start.1 = (f32[5,8,8]{2,1,0:T(8,128)S(1)}, f32[5,8,8]{2,1,0:T(8,128)S(1)}, u32[]{:S(2)}, u32[]{:S(2)}) collective-permute-start(f32[5,8,8]{2,1,0:T(8,128)S(1)} %reshape.37), channel_id=1, source_target_pairs={{0,1},{1,2},{2,3},{3,0},{4,5},{5,6},{6,7},{7,4},{8,9},{9,10},{10,1... | collective-permute-start | bytes 3848 | tf_op jit(solution)/shard_map/ppermute | solution.py:420
  86.6 4.6 %collective-permute-start = (f32[5,8,8]{2,1,0:T(8,128)S(1)}, f32[5,8,8]{2,1,0:T(8,128)S(1)}, u32[]{:S(2)}, u32[]{:S(2)}) collective-permute-start(f32[5,8,8]{2,1,0:T(8,128)S(1)} %reshape.37), channel_id=1, source_target_pairs={{0,2},{1,3},{2,0},{3,1},{4,6},{5,7},{6,4},{7,5},{8,10},{9,11},{10,... | collective-permute-start | bytes 3848 | tf_op jit(solution)/shard_map/ppermute | solution.py:420

commit v7 on v6

--- a/solution.py
+++ b/solution.py
@@ -73,10 +73,10 @@
 
 
 def first_kernel(
-    route_hbm, src_hbm, dst_hbm, counts_hbm, volts_hbm, pops_hbm, table_hbm,
-    out_ref, spikes_ref, act_ref, chosen_ref,
-    route_s, src_s, routes_ref, from_ref, dst_ref, counts_ref, volts_ref, pops_ref, tiles_ref,
-    blocks_ref, rows_ref, sems, whole_sems, routed_sems,
+    route_hbm, src_hbm, dst_hbm, counts_hbm, volts_hbm, table_hbm,
+    out_ref, spikes_ref, chosen_ref,
+    route_s, src_s, routes_ref, from_ref, dst_ref, counts_ref, volts_ref, tiles_ref,
+    blocks_ref, sems, whole_sems, routed_sems,
 ):
     tpt, devs = dst_ref.shape
     steps = routes_ref.shape[0]
@@ -91,7 +91,6 @@
                 (dst_hbm, dst_ref),
                 (counts_hbm, counts_ref),
                 (src_hbm, from_ref),
-                (pops_hbm, pops_ref),
             )
         )
     ]
@@ -130,8 +129,8 @@
         target = jnp.where(counts_ref[t] > 0, target, NO_BLOCK)
         targets = jnp.where(step == t, target, targets)
         device = lax.broadcasted_iota(jnp.int32, (1, devs), 1)
-        chosen_ref[t, 0:1, :] = device * tpt + routes_ref[t]
-        chosen_ref[t, 1:2, :] = jnp.where(routes_ref[t] == 0, from_ref[0:1, :], from_ref[1:2, :])
+        chosen_ref[t, 0] = device * tpt + routes_ref[t]
+        chosen_ref[t, 1] = jnp.where(routes_ref[t] == 0, from_ref[0:1, :], from_ref[1:2, :])
     targets = targets.astype(jnp.float32).astype(jnp.bfloat16)
     rows = lax.broadcasted_iota(jnp.int32, (devs * EXTRA, devs), 0) // EXTRA
     cols = lax.broadcasted_iota(jnp.int32, (devs * EXTRA, devs), 1)
@@ -147,10 +146,7 @@
     for b in range(blocks_ref.shape[0]):
         spikes = spike_of(volts_ref[:, lanes(b)])
         spikes_ref[:, lanes(b)] = spikes
-        rows_ref[b * TRIALS : (b + 1) * TRIALS, :] = spikes
         blocks_ref[b] = spikes.astype(jnp.bfloat16)
-    copies[7].wait()
-    act_ref[...] = activity_of(population_rows(pops_ref[...]), rows_ref[...])
     copies[1].wait()
 
     def store(d, current):
@@ -227,18 +223,25 @@
 
 def step_kernel(step, last, *refs):
     (chosen_ref, arrived_ref, codes_ref, volts_ref, cur_ref, ext_ref,
-     spikes_ref, dsyn_ref, dmem_ref, pops_ref, table_ref) = refs[:11]
-    volts_out, cur_out, spikes_out, out_ref, act_ref = refs[11:16]
-    chosen_s, blocks_ref, rows_ref, sems = refs[-5:-1]
+     spikes_ref, dsyn_ref, dmem_ref, table_ref) = refs[:10]
+    volts_out, cur_out, spikes_out, out_ref = refs[10:14]
+    chosen_s, blocks_ref, sems = refs[-4:-1]
     sent_ref = refs[-1]
     devs = out_ref.shape[0]
     count = blocks_ref.shape[0]
-    to_smem = pltpu.make_async_copy(chosen_ref.at[step], chosen_s, sems.at[0])
-    to_smem.start()
+
+    def to_smem(row):
+        return pltpu.make_async_copy(chosen_ref.at[step, row], chosen_s.at[row], sems.at[row])
+
+    def start(row, carry):
+        to_smem(row).start()
+        return carry
+
+    lax.fori_loop(0, 2, start, 0)
     if step == 1:
         arrived = arrived_ref[...]
         codes, later = codes_of(arrived, devs)
-        refs[16][...] = later
+        refs[14][...] = later
     else:
         codes = codes_ref[...]
         arrived = arrived_ref[...].reshape(devs * TRIALS, BLOCK)
@@ -251,13 +254,12 @@
         cur_out[:, lanes(b)] = cur
         spikes = spike_of(volts)
         spikes_out[:, lanes(b)] = spikes
-        rows_ref[b * TRIALS : (b + 1) * TRIALS, :] = spikes
         blocks_ref[b] = spikes.astype(jnp.bfloat16)
-    act_ref[...] = activity_of(population_rows(pops_ref[...]), rows_ref[...])
-    to_smem.wait()
+    to_smem(0).wait()
+    to_smem(1).wait()
 
     def pick(d):
-        return chosen_s[1, d], chosen_s[0, d]
+        return chosen_s[1, 0, d], chosen_s[0, 0, d]
 
     if not last:
 
@@ -275,10 +277,19 @@
     for c in range(PIECES):
         send_tiles(c * size, (c + 1) * size, pick, blocks_ref, table_ref, store_sent)
         at = pl.ds(c * size, size)
-        pieces.append(pltpu.make_async_copy(sent_ref.at[at], out_ref.at[at], sems.at[1 + c]))
+        pieces.append(pltpu.make_async_copy(sent_ref.at[at], out_ref.at[at], sems.at[2 + c]))
         pieces[-1].start()
     for piece in pieces:
         piece.wait()
+
+
+def activity_kernel(pops_ref, *refs):
+    spikes_refs, act_ref, rows_ref = refs[:-2], refs[-2], refs[-1]
+    member = population_rows(pops_ref[...])
+    for t, spikes_ref in enumerate(spikes_refs):
+        for b in range(spikes_ref.shape[1] // BLOCK):
+            rows_ref[t, b * TRIALS : (b + 1) * TRIALS, :] = spikes_ref[:, lanes(b)]
+        act_ref[t] = activity_of(member, rows_ref[t])
 
 
 def last_kernel(step, arrived_ref, codes_ref, volts_ref, cur_ref, ext_ref, spikes_ref,
@@ -322,15 +333,11 @@
     pops = blk_pop.reshape(1, count)
     state = jax.ShapeDtypeStruct((TRIALS, count * BLOCK), f32)
     sent = jax.ShapeDtypeStruct((devs, TRIALS, BLOCK), bf16)
-    act = jax.ShapeDtypeStruct((POPS * TRIALS, BLOCK), f32)
     scratch = [
         pltpu.SMEM((1, 1, devs), i32),
         pltpu.SMEM((tpt, devs), i32),
     ]
-    blocks = [
-        pltpu.VMEM((count, TRIALS, BLOCK), bf16),
-        pltpu.VMEM((count * TRIALS, BLOCK), f32),
-    ]
+    blocks = [pltpu.VMEM((count, TRIALS, BLOCK), bf16)]
 
     def exchange(out):
         return lax.all_to_all(out, ("area", "local"), 0, 0, tiled=True)
@@ -339,16 +346,15 @@
         return pltpu.with_memory_space_constraint(array, pltpu.HBM)
 
     long = TRIALS + EXTRA
-    out, spikes, activity, chosen = pl.pallas_call(
+    out, spikes, chosen = pl.pallas_call(
         first_kernel,
         out_shape=(
             jax.ShapeDtypeStruct((devs * long, BLOCK), bf16),
             state,
-            act,
-            jax.ShapeDtypeStruct((steps, 2, devs), i32),
+            jax.ShapeDtypeStruct((steps, 2, 1, devs), i32),
         ),
-        in_specs=[HBM] * 7,
-        out_specs=(VMEM,) * 4,
+        in_specs=[HBM] * 6,
+        out_specs=(VMEM,) * 3,
         scratch_shapes=scratch
         + [
             pltpu.VMEM((steps, 1, devs), i32),
@@ -356,18 +362,17 @@
             pltpu.VMEM((tpt, devs), i32),
             pltpu.VMEM((steps, 1, devs), i32),
             pltpu.VMEM(state.shape, f32),
-            pltpu.VMEM((1, count), i32),
             pltpu.VMEM((devs + WHOLE * (tpt - 1), BLOCK, BLOCK), bf16),
         ]
         + blocks
         + [
-            pltpu.SemaphoreType.DMA((8,)),
+            pltpu.SemaphoreType.DMA((7,)),
             pltpu.SemaphoreType.DMA((WHOLE // CHUNK,)),
             pltpu.SemaphoreType.DMA(((devs - WHOLE) // CHUNK,)),
         ],
         compiler_params=params(16),
         name="first",
-    )(*[in_hbm(a) for a in (route, src, dst, used, potential, pops, table)])
+    )(*[in_hbm(a) for a in (route, src, dst, used, potential, table)])
     for i in range(2):
         out = pl.pallas_call(
             gate_kernel,
@@ -383,9 +388,9 @@
     local_table = table
     volts, cur = potential, current
     codes = jnp.zeros((8, devs * TRIALS), i32)
-    history = [activity]
+    history = [spikes]
     for step in range(1, steps):
-        outs = [state, state, state, sent, act]
+        outs = [state, state, state, sent]
         last = step == steps - 1
         out_specs = [VMEM] * len(outs)
         if step == 1:
@@ -396,25 +401,34 @@
         results = pl.pallas_call(
             functools.partial(step_kernel, step, last),
             out_shape=tuple(outs),
-            in_specs=[VMEM] * 11,
+            in_specs=[VMEM] * 10,
             out_specs=tuple(out_specs),
-            scratch_shapes=[pltpu.SMEM((2, devs), i32)]
+            scratch_shapes=[pltpu.SMEM((2, 1, devs), i32)]
             + blocks
             + [
-                pltpu.SemaphoreType.DMA((1 + PIECES,)),
+                pltpu.SemaphoreType.DMA((2 + PIECES,)),
                 pltpu.VMEM(sent.shape if last else (8, BLOCK), bf16),
             ],
             compiler_params=params(8),
             name=f"step{step}",
-        )(chosen, arrived, codes, volts, cur, ext_drive, spikes, dsyn, dmem, pops, local_table)
-        volts, cur, spikes, out, activity = results[:5]
+        )(chosen, arrived, codes, volts, cur, ext_drive, spikes, dsyn, dmem, local_table)
+        volts, cur, spikes, out = results[:4]
         if step == 1:
-            codes = results[5]
-        history.append(activity)
+            codes = results[4]
+        history.append(spikes)
         if last:
             history, out = lax.optimization_barrier((history, out))
         arrived = exchange(out)
-    rates = jnp.stack(history).sum(axis=2).reshape(steps, TRIALS, POPS)
+    activity = pl.pallas_call(
+        activity_kernel,
+        out_shape=jax.ShapeDtypeStruct((steps, TRIALS * POPS, BLOCK), f32),
+        in_specs=[VMEM] * (1 + steps),
+        out_specs=VMEM,
+        scratch_shapes=[pltpu.VMEM((steps, count * TRIALS, BLOCK), f32)],
+        compiler_params=params(8),
+        name="activity",
+    )(pops, *history)
+    rates = activity.sum(axis=2).reshape(steps, TRIALS, POPS)
     n_local = lax.axis_size("local")
     parts = [rates] + [
         lax.ppermute(rates, "local", [(i, (i + shift) % n_local) for i in range(n_local)])

time: 96.6 us -> 95 us (0.983)
  Pallas kernels: 11.5 us -> 10.4 us
    pallas_call x4, Pallas kernels: 7.47 us -> 6.08 us  [shards(): pl.pallas_call(functools.partial(step_kernel, step, last), out_shape=tupl...]
where the time goes in v7:
time: 95 us; the launch traced here: 94.7 us
  blocking collectives  68.5 us (72%)
  Pallas kernels  10.4 us (11%)
  starting transfers between devices  8.28 us (9%)
  waiting for transfers between devices  5.83 us (6%)
    all_to_all x4, blocking collectives, exchange(): return lax.all_to_all(out, ('area', 'local'), 0, 0, tiled=True)  68.5 us
    pallas_call x4, Pallas kernels, shards(): pl.pallas_call(functools.partial(step_kernel, step, last), out_shape=tupl...  6.08 us
    ppermute x3, starting transfers between devices, shards(): lax.ppermute(rates, 'local', [(i, (i + shift) % n_local) for i in range(n...  4.34 us
    all_to_all x1, starting transfers between devices, exchange(): return lax.all_to_all(out, ('area', 'local'), 0, 0, tiled=True)  3.95 us
    all_to_all x1, waiting for transfers between devices, exchange(): return lax.all_to_all(out, ('area', 'local'), 0, 0, tiled=True)  3.01 us
    pallas_call x1, Pallas kernels, shards(): pl.pallas_call(first_kernel, out_shape=(jax.ShapeDtypeStruct((devs * long...  2.97 us
    ppermute x3, waiting for transfers between devices, shards(): lax.ppermute(rates, 'local', [(i, (i + shift) % n_local) for i in range(n...  2.81 us
  transfers between devices with their start and end apart: 4, of which 3 were waited for; matrix products, arithmetic and copies ran while one was open for 1% of the time, Pallas kernels for 0%

profile of v7, /device:TPU:1, one launch (start us, length us, event | category | flops | bytes accessed | tf_op | source)
XLA Modules:
  0.0 94.7 jit_solution(15183698500138317664)
XLA Ops:
  0.6 3.0 %first.1 = (bf16[1280,128]{1,0:T(8,128)(2,1)S(1)}, f32[8,4096]{1,0:T(8,128)S(1)}, s32[5,2,1,128]{3,2,1,0:T(1,128)S(1)}) custom-call(s32[5,1,128]{2,1,0:T(1,128)} %bitcast.35, s32[2,128]{1,0:T(2,128)} %bitcast.36, s32[2,128]{1,0:T(2,128)} %bitcast.37, s32[5,1,128]{2,1,0:T(1,128)} %counts_hbm.1, f32[8,4096]{1,0:T(8,128)} %refs_3_.1, ...), custom_call_target="tpu_custom_call" | custom-call | tf_op jit(solution)/shard_map/first/pallas_call | solution.py:349
  3.6 0.0 slice-start
  3.6 0.0 slice-start.1
  3.6 0.0 copy-start
  3.7 0.0 copy-start.1
  3.7 0.0 copy-start.2
  3.7 0.0 copy-start.3
  3.7 0.0 copy-start.4
  3.7 23.3 %all_to_all.25 = bf16[128,5,2,128]{3,2,1,0:T(2,128)(2,1)S(1)} all-to-all(bf16[128,5,2,128]{3,2,1,0:T(2,128)(2,1)S(1)} %bitcast.33), channel_id=1, replica_groups=mesh['area'=32,'local'=4] {'area','local'}, dimensions={0} | all-to-all | bytes 655360 | tf_op jit(solution)/shard_map/all_to_all | solution.py:343
  27.0 0.0 slice-done
  27.0 0.0 slice-done.1
  27.0 0.0 copy-done
  27.0 0.0 copy-done.1
  27.0 0.0 copy-done.2
  27.0 0.0 copy-done.3
  27.0 0.0 copy-done.4
  27.1 1.6 %step1.1 = (f32[8,4096]{1,0:T(8,128)S(1)}, f32[8,4096]{1,0:T(8,128)S(1)}, f32[8,4096]{1,0:T(8,128)S(1)}, bf16[128,8,128]{2,1,0:T(8,128)(2,1)S(1)}, s32[8,1024]{1,0:T(8,128)S(1)}) custom-call(s32[5,2,1,128]{3,2,1,0:T(1,128)S(1)} %get-tuple-element.32.refs_0_, bf16[1280,128]{1,0:T(8,128)(2,1)S(1)} %bitcast.22, s32[8,1024]{1,0:T(8,128)S(1)} %broadcast_in_dim.6.refs_2_, ...), custom_call_target="tpu_custom_call" | custom-call | tf_op jit(solution)/shard_map/step1/pallas_call | solution.py:401
  28.6 15.1 %all_to_all.26.refs_1_ = bf16[128,8,128]{2,1,0:T(8,128)(2,1)S(1)} all-to-all(bf16[128,8,128]{2,1,0:T(8,128)(2,1)S(1)} %get-tuple-element.35), channel_id=1, replica_groups=mesh['area'=32,'local'=4] {'area','local'}, dimensions={0} | all-to-all | bytes 524288 | tf_op jit(solution)/shard_map/all_to_all | solution.py:343
  43.7 1.3 %step2.1 = (f32[8,4096]{1,0:T(8,128)S(1)}, f32[8,4096]{1,0:T(8,128)S(1)}, f32[8,4096]{1,0:T(8,128)S(1)}, bf16[128,8,128]{2,1,0:T(8,128)(2,1)S(1)}) custom-call(s32[5,2,1,128]{3,2,1,0:T(1,128)S(1)} %get-tuple-element.32.refs_0_, bf16[128,8,128]{2,1,0:T(8,128)(2,1)S(1)} %all_to_all.26.refs_1_, s32[8,1024]{1,0:T(8,128)S(1)} %get-tuple-element.36.refs_2_.codes_ref, ...), custom_call_target="tpu_custom_call" | custom-call | tf_op jit(solution)/shard_map/step2/pallas_call | solution.py:401
  45.0 15.1 %all_to_all.27.refs_1_ = bf16[128,8,128]{2,1,0:T(8,128)(2,1)S(1)} all-to-all(bf16[128,8,128]{2,1,0:T(8,128)(2,1)S(1)} %get-tuple-element.40), channel_id=1, replica_groups=mesh['area'=32,'local'=4] {'area','local'}, dimensions={0} | all-to-all | bytes 524288 | tf_op jit(solution)/shard_map/all_to_all | solution.py:343
  60.1 0.0 copy-start.5
  60.1 1.3 %step3.1 = (f32[8,4096]{1,0:T(8,128)S(1)}, f32[8,4096]{1,0:T(8,128)S(1)}, f32[8,4096]{1,0:T(8,128)S(1)}, bf16[128,8,128]{2,1,0:T(8,128)(2,1)S(1)}) custom-call(s32[5,2,1,128]{3,2,1,0:T(1,128)S(1)} %get-tuple-element.32.refs_0_, bf16[128,8,128]{2,1,0:T(8,128)(2,1)S(1)} %all_to_all.27.refs_1_, s32[8,1024]{1,0:T(8,128)S(1)} %get-tuple-element.36.refs_2_.codes_ref, ...), custom_call_target="tpu_custom_call" | custom-call | tf_op jit(solution)/shard_map/step3/pallas_call | solution.py:401
  61.4 15.1 %all_to_all.28.refs_1_ = bf16[128,8,128]{2,1,0:T(8,128)(2,1)S(1)} all-to-all(bf16[128,8,128]{2,1,0:T(8,128)(2,1)S(1)} %get-tuple-element.44), channel_id=1, replica_groups=mesh['area'=32,'local'=4] {'area','local'}, dimensions={0} | all-to-all | bytes 524288 | tf_op jit(solution)/shard_map/all_to_all | solution.py:343
  76.5 1.9 %step4.1 = (f32[8,4096]{1,0:T(8,128)S(1)}, f32[8,4096]{1,0:T(8,128)S(1)}, f32[8,4096]{1,0:T(8,128)S(1)}, bf16[128,8,128]{2,1,0:T(8,128)(2,1)}) custom-call(s32[5,2,1,128]{3,2,1,0:T(1,128)S(1)} %get-tuple-element.32.refs_0_, bf16[128,8,128]{2,1,0:T(8,128)(2,1)S(1)} %all_to_all.28.refs_1_, s32[8,1024]{1,0:T(8,128)S(1)} %get-tuple-element.36.refs_2_.codes_ref, ...), custom_call_target="tpu_custom_call" | custom-call | tf_op jit(solution)/shard_map/step4/pallas_call | solution.py:401
  78.4 3.9 %all-to-all-start.4 = ((bf16[128,8,128]{2,1,0:T(8,128)(2,1)}), bf16[128,8,128]{2,1,0:T(8,128)(2,1)S(1)}, u32[]{:S(2)}, u32[]{:S(2)}) async-start(bf16[128,8,128]{2,1,0:T(8,128)(2,1)} %get-tuple-element.49), calls=%async_computation.4 | async-start | bytes 524288 | tf_op jit(solution)/shard_map/all_to_all | solution.py:343
  82.3 0.0 copy-done.5
  82.4 0.3 activity.1
  82.7 0.1 reduce_sum.9
  82.8 0.1 reshape.37
  82.9 2.6 %collective-permute-start.2 = (f32[5,8,8]{2,1,0:T(8,128)S(1)}, f32[5,8,8]{2,1,0:T(8,128)S(1)}, u32[]{:S(2)}, u32[]{:S(2)}) collective-permute-start(f32[5,8,8]{2,1,0:T(8,128)S(1)} %reshape.37), channel_id=1, source_target_pairs={{0,3},{1,0},{2,1},{3,2},{4,7},{5,4},{6,5},{7,6},{8,11},{9,8},{10,9... | collective-permute-start | bytes 3848 | tf_op jit(solution)/shard_map/ppermute | solution.py:434
  85.5 0.0 collective-permute-start.1
  85.5 1.8 %collective-permute-start = (f32[5,8,8]{2,1,0:T(8,128)S(1)}, f32[5,8,8]{2,1,0:T(8,128)S(1)}, u32[]{:S(2)}, u32[]{:S(2)}) collective-permute-start(f32[5,8,8]{2,1,0:T(8,128)S(1)} %reshape.37), channel_id=1, source_target_pairs={{0,2},{1,3},{2,0},{3,1},{4,6},{5,7},{6,4},{7,5},{8,10},{9,11},{10,... | collective-permute-start | bytes 3848 | tf_op jit(solution)/shard_map/ppermute | solution.py:434
  87.2 0.0 collective-permute-done.2
  87.3 2.4 %collective-permute-done.1 = f32[5,8,8]{2,1,0:T(8,128)S(1)} collective-permute-done((f32[5,8,8]{2,1,0:T(8,128)S(1)}, f32[5,8,8]{2,1,0:T(8,128)S(1)}, u32[]{:S(2)}, u32[]{:S(2)}) %collective-permute-start.1) | collective-permute-done | bytes 1312 | tf_op jit(solution)/shard_map/ppermute | solution.py:434
  89.6 0.4 collective-permute-done
  90.1 0.6 multiply_bitcast_fusion
  90.7 3.0 %all-to-all-done.4.arrived_ref = bf16[128,8,128]{2,1,0:T(8,128)(2,1)S(1)} async-done(((bf16[128,8,128]{2,1,0:T(8,128)(2,1)}), bf16[128,8,128]{2,1,0:T(8,128)(2,1)S(1)}, u32[]{:S(2)}, u32[]{:S(2)}) %all-to-all-start.4) | async-done | bytes 262176 | tf_op jit(solution)/shard_map/all_to_all | solution.py:343
  93.7 1.0 %last.1 = (f32[8,4096]{1,0:T(8,128)}, f32[8,4096]{1,0:T(8,128)}) custom-call(bf16[128,8,128]{2,1,0:T(8,128)(2,1)S(1)} %all-to-all-done.4.arrived_ref, s32[8,1024]{1,0:T(8,128)S(1)} %get-tuple-element.36.refs_2_.codes_ref, f32[8,4096]{1,0:T(8,128)S(1)} %get-tuple-element.50.volts_ref, f32[8,4096]{1,0:T(8,128)S(1)} %get-tuple-element.51.cur_ref, ...), custom_call_target="tpu_custom_call" | custom-call | tf_op jit(solution)/shard_map/last/pallas_call | solution.py:439
  (4 shorter events, 0.0 us)
Async XLA Ops:
  3.6 23.4 %slice-start = ((s8[8388608]{0:T(1024)(128)(4,1)}), s8[4194304]{0:T(1024)(128)(4,1)S(1)}, s32[]{:S(2)}) async-start(s8[8388608]{0:T(1024)(128)(4,1)} %bitcast.16), calls=%async_computation.5 | async-start | bytes 8388608
  3.6 23.4 %slice-start.1 = ((s8[8388608]{0:T(1024)(128)(4,1)}), s8[4194304]{0:T(1024)(128)(4,1)S(1)}, s32[]{:S(2)}) async-start(s8[8388608]{0:T(1024)(128)(4,1)} %bitcast.16), calls=%async_computation.6 | async-start | bytes 8388608
  3.6 23.3 %copy-start = (f32[8,4096]{1,0:T(8,128)S(1)}, f32[8,4096]{1,0:T(8,128)}, u32[]{:S(2)}) copy-start(f32[8,4096]{1,0:T(8,128)} %ext_ref.1) | copy-start | bytes 393220
  3.7 23.3 %copy-start.1 = (f32[8,4096]{1,0:T(8,128)S(1)}, f32[8,4096]{1,0:T(8,128)}, u32[]{:S(2)}) copy-start(f32[8,4096]{1,0:T(8,128)} %refs_3_.1) | copy-start | bytes 393220
  3.7 23.3 %copy-start.2 = (f32[4096]{0:T(1024)S(1)}, f32[4096]{0:T(1024)}, u32[]{:S(2)}) copy-start(f32[4096]{0:T(1024)} %param.14) | copy-start | bytes 49156
  3.7 23.3 %copy-start.3 = (f32[4096]{0:T(1024)S(1)}, f32[4096]{0:T(1024)}, u32[]{:S(2)}) copy-start(f32[4096]{0:T(1024)} %param.15) | copy-start | bytes 49156
  3.7 23.3 %copy-start.4 = (f32[8,4096]{1,0:T(8,128)S(1)}, f32[8,4096]{1,0:T(8,128)}, u32[]{:S(2)}) copy-start(f32[8,4096]{1,0:T(8,128)} %refs_4_.1) | copy-start | bytes 393220
  60.1 22.3 %copy-start.5 = (s32[32]{0:T(128)S(1)}, s32[32]{0:T(128)}, u32[]{:S(2)}) copy-start(s32[32]{0:T(128)} %param.19) | copy-start | bytes 388
  78.4 15.3 %all-to-all-start.4 = ((bf16[128,8,128]{2,1,0:T(8,128)(2,1)}), bf16[128,8,128]{2,1,0:T(8,128)(2,1)S(1)}, u32[]{:S(2)}, u32[]{:S(2)}) async-start(bf16[128,8,128]{2,1,0:T(8,128)(2,1)} %get-tuple-element.49), calls=%async_computation.4 | async-start | bytes 524288 | tf_op jit(solution)/shard_map/all_to_all | solution.py:343
  82.9 4.3 %collective-permute-start.2 = (f32[5,8,8]{2,1,0:T(8,128)S(1)}, f32[5,8,8]{2,1,0:T(8,128)S(1)}, u32[]{:S(2)}, u32[]{:S(2)}) collective-permute-start(f32[5,8,8]{2,1,0:T(8,128)S(1)} %reshape.37), channel_id=1, source_target_pairs={{0,3},{1,0},{2,1},{3,2},{4,7},{5,4},{6,5},{7,6},{8,11},{9,8},{10,9... | collective-permute-start | bytes 3848 | tf_op jit(solution)/shard_map/ppermute | solution.py:434
  85.5 4.1 %collective-permute-start.1 = (f32[5,8,8]{2,1,0:T(8,128)S(1)}, f32[5,8,8]{2,1,0:T(8,128)S(1)}, u32[]{:S(2)}, u32[]{:S(2)}) collective-permute-start(f32[5,8,8]{2,1,0:T(8,128)S(1)} %reshape.37), channel_id=1, source_target_pairs={{0,1},{1,2},{2,3},{3,0},{4,5},{5,6},{6,7},{7,4},{8,9},{9,10},{10,1... | collective-permute-start | bytes 3848 | tf_op jit(solution)/shard_map/ppermute | solution.py:434
  85.5 4.6 %collective-permute-start = (f32[5,8,8]{2,1,0:T(8,128)S(1)}, f32[5,8,8]{2,1,0:T(8,128)S(1)}, u32[]{:S(2)}, u32[]{:S(2)}) collective-permute-start(f32[5,8,8]{2,1,0:T(8,128)S(1)} %reshape.37), channel_id=1, source_target_pairs={{0,2},{1,3},{2,0},{3,1},{4,6},{5,7},{6,4},{7,5},{8,10},{9,11},{10,... | collective-permute-start | bytes 3848 | tf_op jit(solution)/shard_map/ppermute | solution.py:434

commit v8 on v7

--- a/solution.py
+++ b/solution.py
@@ -74,7 +74,7 @@
 
 def first_kernel(
     route_hbm, src_hbm, dst_hbm, counts_hbm, volts_hbm, table_hbm,
-    out_ref, spikes_ref, chosen_ref,
+    out_ref, spikes_ref, chosen_ref, gather_ref, spread_ref,
     route_s, src_s, routes_ref, from_ref, dst_ref, counts_ref, volts_ref, tiles_ref,
     blocks_ref, sems, whole_sems, routed_sems,
 ):
@@ -142,6 +142,11 @@
     for d in range(devs):
         out_ref[d * long + TRIALS : (d + 1) * long, :] = extra[d * EXTRA : (d + 1) * EXTRA, :]
 
+    row, col = iotas(gather_ref.shape)
+    gather_ref[...] = one_hot(row // long, col)
+    row, col = iotas(spread_ref.shape)
+    spread_ref[...] = one_hot(row, col // TRIALS)
+
     copies[2].wait()
     for b in range(blocks_ref.shape[0]):
         spikes = spike_of(volts_ref[:, lanes(b)])
@@ -178,7 +183,7 @@
     return lax.broadcasted_iota(jnp.int32, shape, 0), lax.broadcasted_iota(jnp.int32, shape, 1)
 
 
-def codes_of(message, devs):
+def codes_of(message, gather, spread):
     long = TRIALS + EXTRA
     read = lax.dot_general(
         one_hot(*iotas((8, BLOCK))), message, (((1,), (1,)), ((), ())), preferred_element_type=jnp.float32
@@ -191,21 +196,26 @@
     near = near + pltpu.roll(near, width - 2, 1)
     near = near + pltpu.roll(near, width - 4, 1)
     here = jnp.where(place < TRIALS, near.astype(jnp.int32) * TRIALS + place, -1)
-    row, col = iotas((devs * long, devs))
     one = jnp.dot(
-        jnp.where(place == TRIALS, blocks, 0.0).astype(jnp.bfloat16),
-        one_hot(row // long, col),
-        preferred_element_type=jnp.float32,
+        jnp.where(place == TRIALS, blocks, 0.0).astype(jnp.bfloat16), gather, preferred_element_type=jnp.float32
     ).astype(jnp.bfloat16)
-    row, col = iotas((devs, devs * TRIALS))
-    later = jnp.dot(one, one_hot(row, col // TRIALS), preferred_element_type=jnp.float32)
+    later = jnp.dot(one, spread, preferred_element_type=jnp.float32)
     trial = lax.broadcasted_iota(jnp.int32, later.shape, 1) % TRIALS
     return here, later.astype(jnp.int32) * TRIALS + trial
 
 
 def inflow_of(code, arrived, rows):
-    row = lax.broadcasted_iota(jnp.int32, (rows, code.shape[1]), 0)
-    return jnp.dot(one_hot(row, code), arrived, preferred_element_type=jnp.float32)
+    row = lax.broadcasted_iota(jnp.int32, (rows, BLOCK), 0).astype(jnp.float32).astype(jnp.bfloat16)
+    code = jnp.broadcast_to(code.astype(jnp.float32), (16, code.shape[1])).astype(jnp.bfloat16)
+    one, zero = jnp.ones((), jnp.bfloat16), jnp.zeros((), jnp.bfloat16)
+    deliver = jnp.concatenate(
+        [
+            jnp.where(row == jnp.concatenate([code[:, lanes(c)]] * (rows // 16), axis=0), one, zero)
+            for c in range(code.shape[1] // BLOCK)
+        ],
+        axis=1,
+    )
+    return jnp.dot(deliver, arrived, preferred_element_type=jnp.float32)
 
 
 def update(b, inflow, volts_ref, cur_ref, ext_ref, spikes_ref, dsyn_ref, dmem_ref):
@@ -224,6 +234,9 @@
 def step_kernel(step, last, *refs):
     (chosen_ref, arrived_ref, codes_ref, volts_ref, cur_ref, ext_ref,
      spikes_ref, dsyn_ref, dmem_ref, table_ref) = refs[:10]
+    if step == 1:
+        gather_ref, spread_ref = refs[10:12]
+        refs = refs[2:]
     volts_out, cur_out, spikes_out, out_ref = refs[10:14]
     chosen_s, blocks_ref, sems = refs[-4:-1]
     sent_ref = refs[-1]
@@ -240,7 +253,7 @@
     lax.fori_loop(0, 2, start, 0)
     if step == 1:
         arrived = arrived_ref[...]
-        codes, later = codes_of(arrived, devs)
+        codes, later = codes_of(arrived, gather_ref[...], spread_ref[...])
         refs[14][...] = later
     else:
         codes = codes_ref[...]
@@ -346,15 +359,17 @@
         return pltpu.with_memory_space_constraint(array, pltpu.HBM)
 
     long = TRIALS + EXTRA
-    out, spikes, chosen = pl.pallas_call(
+    out, spikes, chosen, *constants = pl.pallas_call(
         first_kernel,
         out_shape=(
             jax.ShapeDtypeStruct((devs * long, BLOCK), bf16),
             state,
             jax.ShapeDtypeStruct((steps, 2, 1, devs), i32),
+            jax.ShapeDtypeStruct((devs * long, devs), bf16),
+            jax.ShapeDtypeStruct((devs, devs * TRIALS), bf16),
         ),
         in_specs=[HBM] * 6,
-        out_specs=(VMEM,) * 3,
+        out_specs=(VMEM,) * 5,
         scratch_shapes=scratch
         + [
             pltpu.VMEM((steps, 1, devs), i32),
@@ -396,12 +411,14 @@
         if step == 1:
             outs.append(jax.ShapeDtypeStruct((8, devs * TRIALS), i32))
             out_specs.append(VMEM)
+        else:
+            constants = []
         if last:
             out_specs[3] = HBM
         results = pl.pallas_call(
             functools.partial(step_kernel, step, last),
             out_shape=tuple(outs),
-            in_specs=[VMEM] * 10,
+            in_specs=[VMEM] * (10 + len(constants)),
             out_specs=tuple(out_specs),
             scratch_shapes=[pltpu.SMEM((2, 1, devs), i32)]
             + blocks
@@ -411,7 +428,7 @@
             ],
             compiler_params=params(8),
             name=f"step{step}",
-        )(chosen, arrived, codes, volts, cur, ext_drive, spikes, dsyn, dmem, local_table)
+        )(chosen, arrived, codes, volts, cur, ext_drive, spikes, dsyn, dmem, local_table, *constants)
         volts, cur, spikes, out = results[:4]
         if step == 1:
             codes = results[4]

time: 95 us -> 95 us (level)
  no operation moved by 1% of the time
where the time goes in v8:
time: 95 us; the launch traced here: 94.7 us
  blocking collectives  68.5 us (72%)
  Pallas kernels  10.4 us (11%)
  starting transfers between devices  8.29 us (9%)
  waiting for transfers between devices  5.83 us (6%)
    all_to_all x4, blocking collectives, exchange(): return lax.all_to_all(out, ('area', 'local'), 0, 0, tiled=True)  68.5 us
    pallas_call x4, Pallas kernels, shards(): pl.pallas_call(functools.partial(step_kernel, step, last), out_shape=tupl...  6.07 us
    ppermute x3, starting transfers between devices, shards(): lax.ppermute(rates, 'local', [(i, (i + shift) % n_local) for i in range(n...  4.34 us
    all_to_all x1, starting transfers between devices, exchange(): return lax.all_to_all(out, ('area', 'local'), 0, 0, tiled=True)  3.95 us
    all_to_all x1, waiting for transfers between devices, exchange(): return lax.all_to_all(out, ('area', 'local'), 0, 0, tiled=True)  3.01 us
    pallas_call x1, Pallas kernels, shards(): pl.pallas_call(first_kernel, out_shape=(jax.ShapeDtypeStruct((devs * long...  2.97 us
    ppermute x3, waiting for transfers between devices, shards(): lax.ppermute(rates, 'local', [(i, (i + shift) % n_local) for i in range(n...  2.82 us
  transfers between devices with their start and end apart: 4, of which 3 were waited for; matrix products, arithmetic and copies ran while one was open for 1% of the time, Pallas kernels for 0%

profile of v8, /device:TPU:1, one launch (start us, length us, event | category | flops | bytes accessed | tf_op | source)
XLA Modules:
  0.0 94.7 jit_solution(5483890623268152801)
XLA Ops:
  0.6 3.0 %first.1 = (bf16[1280,128]{1,0:T(8,128)(2,1)S(1)}, f32[8,4096]{1,0:T(8,128)S(1)}, s32[5,2,1,128]{3,2,1,0:T(1,128)S(1)}, bf16[1280,128]{1,0:T(8,128)(2,1)S(1)}, bf16[128,1024]{1,0:T(8,128)(2,1)S(1)}) custom-call(s32[5,1,128]{2,1,0:T(1,128)} %bitcast.35, s32[2,128]{1,0:T(2,128)} %bitcast.36, s32[2,128]{1,0:T(2,128)} %bitcast.37, s32[5,1,128]{2,1,0:T(1,128)} %counts_hbm.1, ...), custom_call_target="tpu_custom_call" | custom-call | tf_op jit(solution)/shard_map/first/pallas_call | solution.py:362
  3.6 0.0 slice-start
  3.6 0.0 slice-start.1
  3.6 0.0 copy-start
  3.7 0.0 copy-start.1
  3.7 0.0 copy-start.2
  3.7 0.0 copy-start.3
  3.7 0.0 copy-start.4
  3.7 23.3 %all_to_all.25 = bf16[128,5,2,128]{3,2,1,0:T(2,128)(2,1)S(1)} all-to-all(bf16[128,5,2,128]{3,2,1,0:T(2,128)(2,1)S(1)} %bitcast.33), channel_id=1, replica_groups=mesh['area'=32,'local'=4] {'area','local'}, dimensions={0} | all-to-all | bytes 655360 | tf_op jit(solution)/shard_map/all_to_all | solution.py:356
  27.0 0.0 slice-done
  27.0 0.0 slice-done.1
  27.0 0.0 copy-done
  27.0 0.0 copy-done.1
  27.0 0.0 copy-done.2
  27.0 0.0 copy-done.3
  27.0 0.0 copy-done.4
  27.1 1.6 %step1.1 = (f32[8,4096]{1,0:T(8,128)S(1)}, f32[8,4096]{1,0:T(8,128)S(1)}, f32[8,4096]{1,0:T(8,128)S(1)}, bf16[128,8,128]{2,1,0:T(8,128)(2,1)S(1)}, s32[8,1024]{1,0:T(8,128)S(1)}) custom-call(s32[5,2,1,128]{3,2,1,0:T(1,128)S(1)} %get-tuple-element.34.refs_0_, bf16[1280,128]{1,0:T(8,128)(2,1)S(1)} %bitcast.22, s32[8,1024]{1,0:T(8,128)S(1)} %broadcast_in_dim.6.refs_2_, ...), custom_call_target="tpu_custom_call" | custom-call | tf_op jit(solution)/shard_map/step1/pallas_call | solution.py:418
  28.6 15.1 %all_to_all.26.refs_1_ = bf16[128,8,128]{2,1,0:T(8,128)(2,1)S(1)} all-to-all(bf16[128,8,128]{2,1,0:T(8,128)(2,1)S(1)} %get-tuple-element.39), channel_id=1, replica_groups=mesh['area'=32,'local'=4] {'area','local'}, dimensions={0} | all-to-all | bytes 524288 | tf_op jit(solution)/shard_map/all_to_all | solution.py:356
  43.7 1.3 %step2.1 = (f32[8,4096]{1,0:T(8,128)S(1)}, f32[8,4096]{1,0:T(8,128)S(1)}, f32[8,4096]{1,0:T(8,128)S(1)}, bf16[128,8,128]{2,1,0:T(8,128)(2,1)S(1)}) custom-call(s32[5,2,1,128]{3,2,1,0:T(1,128)S(1)} %get-tuple-element.34.refs_0_, bf16[128,8,128]{2,1,0:T(8,128)(2,1)S(1)} %all_to_all.26.refs_1_, s32[8,1024]{1,0:T(8,128)S(1)} %get-tuple-element.40.refs_2_.codes_ref, ...), custom_call_target="tpu_custom_call" | custom-call | tf_op jit(solution)/shard_map/step2/pallas_call | solution.py:418
  45.0 15.1 %all_to_all.27.refs_1_ = bf16[128,8,128]{2,1,0:T(8,128)(2,1)S(1)} all-to-all(bf16[128,8,128]{2,1,0:T(8,128)(2,1)S(1)} %get-tuple-element.44), channel_id=1, replica_groups=mesh['area'=32,'local'=4] {'area','local'}, dimensions={0} | all-to-all | bytes 524288 | tf_op jit(solution)/shard_map/all_to_all | solution.py:356
  60.1 0.0 copy-start.5
  60.1 1.3 %step3.1 = (f32[8,4096]{1,0:T(8,128)S(1)}, f32[8,4096]{1,0:T(8,128)S(1)}, f32[8,4096]{1,0:T(8,128)S(1)}, bf16[128,8,128]{2,1,0:T(8,128)(2,1)S(1)}) custom-call(s32[5,2,1,128]{3,2,1,0:T(1,128)S(1)} %get-tuple-element.34.refs_0_, bf16[128,8,128]{2,1,0:T(8,128)(2,1)S(1)} %all_to_all.27.refs_1_, s32[8,1024]{1,0:T(8,128)S(1)} %get-tuple-element.40.refs_2_.codes_ref, ...), custom_call_target="tpu_custom_call" | custom-call | tf_op jit(solution)/shard_map/step3/pallas_call | solution.py:418
  61.4 15.1 %all_to_all.28.refs_1_ = bf16[128,8,128]{2,1,0:T(8,128)(2,1)S(1)} all-to-all(bf16[128,8,128]{2,1,0:T(8,128)(2,1)S(1)} %get-tuple-element.48), channel_id=1, replica_groups=mesh['area'=32,'local'=4] {'area','local'}, dimensions={0} | all-to-all | bytes 524288 | tf_op jit(solution)/shard_map/all_to_all | solution.py:356
  76.5 1.9 %step4.1 = (f32[8,4096]{1,0:T(8,128)S(1)}, f32[8,4096]{1,0:T(8,128)S(1)}, f32[8,4096]{1,0:T(8,128)S(1)}, bf16[128,8,128]{2,1,0:T(8,128)(2,1)}) custom-call(s32[5,2,1,128]{3,2,1,0:T(1,128)S(1)} %get-tuple-element.34.refs_0_, bf16[128,8,128]{2,1,0:T(8,128)(2,1)S(1)} %all_to_all.28.refs_1_, s32[8,1024]{1,0:T(8,128)S(1)} %get-tuple-element.40.refs_2_.codes_ref, ...), custom_call_target="tpu_custom_call" | custom-call | tf_op jit(solution)/shard_map/step4/pallas_call | solution.py:418
  78.4 3.9 %all-to-all-start.4 = ((bf16[128,8,128]{2,1,0:T(8,128)(2,1)}), bf16[128,8,128]{2,1,0:T(8,128)(2,1)S(1)}, u32[]{:S(2)}, u32[]{:S(2)}) async-start(bf16[128,8,128]{2,1,0:T(8,128)(2,1)} %get-tuple-element.53), calls=%async_computation.4 | async-start | bytes 524288 | tf_op jit(solution)/shard_map/all_to_all | solution.py:356
  82.3 0.0 copy-done.5
  82.3 0.3 activity.1
  82.7 0.1 reduce_sum.9
  82.8 0.1 reshape.37
  82.9 2.6 %collective-permute-start.2 = (f32[5,8,8]{2,1,0:T(8,128)S(1)}, f32[5,8,8]{2,1,0:T(8,128)S(1)}, u32[]{:S(2)}, u32[]{:S(2)}) collective-permute-start(f32[5,8,8]{2,1,0:T(8,128)S(1)} %reshape.37), channel_id=1, source_target_pairs={{0,3},{1,0},{2,1},{3,2},{4,7},{5,4},{6,5},{7,6},{8,11},{9,8},{10,9... | collective-permute-start | bytes 3848 | tf_op jit(solution)/shard_map/ppermute | solution.py:451
  85.5 0.0 collective-permute-start.1
  85.5 1.8 %collective-permute-start = (f32[5,8,8]{2,1,0:T(8,128)S(1)}, f32[5,8,8]{2,1,0:T(8,128)S(1)}, u32[]{:S(2)}, u32[]{:S(2)}) collective-permute-start(f32[5,8,8]{2,1,0:T(8,128)S(1)} %reshape.37), channel_id=1, source_target_pairs={{0,2},{1,3},{2,0},{3,1},{4,6},{5,7},{6,4},{7,5},{8,10},{9,11},{10,... | collective-permute-start | bytes 3848 | tf_op jit(solution)/shard_map/ppermute | solution.py:451
  87.2 0.0 collective-permute-done.2
  87.2 2.4 %collective-permute-done.1 = f32[5,8,8]{2,1,0:T(8,128)S(1)} collective-permute-done((f32[5,8,8]{2,1,0:T(8,128)S(1)}, f32[5,8,8]{2,1,0:T(8,128)S(1)}, u32[]{:S(2)}, u32[]{:S(2)}) %collective-permute-start.1) | collective-permute-done | bytes 1312 | tf_op jit(solution)/shard_map/ppermute | solution.py:451
  89.6 0.4 collective-permute-done
  90.1 0.6 multiply_bitcast_fusion
  90.7 3.0 %all-to-all-done.4.arrived_ref = bf16[128,8,128]{2,1,0:T(8,128)(2,1)S(1)} async-done(((bf16[128,8,128]{2,1,0:T(8,128)(2,1)}), bf16[128,8,128]{2,1,0:T(8,128)(2,1)S(1)}, u32[]{:S(2)}, u32[]{:S(2)}) %all-to-all-start.4) | async-done | bytes 262176 | tf_op jit(solution)/shard_map/all_to_all | solution.py:356
  93.7 1.0 %last.1 = (f32[8,4096]{1,0:T(8,128)}, f32[8,4096]{1,0:T(8,128)}) custom-call(bf16[128,8,128]{2,1,0:T(8,128)(2,1)S(1)} %all-to-all-done.4.arrived_ref, s32[8,1024]{1,0:T(8,128)S(1)} %get-tuple-element.40.refs_2_.codes_ref, f32[8,4096]{1,0:T(8,128)S(1)} %get-tuple-element.54.volts_ref, f32[8,4096]{1,0:T(8,128)S(1)} %get-tuple-element.55.cur_ref, ...), custom_call_target="tpu_custom_call" | custom-call | tf_op jit(solution)/shard_map/last/pallas_call | solution.py:456
  (4 shorter events, 0.0 us)
Async XLA Ops:
  3.6 23.4 %slice-start = ((s8[8388608]{0:T(1024)(128)(4,1)}), s8[4194304]{0:T(1024)(128)(4,1)S(1)}, s32[]{:S(2)}) async-start(s8[8388608]{0:T(1024)(128)(4,1)} %bitcast.16), calls=%async_computation.5 | async-start | bytes 8388608
  3.6 23.4 %slice-start.1 = ((s8[8388608]{0:T(1024)(128)(4,1)}), s8[4194304]{0:T(1024)(128)(4,1)S(1)}, s32[]{:S(2)}) async-start(s8[8388608]{0:T(1024)(128)(4,1)} %bitcast.16), calls=%async_computation.6 | async-start | bytes 8388608
  3.6 23.3 %copy-start = (f32[8,4096]{1,0:T(8,128)S(1)}, f32[8,4096]{1,0:T(8,128)}, u32[]{:S(2)}) copy-start(f32[8,4096]{1,0:T(8,128)} %ext_ref.1) | copy-start | bytes 393220
  3.7 23.3 %copy-start.1 = (f32[8,4096]{1,0:T(8,128)S(1)}, f32[8,4096]{1,0:T(8,128)}, u32[]{:S(2)}) copy-start(f32[8,4096]{1,0:T(8,128)} %refs_3_.1) | copy-start | bytes 393220
  3.7 23.3 %copy-start.2 = (f32[4096]{0:T(1024)S(1)}, f32[4096]{0:T(1024)}, u32[]{:S(2)}) copy-start(f32[4096]{0:T(1024)} %param.14) | copy-start | bytes 49156
  3.7 23.3 %copy-start.3 = (f32[4096]{0:T(1024)S(1)}, f32[4096]{0:T(1024)}, u32[]{:S(2)}) copy-start(f32[4096]{0:T(1024)} %param.15) | copy-start | bytes 49156
  3.7 23.3 %copy-start.4 = (f32[8,4096]{1,0:T(8,128)S(1)}, f32[8,4096]{1,0:T(8,128)}, u32[]{:S(2)}) copy-start(f32[8,4096]{1,0:T(8,128)} %refs_4_.1) | copy-start | bytes 393220
  60.1 22.3 %copy-start.5 = (s32[32]{0:T(128)S(1)}, s32[32]{0:T(128)}, u32[]{:S(2)}) copy-start(s32[32]{0:T(128)} %param.19) | copy-start | bytes 388
  78.4 15.3 %all-to-all-start.4 = ((bf16[128,8,128]{2,1,0:T(8,128)(2,1)}), bf16[128,8,128]{2,1,0:T(8,128)(2,1)S(1)}, u32[]{:S(2)}, u32[]{:S(2)}) async-start(bf16[128,8,128]{2,1,0:T(8,128)(2,1)} %get-tuple-element.53), calls=%async_computation.4 | async-start | bytes 524288 | tf_op jit(solution)/shard_map/all_to_all | solution.py:356
  82.9 4.3 %collective-permute-start.2 = (f32[5,8,8]{2,1,0:T(8,128)S(1)}, f32[5,8,8]{2,1,0:T(8,128)S(1)}, u32[]{:S(2)}, u32[]{:S(2)}) collective-permute-start(f32[5,8,8]{2,1,0:T(8,128)S(1)} %reshape.37), channel_id=1, source_target_pairs={{0,3},{1,0},{2,1},{3,2},{4,7},{5,4},{6,5},{7,6},{8,11},{9,8},{10,9... | collective-permute-start | bytes 3848 | tf_op jit(solution)/shard_map/ppermute | solution.py:451
  85.5 4.1 %collective-permute-start.1 = (f32[5,8,8]{2,1,0:T(8,128)S(1)}, f32[5,8,8]{2,1,0:T(8,128)S(1)}, u32[]{:S(2)}, u32[]{:S(2)}) collective-permute-start(f32[5,8,8]{2,1,0:T(8,128)S(1)} %reshape.37), channel_id=1, source_target_pairs={{0,1},{1,2},{2,3},{3,0},{4,5},{5,6},{6,7},{7,4},{8,9},{9,10},{10,1... | collective-permute-start | bytes 3848 | tf_op jit(solution)/shard_map/ppermute | solution.py:451
  85.5 4.6 %collective-permute-start = (f32[5,8,8]{2,1,0:T(8,128)S(1)}, f32[5,8,8]{2,1,0:T(8,128)S(1)}, u32[]{:S(2)}, u32[]{:S(2)}) collective-permute-start(f32[5,8,8]{2,1,0:T(8,128)S(1)} %reshape.37), channel_id=1, source_target_pairs={{0,2},{1,3},{2,0},{3,1},{4,6},{5,7},{6,4},{7,5},{8,10},{9,11},{10,... | collective-permute-start | bytes 3848 | tf_op jit(solution)/shard_map/ppermute | solution.py:451

commit v9 on v8

--- a/solution.py
+++ b/solution.py
@@ -12,6 +12,8 @@
 TRIALS = 8
 NO_BLOCK = 64
 EXTRA = 2
+EARLY = 32
+HALVES = 2
 PIECES = 4
 CHUNK = 32
 WHOLE = 32
@@ -268,10 +270,14 @@
         spikes = spike_of(volts)
         spikes_out[:, lanes(b)] = spikes
         blocks_ref[b] = spikes.astype(jnp.bfloat16)
-    to_smem(0).wait()
-    to_smem(1).wait()
+    tile_row, block_row = chosen_ref[step, 0], chosen_ref[step, 1]
 
     def pick(d):
+        if d < EARLY:
+            return block_row[0, d], tile_row[0, d]
+        if d == EARLY:
+            to_smem(0).wait()
+            to_smem(1).wait()
         return chosen_s[1, 0, d], chosen_s[0, 0, d]
 
     if not last:
@@ -306,17 +312,26 @@
 
 
 def last_kernel(step, arrived_ref, codes_ref, volts_ref, cur_ref, ext_ref, spikes_ref,
-                dsyn_ref, dmem_ref, volts_out, cur_out):
+                dsyn_ref, dmem_ref, volts_hbm, cur_hbm, volts_out, cur_out, sems):
     devs = arrived_ref.shape[0]
     count = dsyn_ref.shape[0]
     arrived = arrived_ref[...].reshape(devs * TRIALS, BLOCK)
     inflow = inflow_of(codes_ref[step - 1 : step, :], arrived, count * TRIALS)
-    for b in range(count):
-        volts, cur = update(
-            b, inflow, volts_ref, cur_ref, ext_ref, spikes_ref, dsyn_ref, dmem_ref
-        )
-        volts_out[:, lanes(b)] = volts
-        cur_out[:, lanes(b)] = cur
+    size = count // HALVES
+    copies = []
+    for c in range(HALVES):
+        for b in range(c * size, (c + 1) * size):
+            volts, cur = update(
+                b, inflow, volts_ref, cur_ref, ext_ref, spikes_ref, dsyn_ref, dmem_ref
+            )
+            volts_out[:, lanes(b)] = volts
+            cur_out[:, lanes(b)] = cur
+        at = pl.ds(c * size * BLOCK, size * BLOCK)
+        for i, (here, there) in enumerate(((volts_out, volts_hbm), (cur_out, cur_hbm))):
+            copies.append(pltpu.make_async_copy(here.at[:, at], there.at[:, at], sems.at[2 * c + i]))
+            copies[-1].start()
+    for copy in copies:
+        copy.wait()
 
 
 def shards(
@@ -457,7 +472,12 @@
         functools.partial(last_kernel, steps),
         out_shape=(state, state),
         in_specs=[VMEM] * 8,
-        out_specs=(VMEM, VMEM),
+        out_specs=(HBM, HBM),
+        scratch_shapes=[
+            pltpu.VMEM(state.shape, f32),
+            pltpu.VMEM(state.shape, f32),
+            pltpu.SemaphoreType.DMA((2 * HALVES,)),
+        ],
         compiler_params=params(8),
         name="last",
     )(arrived, codes, volts, cur, ext_drive, spikes, dsyn, dmem)

time: 95 us -> 94.9 us (level)
  no operation moved by 1% of the time
where the time goes in v9:
time: 94.9 us; the launch traced here: 94.6 us
  blocking collectives  68.5 us (72%)
  Pallas kernels  10.3 us (11%)
  starting transfers between devices  8.29 us (9%)
  waiting for transfers between devices  5.83 us (6%)
    all_to_all x4, blocking collectives, exchange(): return lax.all_to_all(out, ('area', 'local'), 0, 0, tiled=True)  68.5 us
    pallas_call x4, Pallas kernels, shards(): pl.pallas_call(functools.partial(step_kernel, step, last), out_shape=tupl...  5.96 us
    ppermute x3, starting transfers between devices, shards(): lax.ppermute(rates, 'local', [(i, (i + shift) % n_local) for i in range(n...  4.34 us
    all_to_all x1, starting transfers between devices, exchange(): return lax.all_to_all(out, ('area', 'local'), 0, 0, tiled=True)  3.95 us
    all_to_all x1, waiting for transfers between devices, exchange(): return lax.all_to_all(out, ('area', 'local'), 0, 0, tiled=True)  3.02 us
    pallas_call x1, Pallas kernels, shards(): pl.pallas_call(first_kernel, out_shape=(jax.ShapeDtypeStruct((devs * long...  2.98 us
    ppermute x3, waiting for transfers between devices, shards(): lax.ppermute(rates, 'local', [(i, (i + shift) % n_local) for i in range(n...  2.81 us
  transfers between devices with their start and end apart: 4, of which 3 were waited for; matrix products, arithmetic and copies ran while one was open for 1% of the time, Pallas kernels for 0%

profile of v9, /device:TPU:1, one launch (start us, length us, event | category | flops | bytes accessed | tf_op | source)
XLA Modules:
  0.0 94.6 jit_solution(7593924318620308277)
XLA Ops:
  0.6 3.0 %first.1 = (bf16[1280,128]{1,0:T(8,128)(2,1)S(1)}, f32[8,4096]{1,0:T(8,128)S(1)}, s32[5,2,1,128]{3,2,1,0:T(1,128)S(1)}, bf16[1280,128]{1,0:T(8,128)(2,1)S(1)}, bf16[128,1024]{1,0:T(8,128)(2,1)S(1)}) custom-call(s32[5,1,128]{2,1,0:T(1,128)} %bitcast.35, s32[2,128]{1,0:T(2,128)} %bitcast.36, s32[2,128]{1,0:T(2,128)} %bitcast.37, s32[5,1,128]{2,1,0:T(1,128)} %counts_hbm.1, ...), custom_call_target="tpu_custom_call" | custom-call | tf_op jit(solution)/shard_map/first/pallas_call | solution.py:377
  3.6 0.0 slice-start
  3.6 0.0 slice-start.1
  3.7 0.0 copy-start
  3.7 0.0 copy-start.1
  3.7 0.0 copy-start.2
  3.7 0.0 copy-start.3
  3.7 0.0 copy-start.4
  3.7 23.3 %all_to_all.25 = bf16[128,5,2,128]{3,2,1,0:T(2,128)(2,1)S(1)} all-to-all(bf16[128,5,2,128]{3,2,1,0:T(2,128)(2,1)S(1)} %bitcast.33), channel_id=1, replica_groups=mesh['area'=32,'local'=4] {'area','local'}, dimensions={0} | all-to-all | bytes 655360 | tf_op jit(solution)/shard_map/all_to_all | solution.py:371
  27.0 0.0 slice-done
  27.0 0.0 slice-done.1
  27.0 0.0 copy-done
  27.0 0.0 copy-done.1
  27.0 0.0 copy-done.2
  27.0 0.0 copy-done.3
  27.0 0.0 copy-done.4
  27.1 1.7 %step1.1 = (f32[8,4096]{1,0:T(8,128)S(1)}, f32[8,4096]{1,0:T(8,128)S(1)}, f32[8,4096]{1,0:T(8,128)S(1)}, bf16[128,8,128]{2,1,0:T(8,128)(2,1)S(1)}, s32[8,1024]{1,0:T(8,128)S(1)}) custom-call(s32[5,2,1,128]{3,2,1,0:T(1,128)S(1)} %get-tuple-element.34.refs_0_, bf16[1280,128]{1,0:T(8,128)(2,1)S(1)} %bitcast.22, s32[8,1024]{1,0:T(8,128)S(1)} %broadcast_in_dim.6.refs_2_, ...), custom_call_target="tpu_custom_call" | custom-call | tf_op jit(solution)/shard_map/step1/pallas_call | solution.py:433
  28.8 15.1 %all_to_all.26.refs_1_ = bf16[128,8,128]{2,1,0:T(8,128)(2,1)S(1)} all-to-all(bf16[128,8,128]{2,1,0:T(8,128)(2,1)S(1)} %get-tuple-element.39), channel_id=1, replica_groups=mesh['area'=32,'local'=4] {'area','local'}, dimensions={0} | all-to-all | bytes 524288 | tf_op jit(solution)/shard_map/all_to_all | solution.py:371
  43.8 1.2 %step2.1 = (f32[8,4096]{1,0:T(8,128)S(1)}, f32[8,4096]{1,0:T(8,128)S(1)}, f32[8,4096]{1,0:T(8,128)S(1)}, bf16[128,8,128]{2,1,0:T(8,128)(2,1)S(1)}) custom-call(s32[5,2,1,128]{3,2,1,0:T(1,128)S(1)} %get-tuple-element.34.refs_0_, bf16[128,8,128]{2,1,0:T(8,128)(2,1)S(1)} %all_to_all.26.refs_1_, s32[8,1024]{1,0:T(8,128)S(1)} %get-tuple-element.40.refs_2_.codes_ref, ...), custom_call_target="tpu_custom_call" | custom-call | tf_op jit(solution)/shard_map/step2/pallas_call | solution.py:433
  45.1 15.1 %all_to_all.27.refs_1_ = bf16[128,8,128]{2,1,0:T(8,128)(2,1)S(1)} all-to-all(bf16[128,8,128]{2,1,0:T(8,128)(2,1)S(1)} %get-tuple-element.44), channel_id=1, replica_groups=mesh['area'=32,'local'=4] {'area','local'}, dimensions={0} | all-to-all | bytes 524288 | tf_op jit(solution)/shard_map/all_to_all | solution.py:371
  60.1 0.0 copy-start.5
  60.1 1.2 %step3.1 = (f32[8,4096]{1,0:T(8,128)S(1)}, f32[8,4096]{1,0:T(8,128)S(1)}, f32[8,4096]{1,0:T(8,128)S(1)}, bf16[128,8,128]{2,1,0:T(8,128)(2,1)S(1)}) custom-call(s32[5,2,1,128]{3,2,1,0:T(1,128)S(1)} %get-tuple-element.34.refs_0_, bf16[128,8,128]{2,1,0:T(8,128)(2,1)S(1)} %all_to_all.27.refs_1_, s32[8,1024]{1,0:T(8,128)S(1)} %get-tuple-element.40.refs_2_.codes_ref, ...), custom_call_target="tpu_custom_call" | custom-call | tf_op jit(solution)/shard_map/step3/pallas_call | solution.py:433
  61.4 15.1 %all_to_all.28.refs_1_ = bf16[128,8,128]{2,1,0:T(8,128)(2,1)S(1)} all-to-all(bf16[128,8,128]{2,1,0:T(8,128)(2,1)S(1)} %get-tuple-element.48), channel_id=1, replica_groups=mesh['area'=32,'local'=4] {'area','local'}, dimensions={0} | all-to-all | bytes 524288 | tf_op jit(solution)/shard_map/all_to_all | solution.py:371
  76.4 1.8 %step4.1 = (f32[8,4096]{1,0:T(8,128)S(1)}, f32[8,4096]{1,0:T(8,128)S(1)}, f32[8,4096]{1,0:T(8,128)S(1)}, bf16[128,8,128]{2,1,0:T(8,128)(2,1)}) custom-call(s32[5,2,1,128]{3,2,1,0:T(1,128)S(1)} %get-tuple-element.34.refs_0_, bf16[128,8,128]{2,1,0:T(8,128)(2,1)S(1)} %all_to_all.28.refs_1_, s32[8,1024]{1,0:T(8,128)S(1)} %get-tuple-element.40.refs_2_.codes_ref, ...), custom_call_target="tpu_custom_call" | custom-call | tf_op jit(solution)/shard_map/step4/pallas_call | solution.py:433
  78.3 3.9 %all-to-all-start.4 = ((bf16[128,8,128]{2,1,0:T(8,128)(2,1)}), bf16[128,8,128]{2,1,0:T(8,128)(2,1)S(1)}, u32[]{:S(2)}, u32[]{:S(2)}) async-start(bf16[128,8,128]{2,1,0:T(8,128)(2,1)} %get-tuple-element.53), calls=%async_computation.4 | async-start | bytes 524288 | tf_op jit(solution)/shard_map/all_to_all | solution.py:371
  82.2 0.0 copy-done.5
  82.2 0.3 activity.1
  82.6 0.1 reduce_sum.9
  82.7 0.1 reshape.37
  82.8 2.6 %collective-permute-start.2 = (f32[5,8,8]{2,1,0:T(8,128)S(1)}, f32[5,8,8]{2,1,0:T(8,128)S(1)}, u32[]{:S(2)}, u32[]{:S(2)}) collective-permute-start(f32[5,8,8]{2,1,0:T(8,128)S(1)} %reshape.37), channel_id=1, source_target_pairs={{0,3},{1,0},{2,1},{3,2},{4,7},{5,4},{6,5},{7,6},{8,11},{9,8},{10,9... | collective-permute-start | bytes 3848 | tf_op jit(solution)/shard_map/ppermute | solution.py:466
  85.4 0.0 collective-permute-start.1
  85.4 1.8 %collective-permute-start = (f32[5,8,8]{2,1,0:T(8,128)S(1)}, f32[5,8,8]{2,1,0:T(8,128)S(1)}, u32[]{:S(2)}, u32[]{:S(2)}) collective-permute-start(f32[5,8,8]{2,1,0:T(8,128)S(1)} %reshape.37), channel_id=1, source_target_pairs={{0,2},{1,3},{2,0},{3,1},{4,6},{5,7},{6,4},{7,5},{8,10},{9,11},{10,... | collective-permute-start | bytes 3848 | tf_op jit(solution)/shard_map/ppermute | solution.py:466
  87.1 0.0 collective-permute-done.2
  87.1 2.4 %collective-permute-done.1 = f32[5,8,8]{2,1,0:T(8,128)S(1)} collective-permute-done((f32[5,8,8]{2,1,0:T(8,128)S(1)}, f32[5,8,8]{2,1,0:T(8,128)S(1)}, u32[]{:S(2)}, u32[]{:S(2)}) %collective-permute-start.1) | collective-permute-done | bytes 1312 | tf_op jit(solution)/shard_map/ppermute | solution.py:466
  89.5 0.4 collective-permute-done
  89.9 0.6 multiply_bitcast_fusion
  90.6 3.0 %all-to-all-done.4.arrived_ref = bf16[128,8,128]{2,1,0:T(8,128)(2,1)S(1)} async-done(((bf16[128,8,128]{2,1,0:T(8,128)(2,1)}), bf16[128,8,128]{2,1,0:T(8,128)(2,1)S(1)}, u32[]{:S(2)}, u32[]{:S(2)}) %all-to-all-start.4) | async-done | bytes 262176 | tf_op jit(solution)/shard_map/all_to_all | solution.py:371
  93.6 1.0 %last.1 = (f32[8,4096]{1,0:T(8,128)}, f32[8,4096]{1,0:T(8,128)}) custom-call(bf16[128,8,128]{2,1,0:T(8,128)(2,1)S(1)} %all-to-all-done.4.arrived_ref, s32[8,1024]{1,0:T(8,128)S(1)} %get-tuple-element.40.refs_2_.codes_ref, f32[8,4096]{1,0:T(8,128)S(1)} %get-tuple-element.54.volts_ref, f32[8,4096]{1,0:T(8,128)S(1)} %get-tuple-element.55.cur_ref, ...), custom_call_target="tpu_custom_call" | custom-call | tf_op jit(solution)/shard_map/last/pallas_call | solution.py:471
  (4 shorter events, 0.0 us)
Async XLA Ops:
  3.6 23.4 %slice-start = ((s8[8388608]{0:T(1024)(128)(4,1)}), s8[4194304]{0:T(1024)(128)(4,1)S(1)}, s32[]{:S(2)}) async-start(s8[8388608]{0:T(1024)(128)(4,1)} %bitcast.16), calls=%async_computation.5 | async-start | bytes 8388608
  3.6 23.4 %slice-start.1 = ((s8[8388608]{0:T(1024)(128)(4,1)}), s8[4194304]{0:T(1024)(128)(4,1)S(1)}, s32[]{:S(2)}) async-start(s8[8388608]{0:T(1024)(128)(4,1)} %bitcast.16), calls=%async_computation.6 | async-start | bytes 8388608
  3.7 23.3 %copy-start = (f32[8,4096]{1,0:T(8,128)S(1)}, f32[8,4096]{1,0:T(8,128)}, u32[]{:S(2)}) copy-start(f32[8,4096]{1,0:T(8,128)} %ext_ref.1) | copy-start | bytes 393220
  3.7 23.3 %copy-start.1 = (f32[8,4096]{1,0:T(8,128)S(1)}, f32[8,4096]{1,0:T(8,128)}, u32[]{:S(2)}) copy-start(f32[8,4096]{1,0:T(8,128)} %refs_3_.1) | copy-start | bytes 393220
  3.7 23.3 %copy-start.2 = (f32[4096]{0:T(1024)S(1)}, f32[4096]{0:T(1024)}, u32[]{:S(2)}) copy-start(f32[4096]{0:T(1024)} %param.14) | copy-start | bytes 49156
  3.7 23.3 %copy-start.3 = (f32[4096]{0:T(1024)S(1)}, f32[4096]{0:T(1024)}, u32[]{:S(2)}) copy-start(f32[4096]{0:T(1024)} %param.15) | copy-start | bytes 49156
  3.7 23.3 %copy-start.4 = (f32[8,4096]{1,0:T(8,128)S(1)}, f32[8,4096]{1,0:T(8,128)}, u32[]{:S(2)}) copy-start(f32[8,4096]{1,0:T(8,128)} %refs_4_.1) | copy-start | bytes 393220
  60.1 22.1 %copy-start.5 = (s32[32]{0:T(128)S(1)}, s32[32]{0:T(128)}, u32[]{:S(2)}) copy-start(s32[32]{0:T(128)} %param.19) | copy-start | bytes 388
  78.3 15.3 %all-to-all-start.4 = ((bf16[128,8,128]{2,1,0:T(8,128)(2,1)}), bf16[128,8,128]{2,1,0:T(8,128)(2,1)S(1)}, u32[]{:S(2)}, u32[]{:S(2)}) async-start(bf16[128,8,128]{2,1,0:T(8,128)(2,1)} %get-tuple-element.53), calls=%async_computation.4 | async-start | bytes 524288 | tf_op jit(solution)/shard_map/all_to_all | solution.py:371
  82.8 4.3 %collective-permute-start.2 = (f32[5,8,8]{2,1,0:T(8,128)S(1)}, f32[5,8,8]{2,1,0:T(8,128)S(1)}, u32[]{:S(2)}, u32[]{:S(2)}) collective-permute-start(f32[5,8,8]{2,1,0:T(8,128)S(1)} %reshape.37), channel_id=1, source_target_pairs={{0,3},{1,0},{2,1},{3,2},{4,7},{5,4},{6,5},{7,6},{8,11},{9,8},{10,9... | collective-permute-start | bytes 3848 | tf_op jit(solution)/shard_map/ppermute | solution.py:466
  85.4 4.1 %collective-permute-start.1 = (f32[5,8,8]{2,1,0:T(8,128)S(1)}, f32[5,8,8]{2,1,0:T(8,128)S(1)}, u32[]{:S(2)}, u32[]{:S(2)}) collective-permute-start(f32[5,8,8]{2,1,0:T(8,128)S(1)} %reshape.37), channel_id=1, source_target_pairs={{0,1},{1,2},{2,3},{3,0},{4,5},{5,6},{6,7},{7,4},{8,9},{9,10},{10,1... | collective-permute-start | bytes 3848 | tf_op jit(solution)/shard_map/ppermute | solution.py:466
  85.4 4.6 %collective-permute-start = (f32[5,8,8]{2,1,0:T(8,128)S(1)}, f32[5,8,8]{2,1,0:T(8,128)S(1)}, u32[]{:S(2)}, u32[]{:S(2)}) collective-permute-start(f32[5,8,8]{2,1,0:T(8,128)S(1)} %reshape.37), channel_id=1, source_target_pairs={{0,2},{1,3},{2,0},{3,1},{4,6},{5,7},{6,4},{7,5},{8,10},{9,11},{10,... | collective-permute-start | bytes 3848 | tf_op jit(solution)/shard_map/ppermute | solution.py:466

commit v10 on v9

--- a/solution.py
+++ b/solution.py
@@ -15,6 +15,7 @@
 EARLY = 32
 HALVES = 2
 PIECES = 4
+PART = 16
 CHUNK = 32
 WHOLE = 32
 
@@ -113,14 +114,14 @@
     base = WHOLE * tpt - WHOLE
 
     def start_routed(c, carry):
-        for j in range(CHUNK):
-            d = WHOLE + c * CHUNK + j
+        for j in range(PART):
+            d = WHOLE + c * PART + j
             pltpu.make_async_copy(
                 table_hbm.at[d * tpt + route_s[0, 0, d]], tiles_ref.at[base + d], routed_sems.at[c]
             ).start()
         return carry
 
-    lax.fori_loop(0, (devs - WHOLE) // CHUNK, start_routed, 0)
+    lax.fori_loop(0, (devs - WHOLE) // PART, start_routed, 0)
     for copy in copies[3:7]:
         copy.wait()
 
@@ -169,12 +170,15 @@
     for c in range(WHOLE // CHUNK):
         whole(c).wait()
         send_tiles(c * CHUNK, (c + 1) * CHUNK, pick_whole, blocks_ref, tiles_ref, store)
-    for c in range((devs - WHOLE) // CHUNK):
-        at = WHOLE + c * CHUNK
-        pltpu.make_async_copy(
-            table_hbm.at[pl.ds(0, CHUNK)], tiles_ref.at[pl.ds(base + at, CHUNK)], routed_sems.at[c]
-        ).wait()
-        send_tiles(at, at + CHUNK, pick_routed, blocks_ref, tiles_ref, store)
+    at = WHOLE
+    while at < devs:
+        size = CHUNK if at + CHUNK < devs else PART
+        for c in range((at - WHOLE) // PART, (at - WHOLE + size) // PART):
+            pltpu.make_async_copy(
+                table_hbm.at[pl.ds(0, PART)], tiles_ref.at[pl.ds(base + WHOLE + c * PART, PART)], routed_sems.at[c]
+            ).wait()
+        send_tiles(at, at + size, pick_routed, blocks_ref, tiles_ref, store)
+        at += size
 
 
 def gate_kernel(message_ref, out_ref):
@@ -271,11 +275,12 @@
         spikes_out[:, lanes(b)] = spikes
         blocks_ref[b] = spikes.astype(jnp.bfloat16)
     tile_row, block_row = chosen_ref[step, 0], chosen_ref[step, 1]
+    early = EARLY if step > 1 else 0
 
     def pick(d):
-        if d < EARLY:
+        if d < early:
             return block_row[0, d], tile_row[0, d]
-        if d == EARLY:
+        if d == early:
             to_smem(0).wait()
             to_smem(1).wait()
         return chosen_s[1, 0, d], chosen_s[0, 0, d]
@@ -398,7 +403,7 @@
         + [
             pltpu.SemaphoreType.DMA((7,)),
             pltpu.SemaphoreType.DMA((WHOLE // CHUNK,)),
-            pltpu.SemaphoreType.DMA(((devs - WHOLE) // CHUNK,)),
+            pltpu.SemaphoreType.DMA(((devs - WHOLE) // PART,)),
         ],
         compiler_params=params(16),
         name="first",

time: 94.9 us -> 94.8 us (level)
  no operation moved by 1% of the time
where the time goes in v10:
time: 94.8 us; the launch traced here: 94.5 us
  blocking collectives  68.5 us (72%)
  Pallas kernels  10.2 us (11%)
  starting transfers between devices  8.29 us (9%)
  waiting for transfers between devices  5.83 us (6%)
    all_to_all x4, blocking collectives, exchange(): return lax.all_to_all(out, ('area', 'local'), 0, 0, tiled=True)  68.5 us
    pallas_call x4, Pallas kernels, shards(): pl.pallas_call(functools.partial(step_kernel, step, last), out_shape=tupl...  5.82 us
    ppermute x3, starting transfers between devices, shards(): lax.ppermute(rates, 'local', [(i, (i + shift) % n_local) for i in range(n...  4.34 us
    all_to_all x1, starting transfers between devices, exchange(): return lax.all_to_all(out, ('area', 'local'), 0, 0, tiled=True)  3.95 us
    pallas_call x1, Pallas kernels, shards(): pl.pallas_call(first_kernel, out_shape=(jax.ShapeDtypeStruct((devs * long...  3.07 us
    all_to_all x1, waiting for transfers between devices, exchange(): return lax.all_to_all(out, ('area', 'local'), 0, 0, tiled=True)  3.01 us
    ppermute x3, waiting for transfers between devices, shards(): lax.ppermute(rates, 'local', [(i, (i + shift) % n_local) for i in range(n...  2.81 us
  transfers between devices with their start and end apart: 4, of which 3 were waited for; matrix products, arithmetic and copies ran while one was open for 1% of the time, Pallas kernels for 0%

profile of v10, /device:TPU:1, one launch (start us, length us, event | category | flops | bytes accessed | tf_op | source)
XLA Modules:
  0.0 94.5 jit_solution(3121971358201626348)
XLA Ops:
  0.6 3.1 %first.1 = (bf16[1280,128]{1,0:T(8,128)(2,1)S(1)}, f32[8,4096]{1,0:T(8,128)S(1)}, s32[5,2,1,128]{3,2,1,0:T(1,128)S(1)}, bf16[1280,128]{1,0:T(8,128)(2,1)S(1)}, bf16[128,1024]{1,0:T(8,128)(2,1)S(1)}) custom-call(s32[5,1,128]{2,1,0:T(1,128)} %bitcast.35, s32[2,128]{1,0:T(2,128)} %bitcast.36, s32[2,128]{1,0:T(2,128)} %bitcast.37, s32[5,1,128]{2,1,0:T(1,128)} %counts_hbm.1, ...), custom_call_target="tpu_custom_call" | custom-call | tf_op jit(solution)/shard_map/first/pallas_call | solution.py:382
  3.7 0.0 slice-start
  3.7 0.0 slice-start.1
  3.7 0.0 copy-start
  3.8 0.0 copy-start.1
  3.8 0.0 copy-start.2
  3.8 0.0 copy-start.3
  3.8 0.0 copy-start.4
  3.8 23.3 %all_to_all.25 = bf16[128,5,2,128]{3,2,1,0:T(2,128)(2,1)S(1)} all-to-all(bf16[128,5,2,128]{3,2,1,0:T(2,128)(2,1)S(1)} %bitcast.33), channel_id=1, replica_groups=mesh['area'=32,'local'=4] {'area','local'}, dimensions={0} | all-to-all | bytes 655360 | tf_op jit(solution)/shard_map/all_to_all | solution.py:376
  27.1 0.0 slice-done
  27.1 0.0 slice-done.1
  27.1 0.0 copy-done
  27.1 0.0 copy-done.1
  27.1 0.0 copy-done.2
  27.1 0.0 copy-done.3
  27.1 0.0 copy-done.4
  27.1 1.6 %step1.1 = (f32[8,4096]{1,0:T(8,128)S(1)}, f32[8,4096]{1,0:T(8,128)S(1)}, f32[8,4096]{1,0:T(8,128)S(1)}, bf16[128,8,128]{2,1,0:T(8,128)(2,1)S(1)}, s32[8,1024]{1,0:T(8,128)S(1)}) custom-call(s32[5,2,1,128]{3,2,1,0:T(1,128)S(1)} %get-tuple-element.34.refs_0_, bf16[1280,128]{1,0:T(8,128)(2,1)S(1)} %bitcast.22, s32[8,1024]{1,0:T(8,128)S(1)} %broadcast_in_dim.6.refs_2_, ...), custom_call_target="tpu_custom_call" | custom-call | tf_op jit(solution)/shard_map/step1/pallas_call | solution.py:438
  28.7 15.1 %all_to_all.26.refs_1_ = bf16[128,8,128]{2,1,0:T(8,128)(2,1)S(1)} all-to-all(bf16[128,8,128]{2,1,0:T(8,128)(2,1)S(1)} %get-tuple-element.39), channel_id=1, replica_groups=mesh['area'=32,'local'=4] {'area','local'}, dimensions={0} | all-to-all | bytes 524288 | tf_op jit(solution)/shard_map/all_to_all | solution.py:376
  43.8 1.2 %step2.1 = (f32[8,4096]{1,0:T(8,128)S(1)}, f32[8,4096]{1,0:T(8,128)S(1)}, f32[8,4096]{1,0:T(8,128)S(1)}, bf16[128,8,128]{2,1,0:T(8,128)(2,1)S(1)}) custom-call(s32[5,2,1,128]{3,2,1,0:T(1,128)S(1)} %get-tuple-element.34.refs_0_, bf16[128,8,128]{2,1,0:T(8,128)(2,1)S(1)} %all_to_all.26.refs_1_, s32[8,1024]{1,0:T(8,128)S(1)} %get-tuple-element.40.refs_2_.codes_ref, ...), custom_call_target="tpu_custom_call" | custom-call | tf_op jit(solution)/shard_map/step2/pallas_call | solution.py:438
  45.0 15.1 %all_to_all.27.refs_1_ = bf16[128,8,128]{2,1,0:T(8,128)(2,1)S(1)} all-to-all(bf16[128,8,128]{2,1,0:T(8,128)(2,1)S(1)} %get-tuple-element.44), channel_id=1, replica_groups=mesh['area'=32,'local'=4] {'area','local'}, dimensions={0} | all-to-all | bytes 524288 | tf_op jit(solution)/shard_map/all_to_all | solution.py:376
  60.1 0.0 copy-start.5
  60.1 1.2 %step3.1 = (f32[8,4096]{1,0:T(8,128)S(1)}, f32[8,4096]{1,0:T(8,128)S(1)}, f32[8,4096]{1,0:T(8,128)S(1)}, bf16[128,8,128]{2,1,0:T(8,128)(2,1)S(1)}) custom-call(s32[5,2,1,128]{3,2,1,0:T(1,128)S(1)} %get-tuple-element.34.refs_0_, bf16[128,8,128]{2,1,0:T(8,128)(2,1)S(1)} %all_to_all.27.refs_1_, s32[8,1024]{1,0:T(8,128)S(1)} %get-tuple-element.40.refs_2_.codes_ref, ...), custom_call_target="tpu_custom_call" | custom-call | tf_op jit(solution)/shard_map/step3/pallas_call | solution.py:438
  61.3 15.1 %all_to_all.28.refs_1_ = bf16[128,8,128]{2,1,0:T(8,128)(2,1)S(1)} all-to-all(bf16[128,8,128]{2,1,0:T(8,128)(2,1)S(1)} %get-tuple-element.48), channel_id=1, replica_groups=mesh['area'=32,'local'=4] {'area','local'}, dimensions={0} | all-to-all | bytes 524288 | tf_op jit(solution)/shard_map/all_to_all | solution.py:376
  76.4 1.8 %step4.1 = (f32[8,4096]{1,0:T(8,128)S(1)}, f32[8,4096]{1,0:T(8,128)S(1)}, f32[8,4096]{1,0:T(8,128)S(1)}, bf16[128,8,128]{2,1,0:T(8,128)(2,1)}) custom-call(s32[5,2,1,128]{3,2,1,0:T(1,128)S(1)} %get-tuple-element.34.refs_0_, bf16[128,8,128]{2,1,0:T(8,128)(2,1)S(1)} %all_to_all.28.refs_1_, s32[8,1024]{1,0:T(8,128)S(1)} %get-tuple-element.40.refs_2_.codes_ref, ...), custom_call_target="tpu_custom_call" | custom-call | tf_op jit(solution)/shard_map/step4/pallas_call | solution.py:438
  78.2 3.9 %all-to-all-start.4 = ((bf16[128,8,128]{2,1,0:T(8,128)(2,1)}), bf16[128,8,128]{2,1,0:T(8,128)(2,1)S(1)}, u32[]{:S(2)}, u32[]{:S(2)}) async-start(bf16[128,8,128]{2,1,0:T(8,128)(2,1)} %get-tuple-element.53), calls=%async_computation.4 | async-start | bytes 524288 | tf_op jit(solution)/shard_map/all_to_all | solution.py:376
  82.2 0.0 copy-done.5
  82.2 0.4 activity.1
  82.6 0.1 reduce_sum.9
  82.7 0.1 reshape.37
  82.7 2.6 %collective-permute-start.2 = (f32[5,8,8]{2,1,0:T(8,128)S(1)}, f32[5,8,8]{2,1,0:T(8,128)S(1)}, u32[]{:S(2)}, u32[]{:S(2)}) collective-permute-start(f32[5,8,8]{2,1,0:T(8,128)S(1)} %reshape.37), channel_id=1, source_target_pairs={{0,3},{1,0},{2,1},{3,2},{4,7},{5,4},{6,5},{7,6},{8,11},{9,8},{10,9... | collective-permute-start | bytes 3848 | tf_op jit(solution)/shard_map/ppermute | solution.py:471
  85.3 0.0 collective-permute-start.1
  85.3 1.8 %collective-permute-start = (f32[5,8,8]{2,1,0:T(8,128)S(1)}, f32[5,8,8]{2,1,0:T(8,128)S(1)}, u32[]{:S(2)}, u32[]{:S(2)}) collective-permute-start(f32[5,8,8]{2,1,0:T(8,128)S(1)} %reshape.37), channel_id=1, source_target_pairs={{0,2},{1,3},{2,0},{3,1},{4,6},{5,7},{6,4},{7,5},{8,10},{9,11},{10,... | collective-permute-start | bytes 3848 | tf_op jit(solution)/shard_map/ppermute | solution.py:471
  87.1 0.0 collective-permute-done.2
  87.1 2.4 %collective-permute-done.1 = f32[5,8,8]{2,1,0:T(8,128)S(1)} collective-permute-done((f32[5,8,8]{2,1,0:T(8,128)S(1)}, f32[5,8,8]{2,1,0:T(8,128)S(1)}, u32[]{:S(2)}, u32[]{:S(2)}) %collective-permute-start.1) | collective-permute-done | bytes 1312 | tf_op jit(solution)/shard_map/ppermute | solution.py:471
  89.5 0.4 collective-permute-done
  89.9 0.6 multiply_bitcast_fusion
  90.5 3.0 %all-to-all-done.4.arrived_ref = bf16[128,8,128]{2,1,0:T(8,128)(2,1)S(1)} async-done(((bf16[128,8,128]{2,1,0:T(8,128)(2,1)}), bf16[128,8,128]{2,1,0:T(8,128)(2,1)S(1)}, u32[]{:S(2)}, u32[]{:S(2)}) %all-to-all-start.4) | async-done | bytes 262176 | tf_op jit(solution)/shard_map/all_to_all | solution.py:376
  93.5 1.0 %last.1 = (f32[8,4096]{1,0:T(8,128)}, f32[8,4096]{1,0:T(8,128)}) custom-call(bf16[128,8,128]{2,1,0:T(8,128)(2,1)S(1)} %all-to-all-done.4.arrived_ref, s32[8,1024]{1,0:T(8,128)S(1)} %get-tuple-element.40.refs_2_.codes_ref, f32[8,4096]{1,0:T(8,128)S(1)} %get-tuple-element.54.volts_ref, f32[8,4096]{1,0:T(8,128)S(1)} %get-tuple-element.55.cur_ref, ...), custom_call_target="tpu_custom_call" | custom-call | tf_op jit(solution)/shard_map/last/pallas_call | solution.py:476
  (4 shorter events, 0.0 us)
Async XLA Ops:
  3.7 23.4 %slice-start = ((s8[8388608]{0:T(1024)(128)(4,1)}), s8[4194304]{0:T(1024)(128)(4,1)S(1)}, s32[]{:S(2)}) async-start(s8[8388608]{0:T(1024)(128)(4,1)} %bitcast.16), calls=%async_computation.5 | async-start | bytes 8388608
  3.7 23.4 %slice-start.1 = ((s8[8388608]{0:T(1024)(128)(4,1)}), s8[4194304]{0:T(1024)(128)(4,1)S(1)}, s32[]{:S(2)}) async-start(s8[8388608]{0:T(1024)(128)(4,1)} %bitcast.16), calls=%async_computation.6 | async-start | bytes 8388608
  3.7 23.3 %copy-start = (f32[8,4096]{1,0:T(8,128)S(1)}, f32[8,4096]{1,0:T(8,128)}, u32[]{:S(2)}) copy-start(f32[8,4096]{1,0:T(8,128)} %ext_ref.1) | copy-start | bytes 393220
  3.8 23.3 %copy-start.1 = (f32[8,4096]{1,0:T(8,128)S(1)}, f32[8,4096]{1,0:T(8,128)}, u32[]{:S(2)}) copy-start(f32[8,4096]{1,0:T(8,128)} %refs_3_.1) | copy-start | bytes 393220
  3.8 23.3 %copy-start.2 = (f32[4096]{0:T(1024)S(1)}, f32[4096]{0:T(1024)}, u32[]{:S(2)}) copy-start(f32[4096]{0:T(1024)} %param.14) | copy-start | bytes 49156
  3.8 23.3 %copy-start.3 = (f32[4096]{0:T(1024)S(1)}, f32[4096]{0:T(1024)}, u32[]{:S(2)}) copy-start(f32[4096]{0:T(1024)} %param.15) | copy-start | bytes 49156
  3.8 23.3 %copy-start.4 = (f32[8,4096]{1,0:T(8,128)S(1)}, f32[8,4096]{1,0:T(8,128)}, u32[]{:S(2)}) copy-start(f32[8,4096]{1,0:T(8,128)} %refs_4_.1) | copy-start | bytes 393220
  60.1 22.1 %copy-start.5 = (s32[32]{0:T(128)S(1)}, s32[32]{0:T(128)}, u32[]{:S(2)}) copy-start(s32[32]{0:T(128)} %param.19) | copy-start | bytes 388
  78.2 15.3 %all-to-all-start.4 = ((bf16[128,8,128]{2,1,0:T(8,128)(2,1)}), bf16[128,8,128]{2,1,0:T(8,128)(2,1)S(1)}, u32[]{:S(2)}, u32[]{:S(2)}) async-start(bf16[128,8,128]{2,1,0:T(8,128)(2,1)} %get-tuple-element.53), calls=%async_computation.4 | async-start | bytes 524288 | tf_op jit(solution)/shard_map/all_to_all | solution.py:376
  82.7 4.3 %collective-permute-start.2 = (f32[5,8,8]{2,1,0:T(8,128)S(1)}, f32[5,8,8]{2,1,0:T(8,128)S(1)}, u32[]{:S(2)}, u32[]{:S(2)}) collective-permute-start(f32[5,8,8]{2,1,0:T(8,128)S(1)} %reshape.37), channel_id=1, source_target_pairs={{0,3},{1,0},{2,1},{3,2},{4,7},{5,4},{6,5},{7,6},{8,11},{9,8},{10,9... | collective-permute-start | bytes 3848 | tf_op jit(solution)/shard_map/ppermute | solution.py:471
  85.3 4.1 %collective-permute-start.1 = (f32[5,8,8]{2,1,0:T(8,128)S(1)}, f32[5,8,8]{2,1,0:T(8,128)S(1)}, u32[]{:S(2)}, u32[]{:S(2)}) collective-permute-start(f32[5,8,8]{2,1,0:T(8,128)S(1)} %reshape.37), channel_id=1, source_target_pairs={{0,1},{1,2},{2,3},{3,0},{4,5},{5,6},{6,7},{7,4},{8,9},{9,10},{10,1... | collective-permute-start | bytes 3848 | tf_op jit(solution)/shard_map/ppermute | solution.py:471
  85.3 4.6 %collective-permute-start = (f32[5,8,8]{2,1,0:T(8,128)S(1)}, f32[5,8,8]{2,1,0:T(8,128)S(1)}, u32[]{:S(2)}, u32[]{:S(2)}) collective-permute-start(f32[5,8,8]{2,1,0:T(8,128)S(1)} %reshape.37), channel_id=1, source_target_pairs={{0,2},{1,3},{2,0},{3,1},{4,6},{5,7},{6,4},{7,5},{8,10},{9,11},{10,... | collective-permute-start | bytes 3848 | tf_op jit(solution)/shard_map/ppermute | solution.py:471

commit v11 on v9

--- a/solution.py
+++ b/solution.py
@@ -271,11 +271,12 @@
         spikes_out[:, lanes(b)] = spikes
         blocks_ref[b] = spikes.astype(jnp.bfloat16)
     tile_row, block_row = chosen_ref[step, 0], chosen_ref[step, 1]
+    early = EARLY if step > 1 else 0
 
     def pick(d):
-        if d < EARLY:
+        if d < early:
             return block_row[0, d], tile_row[0, d]
-        if d == EARLY:
+        if d == early:
             to_smem(0).wait()
             to_smem(1).wait()
         return chosen_s[1, 0, d], chosen_s[0, 0, d]

time: 94.9 us -> 94.7 us (level)
  no operation moved by 1% of the time
where the time goes in v11:
time: 94.7 us; the launch traced here: 94.4 us
  blocking collectives  68.5 us (72%)
  Pallas kernels  10.1 us (11%)
  starting transfers between devices  8.28 us (9%)
  waiting for transfers between devices  5.83 us (6%)
    all_to_all x4, blocking collectives, exchange(): return lax.all_to_all(out, ('area', 'local'), 0, 0, tiled=True)  68.5 us
    pallas_call x4, Pallas kernels, shards(): pl.pallas_call(functools.partial(step_kernel, step, last), out_shape=tupl...  5.83 us
    ppermute x3, starting transfers between devices, shards(): lax.ppermute(rates, 'local', [(i, (i + shift) % n_local) for i in range(n...  4.34 us
    all_to_all x1, starting transfers between devices, exchange(): return lax.all_to_all(out, ('area', 'local'), 0, 0, tiled=True)  3.94 us
    all_to_all x1, waiting for transfers between devices, exchange(): return lax.all_to_all(out, ('area', 'local'), 0, 0, tiled=True)  3.02 us
    pallas_call x1, Pallas kernels, shards(): pl.pallas_call(first_kernel, out_shape=(jax.ShapeDtypeStruct((devs * long...  2.98 us
    ppermute x3, waiting for transfers between devices, shards(): lax.ppermute(rates, 'local', [(i, (i + shift) % n_local) for i in range(n...  2.81 us
  transfers between devices with their start and end apart: 4, of which 3 were waited for; matrix products, arithmetic and copies ran while one was open for 1% of the time, Pallas kernels for 0%

profile of v11, /device:TPU:1, one launch (start us, length us, event | category | flops | bytes accessed | tf_op | source)
XLA Modules:
  0.0 94.4 jit_solution(12588315618760466218)
XLA Ops:
  0.6 3.0 %first.1 = (bf16[1280,128]{1,0:T(8,128)(2,1)S(1)}, f32[8,4096]{1,0:T(8,128)S(1)}, s32[5,2,1,128]{3,2,1,0:T(1,128)S(1)}, bf16[1280,128]{1,0:T(8,128)(2,1)S(1)}, bf16[128,1024]{1,0:T(8,128)(2,1)S(1)}) custom-call(s32[5,1,128]{2,1,0:T(1,128)} %bitcast.35, s32[2,128]{1,0:T(2,128)} %bitcast.36, s32[2,128]{1,0:T(2,128)} %bitcast.37, s32[5,1,128]{2,1,0:T(1,128)} %counts_hbm.1, ...), custom_call_target="tpu_custom_call" | custom-call | tf_op jit(solution)/shard_map/first/pallas_call | solution.py:378
  3.6 0.0 slice-start
  3.6 0.0 slice-start.1
  3.7 0.0 copy-start
  3.7 0.0 copy-start.1
  3.7 0.0 copy-start.2
  3.7 0.0 copy-start.3
  3.7 0.0 copy-start.4
  3.7 23.3 %all_to_all.25 = bf16[128,5,2,128]{3,2,1,0:T(2,128)(2,1)S(1)} all-to-all(bf16[128,5,2,128]{3,2,1,0:T(2,128)(2,1)S(1)} %bitcast.33), channel_id=1, replica_groups=mesh['area'=32,'local'=4] {'area','local'}, dimensions={0} | all-to-all | bytes 655360 | tf_op jit(solution)/shard_map/all_to_all | solution.py:372
  27.0 0.0 slice-done
  27.0 0.0 slice-done.1
  27.0 0.0 copy-done
  27.0 0.0 copy-done.1
  27.0 0.0 copy-done.2
  27.0 0.0 copy-done.3
  27.0 0.0 copy-done.4
  27.1 1.6 %step1.1 = (f32[8,4096]{1,0:T(8,128)S(1)}, f32[8,4096]{1,0:T(8,128)S(1)}, f32[8,4096]{1,0:T(8,128)S(1)}, bf16[128,8,128]{2,1,0:T(8,128)(2,1)S(1)}, s32[8,1024]{1,0:T(8,128)S(1)}) custom-call(s32[5,2,1,128]{3,2,1,0:T(1,128)S(1)} %get-tuple-element.34.refs_0_, bf16[1280,128]{1,0:T(8,128)(2,1)S(1)} %bitcast.22, s32[8,1024]{1,0:T(8,128)S(1)} %broadcast_in_dim.6.refs_2_, ...), custom_call_target="tpu_custom_call" | custom-call | tf_op jit(solution)/shard_map/step1/pallas_call | solution.py:434
  28.6 15.1 %all_to_all.26.refs_1_ = bf16[128,8,128]{2,1,0:T(8,128)(2,1)S(1)} all-to-all(bf16[128,8,128]{2,1,0:T(8,128)(2,1)S(1)} %get-tuple-element.39), channel_id=1, replica_groups=mesh['area'=32,'local'=4] {'area','local'}, dimensions={0} | all-to-all | bytes 524288 | tf_op jit(solution)/shard_map/all_to_all | solution.py:372
  43.7 1.2 %step2.1 = (f32[8,4096]{1,0:T(8,128)S(1)}, f32[8,4096]{1,0:T(8,128)S(1)}, f32[8,4096]{1,0:T(8,128)S(1)}, bf16[128,8,128]{2,1,0:T(8,128)(2,1)S(1)}) custom-call(s32[5,2,1,128]{3,2,1,0:T(1,128)S(1)} %get-tuple-element.34.refs_0_, bf16[128,8,128]{2,1,0:T(8,128)(2,1)S(1)} %all_to_all.26.refs_1_, s32[8,1024]{1,0:T(8,128)S(1)} %get-tuple-element.40.refs_2_.codes_ref, ...), custom_call_target="tpu_custom_call" | custom-call | tf_op jit(solution)/shard_map/step2/pallas_call | solution.py:434
  44.9 15.1 %all_to_all.27.refs_1_ = bf16[128,8,128]{2,1,0:T(8,128)(2,1)S(1)} all-to-all(bf16[128,8,128]{2,1,0:T(8,128)(2,1)S(1)} %get-tuple-element.44), channel_id=1, replica_groups=mesh['area'=32,'local'=4] {'area','local'}, dimensions={0} | all-to-all | bytes 524288 | tf_op jit(solution)/shard_map/all_to_all | solution.py:372
  60.0 0.0 copy-start.5
  60.0 1.2 %step3.1 = (f32[8,4096]{1,0:T(8,128)S(1)}, f32[8,4096]{1,0:T(8,128)S(1)}, f32[8,4096]{1,0:T(8,128)S(1)}, bf16[128,8,128]{2,1,0:T(8,128)(2,1)S(1)}) custom-call(s32[5,2,1,128]{3,2,1,0:T(1,128)S(1)} %get-tuple-element.34.refs_0_, bf16[128,8,128]{2,1,0:T(8,128)(2,1)S(1)} %all_to_all.27.refs_1_, s32[8,1024]{1,0:T(8,128)S(1)} %get-tuple-element.40.refs_2_.codes_ref, ...), custom_call_target="tpu_custom_call" | custom-call | tf_op jit(solution)/shard_map/step3/pallas_call | solution.py:434
  61.2 15.1 %all_to_all.28.refs_1_ = bf16[128,8,128]{2,1,0:T(8,128)(2,1)S(1)} all-to-all(bf16[128,8,128]{2,1,0:T(8,128)(2,1)S(1)} %get-tuple-element.48), channel_id=1, replica_groups=mesh['area'=32,'local'=4] {'area','local'}, dimensions={0} | all-to-all | bytes 524288 | tf_op jit(solution)/shard_map/all_to_all | solution.py:372
  76.3 1.8 %step4.1 = (f32[8,4096]{1,0:T(8,128)S(1)}, f32[8,4096]{1,0:T(8,128)S(1)}, f32[8,4096]{1,0:T(8,128)S(1)}, bf16[128,8,128]{2,1,0:T(8,128)(2,1)}) custom-call(s32[5,2,1,128]{3,2,1,0:T(1,128)S(1)} %get-tuple-element.34.refs_0_, bf16[128,8,128]{2,1,0:T(8,128)(2,1)S(1)} %all_to_all.28.refs_1_, s32[8,1024]{1,0:T(8,128)S(1)} %get-tuple-element.40.refs_2_.codes_ref, ...), custom_call_target="tpu_custom_call" | custom-call | tf_op jit(solution)/shard_map/step4/pallas_call | solution.py:434
  78.1 3.9 %all-to-all-start.4 = ((bf16[128,8,128]{2,1,0:T(8,128)(2,1)}), bf16[128,8,128]{2,1,0:T(8,128)(2,1)S(1)}, u32[]{:S(2)}, u32[]{:S(2)}) async-start(bf16[128,8,128]{2,1,0:T(8,128)(2,1)} %get-tuple-element.53), calls=%async_computation.4 | async-start | bytes 524288 | tf_op jit(solution)/shard_map/all_to_all | solution.py:372
  82.1 0.0 copy-done.5
  82.1 0.3 activity.1
  82.5 0.1 reduce_sum.9
  82.6 0.1 reshape.37
  82.6 2.6 %collective-permute-start.2 = (f32[5,8,8]{2,1,0:T(8,128)S(1)}, f32[5,8,8]{2,1,0:T(8,128)S(1)}, u32[]{:S(2)}, u32[]{:S(2)}) collective-permute-start(f32[5,8,8]{2,1,0:T(8,128)S(1)} %reshape.37), channel_id=1, source_target_pairs={{0,3},{1,0},{2,1},{3,2},{4,7},{5,4},{6,5},{7,6},{8,11},{9,8},{10,9... | collective-permute-start | bytes 3848 | tf_op jit(solution)/shard_map/ppermute | solution.py:467
  85.2 0.0 collective-permute-start.1
  85.2 1.8 %collective-permute-start = (f32[5,8,8]{2,1,0:T(8,128)S(1)}, f32[5,8,8]{2,1,0:T(8,128)S(1)}, u32[]{:S(2)}, u32[]{:S(2)}) collective-permute-start(f32[5,8,8]{2,1,0:T(8,128)S(1)} %reshape.37), channel_id=1, source_target_pairs={{0,2},{1,3},{2,0},{3,1},{4,6},{5,7},{6,4},{7,5},{8,10},{9,11},{10,... | collective-permute-start | bytes 3848 | tf_op jit(solution)/shard_map/ppermute | solution.py:467
  87.0 0.0 collective-permute-done.2
  87.0 2.4 %collective-permute-done.1 = f32[5,8,8]{2,1,0:T(8,128)S(1)} collective-permute-done((f32[5,8,8]{2,1,0:T(8,128)S(1)}, f32[5,8,8]{2,1,0:T(8,128)S(1)}, u32[]{:S(2)}, u32[]{:S(2)}) %collective-permute-start.1) | collective-permute-done | bytes 1312 | tf_op jit(solution)/shard_map/ppermute | solution.py:467
  89.4 0.4 collective-permute-done
  89.8 0.6 multiply_bitcast_fusion
  90.4 3.0 %all-to-all-done.4.arrived_ref = bf16[128,8,128]{2,1,0:T(8,128)(2,1)S(1)} async-done(((bf16[128,8,128]{2,1,0:T(8,128)(2,1)}), bf16[128,8,128]{2,1,0:T(8,128)(2,1)S(1)}, u32[]{:S(2)}, u32[]{:S(2)}) %all-to-all-start.4) | async-done | bytes 262176 | tf_op jit(solution)/shard_map/all_to_all | solution.py:372
  93.4 1.0 %last.1 = (f32[8,4096]{1,0:T(8,128)}, f32[8,4096]{1,0:T(8,128)}) custom-call(bf16[128,8,128]{2,1,0:T(8,128)(2,1)S(1)} %all-to-all-done.4.arrived_ref, s32[8,1024]{1,0:T(8,128)S(1)} %get-tuple-element.40.refs_2_.codes_ref, f32[8,4096]{1,0:T(8,128)S(1)} %get-tuple-element.54.volts_ref, f32[8,4096]{1,0:T(8,128)S(1)} %get-tuple-element.55.cur_ref, ...), custom_call_target="tpu_custom_call" | custom-call | tf_op jit(solution)/shard_map/last/pallas_call | solution.py:472
  (4 shorter events, 0.0 us)
Async XLA Ops:
  3.6 23.4 %slice-start = ((s8[8388608]{0:T(1024)(128)(4,1)}), s8[4194304]{0:T(1024)(128)(4,1)S(1)}, s32[]{:S(2)}) async-start(s8[8388608]{0:T(1024)(128)(4,1)} %bitcast.16), calls=%async_computation.5 | async-start | bytes 8388608
  3.6 23.4 %slice-start.1 = ((s8[8388608]{0:T(1024)(128)(4,1)}), s8[4194304]{0:T(1024)(128)(4,1)S(1)}, s32[]{:S(2)}) async-start(s8[8388608]{0:T(1024)(128)(4,1)} %bitcast.16), calls=%async_computation.6 | async-start | bytes 8388608
  3.7 23.3 %copy-start = (f32[8,4096]{1,0:T(8,128)S(1)}, f32[8,4096]{1,0:T(8,128)}, u32[]{:S(2)}) copy-start(f32[8,4096]{1,0:T(8,128)} %ext_ref.1) | copy-start | bytes 393220
  3.7 23.3 %copy-start.1 = (f32[8,4096]{1,0:T(8,128)S(1)}, f32[8,4096]{1,0:T(8,128)}, u32[]{:S(2)}) copy-start(f32[8,4096]{1,0:T(8,128)} %refs_3_.1) | copy-start | bytes 393220
  3.7 23.3 %copy-start.2 = (f32[4096]{0:T(1024)S(1)}, f32[4096]{0:T(1024)}, u32[]{:S(2)}) copy-start(f32[4096]{0:T(1024)} %param.14) | copy-start | bytes 49156
  3.7 23.3 %copy-start.3 = (f32[4096]{0:T(1024)S(1)}, f32[4096]{0:T(1024)}, u32[]{:S(2)}) copy-start(f32[4096]{0:T(1024)} %param.15) | copy-start | bytes 49156
  3.7 23.3 %copy-start.4 = (f32[8,4096]{1,0:T(8,128)S(1)}, f32[8,4096]{1,0:T(8,128)}, u32[]{:S(2)}) copy-start(f32[8,4096]{1,0:T(8,128)} %refs_4_.1) | copy-start | bytes 393220
  60.0 22.1 %copy-start.5 = (s32[32]{0:T(128)S(1)}, s32[32]{0:T(128)}, u32[]{:S(2)}) copy-start(s32[32]{0:T(128)} %param.19) | copy-start | bytes 388
  78.1 15.3 %all-to-all-start.4 = ((bf16[128,8,128]{2,1,0:T(8,128)(2,1)}), bf16[128,8,128]{2,1,0:T(8,128)(2,1)S(1)}, u32[]{:S(2)}, u32[]{:S(2)}) async-start(bf16[128,8,128]{2,1,0:T(8,128)(2,1)} %get-tuple-element.53), calls=%async_computation.4 | async-start | bytes 524288 | tf_op jit(solution)/shard_map/all_to_all | solution.py:372
  82.6 4.3 %collective-permute-start.2 = (f32[5,8,8]{2,1,0:T(8,128)S(1)}, f32[5,8,8]{2,1,0:T(8,128)S(1)}, u32[]{:S(2)}, u32[]{:S(2)}) collective-permute-start(f32[5,8,8]{2,1,0:T(8,128)S(1)} %reshape.37), channel_id=1, source_target_pairs={{0,3},{1,0},{2,1},{3,2},{4,7},{5,4},{6,5},{7,6},{8,11},{9,8},{10,9... | collective-permute-start | bytes 3848 | tf_op jit(solution)/shard_map/ppermute | solution.py:467
  85.2 4.1 %collective-permute-start.1 = (f32[5,8,8]{2,1,0:T(8,128)S(1)}, f32[5,8,8]{2,1,0:T(8,128)S(1)}, u32[]{:S(2)}, u32[]{:S(2)}) collective-permute-start(f32[5,8,8]{2,1,0:T(8,128)S(1)} %reshape.37), channel_id=1, source_target_pairs={{0,1},{1,2},{2,3},{3,0},{4,5},{5,6},{6,7},{7,4},{8,9},{9,10},{10,1... | collective-permute-start | bytes 3848 | tf_op jit(solution)/shard_map/ppermute | solution.py:467
  85.2 4.6 %collective-permute-start = (f32[5,8,8]{2,1,0:T(8,128)S(1)}, f32[5,8,8]{2,1,0:T(8,128)S(1)}, u32[]{:S(2)}, u32[]{:S(2)}) collective-permute-start(f32[5,8,8]{2,1,0:T(8,128)S(1)} %reshape.37), channel_id=1, source_target_pairs={{0,2},{1,3},{2,0},{3,1},{4,6},{5,7},{6,4},{7,5},{8,10},{9,11},{10,... | collective-permute-start | bytes 3848 | tf_op jit(solution)/shard_map/ppermute | solution.py:467

commit v12 on v11

--- a/solution.py
+++ b/solution.py
@@ -14,7 +14,7 @@
 EXTRA = 2
 EARLY = 32
 HALVES = 2
-PIECES = 4
+PIECES = 2
 CHUNK = 32
 WHOLE = 32
 

time: 94.7 us -> 94.7 us (level)
  no operation moved by 1% of the time
where the time goes in v12:
time: 94.7 us; the launch traced here: 94.4 us
  blocking collectives  68.5 us (72%)
  Pallas kernels  10.1 us (11%)
  starting transfers between devices  8.28 us (9%)
  waiting for transfers between devices  5.83 us (6%)
    all_to_all x4, blocking collectives, exchange(): return lax.all_to_all(out, ('area', 'local'), 0, 0, tiled=True)  68.5 us
    pallas_call x4, Pallas kernels, shards(): pl.pallas_call(functools.partial(step_kernel, step, last), out_shape=tupl...  5.78 us
    ppermute x3, starting transfers between devices, shards(): lax.ppermute(rates, 'local', [(i, (i + shift) % n_local) for i in range(n...  4.34 us
    all_to_all x1, starting transfers between devices, exchange(): return lax.all_to_all(out, ('area', 'local'), 0, 0, tiled=True)  3.94 us
    all_to_all x1, waiting for transfers between devices, exchange(): return lax.all_to_all(out, ('area', 'local'), 0, 0, tiled=True)  3.01 us
    pallas_call x1, Pallas kernels, shards(): pl.pallas_call(first_kernel, out_shape=(jax.ShapeDtypeStruct((devs * long...  2.97 us
    ppermute x3, waiting for transfers between devices, shards(): lax.ppermute(rates, 'local', [(i, (i + shift) % n_local) for i in range(n...  2.81 us
  transfers between devices with their start and end apart: 4, of which 3 were waited for; matrix products, arithmetic and copies ran while one was open for 1% of the time, Pallas kernels for 0%

profile of v12, /device:TPU:1, one launch (start us, length us, event | category | flops | bytes accessed | tf_op | source)
XLA Modules:
  0.0 94.4 jit_solution(17310753836942269690)
XLA Ops:
  0.6 3.0 %first.1 = (bf16[1280,128]{1,0:T(8,128)(2,1)S(1)}, f32[8,4096]{1,0:T(8,128)S(1)}, s32[5,2,1,128]{3,2,1,0:T(1,128)S(1)}, bf16[1280,128]{1,0:T(8,128)(2,1)S(1)}, bf16[128,1024]{1,0:T(8,128)(2,1)S(1)}) custom-call(s32[5,1,128]{2,1,0:T(1,128)} %bitcast.35, s32[2,128]{1,0:T(2,128)} %bitcast.36, s32[2,128]{1,0:T(2,128)} %bitcast.37, s32[5,1,128]{2,1,0:T(1,128)} %counts_hbm.1, ...), custom_call_target="tpu_custom_call" | custom-call | tf_op jit(solution)/shard_map/first/pallas_call | solution.py:378
  3.6 0.0 slice-start
  3.6 0.0 slice-start.1
  3.6 0.0 copy-start
  3.7 0.0 copy-start.1
  3.7 0.0 copy-start.2
  3.7 0.0 copy-start.3
  3.7 0.0 copy-start.4
  3.7 23.3 %all_to_all.25 = bf16[128,5,2,128]{3,2,1,0:T(2,128)(2,1)S(1)} all-to-all(bf16[128,5,2,128]{3,2,1,0:T(2,128)(2,1)S(1)} %bitcast.33), channel_id=1, replica_groups=mesh['area'=32,'local'=4] {'area','local'}, dimensions={0} | all-to-all | bytes 655360 | tf_op jit(solution)/shard_map/all_to_all | solution.py:372
  27.0 0.0 slice-done
  27.0 0.0 slice-done.1
  27.0 0.0 copy-done
  27.0 0.0 copy-done.1
  27.0 0.0 copy-done.2
  27.0 0.0 copy-done.3
  27.0 0.0 copy-done.4
  27.1 1.6 %step1.1 = (f32[8,4096]{1,0:T(8,128)S(1)}, f32[8,4096]{1,0:T(8,128)S(1)}, f32[8,4096]{1,0:T(8,128)S(1)}, bf16[128,8,128]{2,1,0:T(8,128)(2,1)S(1)}, s32[8,1024]{1,0:T(8,128)S(1)}) custom-call(s32[5,2,1,128]{3,2,1,0:T(1,128)S(1)} %get-tuple-element.34.refs_0_, bf16[1280,128]{1,0:T(8,128)(2,1)S(1)} %bitcast.22, s32[8,1024]{1,0:T(8,128)S(1)} %broadcast_in_dim.6.refs_2_, ...), custom_call_target="tpu_custom_call" | custom-call | tf_op jit(solution)/shard_map/step1/pallas_call | solution.py:434
  28.6 15.1 %all_to_all.26.refs_1_ = bf16[128,8,128]{2,1,0:T(8,128)(2,1)S(1)} all-to-all(bf16[128,8,128]{2,1,0:T(8,128)(2,1)S(1)} %get-tuple-element.39), channel_id=1, replica_groups=mesh['area'=32,'local'=4] {'area','local'}, dimensions={0} | all-to-all | bytes 524288 | tf_op jit(solution)/shard_map/all_to_all | solution.py:372
  43.7 1.2 %step2.1 = (f32[8,4096]{1,0:T(8,128)S(1)}, f32[8,4096]{1,0:T(8,128)S(1)}, f32[8,4096]{1,0:T(8,128)S(1)}, bf16[128,8,128]{2,1,0:T(8,128)(2,1)S(1)}) custom-call(s32[5,2,1,128]{3,2,1,0:T(1,128)S(1)} %get-tuple-element.34.refs_0_, bf16[128,8,128]{2,1,0:T(8,128)(2,1)S(1)} %all_to_all.26.refs_1_, s32[8,1024]{1,0:T(8,128)S(1)} %get-tuple-element.40.refs_2_.codes_ref, ...), custom_call_target="tpu_custom_call" | custom-call | tf_op jit(solution)/shard_map/step2/pallas_call | solution.py:434
  44.9 15.1 %all_to_all.27.refs_1_ = bf16[128,8,128]{2,1,0:T(8,128)(2,1)S(1)} all-to-all(bf16[128,8,128]{2,1,0:T(8,128)(2,1)S(1)} %get-tuple-element.44), channel_id=1, replica_groups=mesh['area'=32,'local'=4] {'area','local'}, dimensions={0} | all-to-all | bytes 524288 | tf_op jit(solution)/shard_map/all_to_all | solution.py:372
  60.0 0.0 copy-start.5
  60.0 1.2 %step3.1 = (f32[8,4096]{1,0:T(8,128)S(1)}, f32[8,4096]{1,0:T(8,128)S(1)}, f32[8,4096]{1,0:T(8,128)S(1)}, bf16[128,8,128]{2,1,0:T(8,128)(2,1)S(1)}) custom-call(s32[5,2,1,128]{3,2,1,0:T(1,128)S(1)} %get-tuple-element.34.refs_0_, bf16[128,8,128]{2,1,0:T(8,128)(2,1)S(1)} %all_to_all.27.refs_1_, s32[8,1024]{1,0:T(8,128)S(1)} %get-tuple-element.40.refs_2_.codes_ref, ...), custom_call_target="tpu_custom_call" | custom-call | tf_op jit(solution)/shard_map/step3/pallas_call | solution.py:434
  61.2 15.1 %all_to_all.28.refs_1_ = bf16[128,8,128]{2,1,0:T(8,128)(2,1)S(1)} all-to-all(bf16[128,8,128]{2,1,0:T(8,128)(2,1)S(1)} %get-tuple-element.48), channel_id=1, replica_groups=mesh['area'=32,'local'=4] {'area','local'}, dimensions={0} | all-to-all | bytes 524288 | tf_op jit(solution)/shard_map/all_to_all | solution.py:372
  76.2 1.8 %step4.1 = (f32[8,4096]{1,0:T(8,128)S(1)}, f32[8,4096]{1,0:T(8,128)S(1)}, f32[8,4096]{1,0:T(8,128)S(1)}, bf16[128,8,128]{2,1,0:T(8,128)(2,1)}) custom-call(s32[5,2,1,128]{3,2,1,0:T(1,128)S(1)} %get-tuple-element.34.refs_0_, bf16[128,8,128]{2,1,0:T(8,128)(2,1)S(1)} %all_to_all.28.refs_1_, s32[8,1024]{1,0:T(8,128)S(1)} %get-tuple-element.40.refs_2_.codes_ref, ...), custom_call_target="tpu_custom_call" | custom-call | tf_op jit(solution)/shard_map/step4/pallas_call | solution.py:434
  78.1 3.9 %all-to-all-start.4 = ((bf16[128,8,128]{2,1,0:T(8,128)(2,1)}), bf16[128,8,128]{2,1,0:T(8,128)(2,1)S(1)}, u32[]{:S(2)}, u32[]{:S(2)}) async-start(bf16[128,8,128]{2,1,0:T(8,128)(2,1)} %get-tuple-element.53), calls=%async_computation.4 | async-start | bytes 524288 | tf_op jit(solution)/shard_map/all_to_all | solution.py:372
  82.0 0.0 copy-done.5
  82.1 0.4 activity.1
  82.4 0.1 reduce_sum.9
  82.5 0.1 reshape.37
  82.6 2.6 %collective-permute-start.2 = (f32[5,8,8]{2,1,0:T(8,128)S(1)}, f32[5,8,8]{2,1,0:T(8,128)S(1)}, u32[]{:S(2)}, u32[]{:S(2)}) collective-permute-start(f32[5,8,8]{2,1,0:T(8,128)S(1)} %reshape.37), channel_id=1, source_target_pairs={{0,3},{1,0},{2,1},{3,2},{4,7},{5,4},{6,5},{7,6},{8,11},{9,8},{10,9... | collective-permute-start | bytes 3848 | tf_op jit(solution)/shard_map/ppermute | solution.py:467
  85.2 0.0 collective-permute-start.1
  85.2 1.8 %collective-permute-start = (f32[5,8,8]{2,1,0:T(8,128)S(1)}, f32[5,8,8]{2,1,0:T(8,128)S(1)}, u32[]{:S(2)}, u32[]{:S(2)}) collective-permute-start(f32[5,8,8]{2,1,0:T(8,128)S(1)} %reshape.37), channel_id=1, source_target_pairs={{0,2},{1,3},{2,0},{3,1},{4,6},{5,7},{6,4},{7,5},{8,10},{9,11},{10,... | collective-permute-start | bytes 3848 | tf_op jit(solution)/shard_map/ppermute | solution.py:467
  86.9 0.0 collective-permute-done.2
  86.9 2.4 %collective-permute-done.1 = f32[5,8,8]{2,1,0:T(8,128)S(1)} collective-permute-done((f32[5,8,8]{2,1,0:T(8,128)S(1)}, f32[5,8,8]{2,1,0:T(8,128)S(1)}, u32[]{:S(2)}, u32[]{:S(2)}) %collective-permute-start.1) | collective-permute-done | bytes 1312 | tf_op jit(solution)/shard_map/ppermute | solution.py:467
  89.3 0.4 collective-permute-done
  89.8 0.6 multiply_bitcast_fusion
  90.4 3.0 %all-to-all-done.4.arrived_ref = bf16[128,8,128]{2,1,0:T(8,128)(2,1)S(1)} async-done(((bf16[128,8,128]{2,1,0:T(8,128)(2,1)}), bf16[128,8,128]{2,1,0:T(8,128)(2,1)S(1)}, u32[]{:S(2)}, u32[]{:S(2)}) %all-to-all-start.4) | async-done | bytes 262176 | tf_op jit(solution)/shard_map/all_to_all | solution.py:372
  93.4 1.0 %last.1 = (f32[8,4096]{1,0:T(8,128)}, f32[8,4096]{1,0:T(8,128)}) custom-call(bf16[128,8,128]{2,1,0:T(8,128)(2,1)S(1)} %all-to-all-done.4.arrived_ref, s32[8,1024]{1,0:T(8,128)S(1)} %get-tuple-element.40.refs_2_.codes_ref, f32[8,4096]{1,0:T(8,128)S(1)} %get-tuple-element.54.volts_ref, f32[8,4096]{1,0:T(8,128)S(1)} %get-tuple-element.55.cur_ref, ...), custom_call_target="tpu_custom_call" | custom-call | tf_op jit(solution)/shard_map/last/pallas_call | solution.py:472
  (4 shorter events, 0.0 us)
Async XLA Ops:
  3.6 23.4 %slice-start = ((s8[8388608]{0:T(1024)(128)(4,1)}), s8[4194304]{0:T(1024)(128)(4,1)S(1)}, s32[]{:S(2)}) async-start(s8[8388608]{0:T(1024)(128)(4,1)} %bitcast.16), calls=%async_computation.5 | async-start | bytes 8388608
  3.6 23.4 %slice-start.1 = ((s8[8388608]{0:T(1024)(128)(4,1)}), s8[4194304]{0:T(1024)(128)(4,1)S(1)}, s32[]{:S(2)}) async-start(s8[8388608]{0:T(1024)(128)(4,1)} %bitcast.16), calls=%async_computation.6 | async-start | bytes 8388608
  3.6 23.3 %copy-start = (f32[8,4096]{1,0:T(8,128)S(1)}, f32[8,4096]{1,0:T(8,128)}, u32[]{:S(2)}) copy-start(f32[8,4096]{1,0:T(8,128)} %ext_ref.1) | copy-start | bytes 393220
  3.7 23.3 %copy-start.1 = (f32[8,4096]{1,0:T(8,128)S(1)}, f32[8,4096]{1,0:T(8,128)}, u32[]{:S(2)}) copy-start(f32[8,4096]{1,0:T(8,128)} %refs_3_.1) | copy-start | bytes 393220
  3.7 23.3 %copy-start.2 = (f32[4096]{0:T(1024)S(1)}, f32[4096]{0:T(1024)}, u32[]{:S(2)}) copy-start(f32[4096]{0:T(1024)} %param.14) | copy-start | bytes 49156
  3.7 23.3 %copy-start.3 = (f32[4096]{0:T(1024)S(1)}, f32[4096]{0:T(1024)}, u32[]{:S(2)}) copy-start(f32[4096]{0:T(1024)} %param.15) | copy-start | bytes 49156
  3.7 23.3 %copy-start.4 = (f32[8,4096]{1,0:T(8,128)S(1)}, f32[8,4096]{1,0:T(8,128)}, u32[]{:S(2)}) copy-start(f32[8,4096]{1,0:T(8,128)} %refs_4_.1) | copy-start | bytes 393220
  60.0 22.1 %copy-start.5 = (s32[32]{0:T(128)S(1)}, s32[32]{0:T(128)}, u32[]{:S(2)}) copy-start(s32[32]{0:T(128)} %param.19) | copy-start | bytes 388
  78.1 15.3 %all-to-all-start.4 = ((bf16[128,8,128]{2,1,0:T(8,128)(2,1)}), bf16[128,8,128]{2,1,0:T(8,128)(2,1)S(1)}, u32[]{:S(2)}, u32[]{:S(2)}) async-start(bf16[128,8,128]{2,1,0:T(8,128)(2,1)} %get-tuple-element.53), calls=%async_computation.4 | async-start | bytes 524288 | tf_op jit(solution)/shard_map/all_to_all | solution.py:372
  82.6 4.3 %collective-permute-start.2 = (f32[5,8,8]{2,1,0:T(8,128)S(1)}, f32[5,8,8]{2,1,0:T(8,128)S(1)}, u32[]{:S(2)}, u32[]{:S(2)}) collective-permute-start(f32[5,8,8]{2,1,0:T(8,128)S(1)} %reshape.37), channel_id=1, source_target_pairs={{0,3},{1,0},{2,1},{3,2},{4,7},{5,4},{6,5},{7,6},{8,11},{9,8},{10,9... | collective-permute-start | bytes 3848 | tf_op jit(solution)/shard_map/ppermute | solution.py:467
  85.2 4.1 %collective-permute-start.1 = (f32[5,8,8]{2,1,0:T(8,128)S(1)}, f32[5,8,8]{2,1,0:T(8,128)S(1)}, u32[]{:S(2)}, u32[]{:S(2)}) collective-permute-start(f32[5,8,8]{2,1,0:T(8,128)S(1)} %reshape.37), channel_id=1, source_target_pairs={{0,1},{1,2},{2,3},{3,0},{4,5},{5,6},{6,7},{7,4},{8,9},{9,10},{10,1... | collective-permute-start | bytes 3848 | tf_op jit(solution)/shard_map/ppermute | solution.py:467
  85.2 4.6 %collective-permute-start = (f32[5,8,8]{2,1,0:T(8,128)S(1)}, f32[5,8,8]{2,1,0:T(8,128)S(1)}, u32[]{:S(2)}, u32[]{:S(2)}) collective-permute-start(f32[5,8,8]{2,1,0:T(8,128)S(1)} %reshape.37), channel_id=1, source_target_pairs={{0,2},{1,3},{2,0},{3,1},{4,6},{5,7},{6,4},{7,5},{8,10},{9,11},{10,... | collective-permute-start | bytes 3848 | tf_op jit(solution)/shard_map/ppermute | solution.py:467
